TPU v7x, 32 devices: a whole 2x2x4 slice. The times are simulated.
32 devices in a mesh: dp: 4 (over y, core), vocab: 8 (over z, x).
Axes of the slice: x: 2, y: 2, z: 4, core: 2. Of those that a mesh axis runs over, the one named last changes fastest.
Arguments:
- student_hidden: bfloat16 [512, 2048], P('dp', 'vocab'), may hold values from -210 to 210
- student_blocks: bfloat16 [8, 1024, 4864], P('vocab', 'dp'), may hold values from -0.375 to 0.375
- teacher_logits: bfloat16 [512, 19456], P('dp', 'vocab'), may hold values from -16 to 308
- token_ids: int32 [512], P('dp'), may hold values from 0 to 19455
- loss_mask: int32 [512], P('dp'), may hold values from 0 to 1, as said below
Outputs:
- hidden_grad: bfloat16 [512, 2048], P('dp', 'vocab')
- token_kl: float32 [512], P('dp')
- sampled_logprob: float32 [512], P('dp')
- loss: float32 [], replicated
Inputs may be any that keep to these rules, and one draw needn't show every extreme that they name: `loss_mask`: in each block of 128 tokens the mask is 0 on a leading run of at most 64 tokens and 1 on the rest.
All inputs are finite; a program needn't handle non-finite values.
Results may differ from a plain program's by a relative error of at most 0.0047.
Values may be sent and summed in bfloat16 or wider, within the bound.
No kernel may reach another device: no remote copies, remote signals or barrier semaphores. Data moves between devices by JAX's collectives and lax.ppermute only.
A program may use at most 64 MiB of HBM per device.

v0:
```python
import jax
import jax.numpy as jnp
from jax import lax
from jax.sharding import PartitionSpec as P

D = 2048
VT = 2432


def swapped(shard, axis, stride):
    return lax.ppermute(shard, axis, [(i, i ^ 1 << stride) for i in range(lax.axis_size(axis))])


def combined_all(part, axis, combine):
    gathered = jax.tree.map(lambda a: lax.all_gather(a, axis), part)

    def take(source):
        return jax.tree.map(lambda a: lax.dynamic_index_in_dim(a, source, 0, False), gathered)

    return lax.fori_loop(
        1, lax.axis_size(axis), lambda source, state: combine(state, take(source)), take(0)
    )


def pair_merge(left_pair, right_pair):
    left_max, left_total = left_pair
    right_max, right_total = right_pair
    top_value = jnp.maximum(left_max, right_max)
    merged_total = left_total * jnp.exp(left_max - top_value) + right_total * jnp.exp(
        right_max - top_value
    )
    return (top_value, merged_total)


def row_stats(values):
    row_max = jnp.max(values, axis=1)
    row_total = jnp.sum(jnp.exp(values - row_max[:, None]), axis=1)
    return (row_max, row_total)


def on_device(student_hidden, student_blocks, teacher_logits, token_ids, loss_mask):
    vocab_index = lax.axis_index("vocab")
    pair_side = vocab_index % 2
    mask_float = loss_mask.astype(jnp.float32)
    mask_total = lax.psum(jnp.sum(mask_float), "dp")
    gathered = lax.all_gather(student_hidden, "vocab", axis=1, tiled=True)
    piece = student_blocks[0]
    own_block = lax.dynamic_slice_in_dim(piece, pair_side * VT, VT, 1)
    far_block = lax.dynamic_slice_in_dim(piece, (1 - pair_side) * VT, VT, 1)
    received = swapped(far_block, "vocab", 0)
    stacked = jnp.where(
        pair_side == 0, jnp.stack([own_block, received]), jnp.stack([received, own_block])
    )
    weight = lax.all_gather(stacked, "dp", axis=1, tiled=True).reshape(D, VT)
    logits = jnp.dot(gathered, weight, preferred_element_type=jnp.float32)
    column_start = vocab_index * VT
    teacher_local = teacher_logits.astype(jnp.float32)
    teacher_full = teacher_logits.astype(jnp.float32)
    teacher_max = lax.pmax(jnp.max(teacher_full, axis=1), "vocab")
    teacher_total = lax.psum(jnp.sum(jnp.exp(teacher_full - teacher_max[:, None]), axis=1), "vocab")
    student_max, student_total = row_stats(logits)
    merged = combined_all((student_max, student_total), "vocab", pair_merge)
    stats = (teacher_max, teacher_total, merged[0], merged[1])
    teacher_logp = teacher_local - stats[0][:, None] - jnp.log(stats[1])[:, None]
    student_logp = logits - stats[2][:, None] - jnp.log(stats[3])[:, None]
    teacher_prob = jnp.exp(teacher_logp)
    kl_part = jnp.sum(teacher_prob * (teacher_logp - student_logp), axis=1)
    columns = lax.broadcasted_iota(jnp.int32, logits.shape, 1) + column_start
    sampled_part = jnp.sum(jnp.where(columns == token_ids[:, None], student_logp, 0.0), axis=1)
    token_kl, sampled = lax.psum((kl_part, sampled_part), "vocab")
    loss = lax.psum(jnp.sum(mask_float * token_kl), "dp") / mask_total
    factor = mask_float / mask_total
    dlogits = (factor[:, None] * (jnp.exp(student_logp) - teacher_prob)).astype(jnp.bfloat16)
    term = lax.dot_general(
        dlogits, weight, (((1,), (1,)), ((), ())), preferred_element_type=jnp.float32
    )
    hidden_grad = lax.psum_scatter(term, "vocab", scatter_dimension=1, tiled=True).astype(
        jnp.bfloat16
    )
    return (hidden_grad, token_kl, sampled, loss)


def solution(mesh):
    return jax.shard_map(
        on_device,
        mesh=mesh,
        in_specs=(P("dp", "vocab"), P("vocab", "dp", None), P("dp", "vocab"), P("dp"), P("dp")),
        out_specs=(P("dp", "vocab"), P("dp"), P("dp"), P()),
        check_vma=False,
    )
```

profile of v0, /device:TPU:0, one launch (start us, length us, event | category | flops | bytes accessed | tf_op | source)
XLA Modules:
  0.0 265.2 jit_solution(2844016320098941567)
XLA Ops:
  7.2 2.9 %constant_dynamic-slice_fusion.1 = (bf16[1,256,2432]{2,1,0:T(8,128)(2,1)S(1)}, bf16[256,2432]{1,0:T(8,128)(2,1)}) fusion(bf16[1,256,4864]{2,1,0:T(8,128)(2,1)} %param.8, s32[]{:T(128)S(6)} %select_n.41, s32[]{:T(128)S(6)} %select_n.42), kind=kLoop, calls=%fused_computation.33 | loop fusion | bytes 4980744 | tf_op jit(solution)/shard_map/dynamic_slice | solution.py:48
  10.1 3.0 %collective-permute-start = (bf16[256,2432]{1,0:T(8,128)(2,1)}, bf16[256,2432]{1,0:T(8,128)(2,1)S(1)}, u32[]{:S(2)}, u32[]{:S(2)}) collective-permute-start(bf16[256,2432]{1,0:T(8,128)(2,1)} %get-tuple-element.160), channel_id=1, source_target_pairs={{0,1},{1,0},{2,3},{3,2},{4,5},{5,4},{6,7},{7,6},{8,9},{9,8},{10,11... | collective-permute-start | bytes 3735560 | tf_op jit(solution)/shard_map/ppermute | solution.py:11
  13.1 27.6 %collective-permute-done = bf16[256,2432]{1,0:T(8,128)(2,1)S(1)} collective-permute-done((bf16[256,2432]{1,0:T(8,128)(2,1)}, bf16[256,2432]{1,0:T(8,128)(2,1)S(1)}, u32[]{:S(2)}, u32[]{:S(2)}) %collective-permute-start) | collective-permute-done | bytes 1245216 | tf_op jit(solution)/shard_map/ppermute | solution.py:11
  40.7 1.8 maximum_select_fusion
  42.6 1.0 copy-done
  43.6 0.3 copy.10
  43.9 0.2 reduce_max.24
  44.1 21.9 %pmax.7 = f32[128]{0:T(128)S(1)} all-reduce(bf16[128]{0:T(256)(128)(2,1)S(1)} %reduce_max.24), channel_id=1, replica_groups=mesh['dp'=4,'vocab'=8] {'vocab'}, use_global_device_ids=true, to_apply=%region_7.8 | all-reduce | flops 128 | bytes 768 | tf_op jit(solution)/shard_map/pmax | solution.py:59
  66.0 0.3 exponential_reduce_fusion
  66.3 17.1 %psum.36 = f32[128]{0:T(128)S(1)} all-reduce(f32[128]{0:T(128)S(1)} %exponential_reduce_fusion), channel_id=1, replica_groups=mesh['dp'=4,'vocab'=8] {'vocab'}, use_global_device_ids=true, to_apply=%region_9.10 | all-reduce | flops 128 | bytes 1024 | tf_op jit(solution)/shard_map/psum | solution.py:60
  83.5 31.2 %all_gather.19 = bf16[128,2048]{1,0:T(8,128)(2,1)S(1)} all-gather(bf16[128,256]{1,0:T(8,128)(2,1)S(1)} %copy-done.1), channel_id=1, replica_groups=mesh['dp'=4,'vocab'=8] {'vocab'}, dimensions={1}, use_global_device_ids=true | all-gather | bytes 589824 | tf_op jit(solution)/shard_map/all_gather | solution.py:46
  114.7 6.6 %fusion.17 = (f32[128]{0:T(128)S(1)}, f32[2432,128]{1,0:T(8,128)S(1)}) fusion(bf16[2048,2432]{1,0:T(8,128)(2,1)} %bitcast.46, bf16[128,2048]{1,0:T(8,128)(2,1)S(1)} %all_gather.19), kind=kOutput, calls=%fused_computation.36 | convolution fusion | flops 1275379584 | bytes 11731456 | tf_op jit(solution)/shard_map/dot_general | solution.py:55
  121.4 0.3 exponential_reduce_fusion.1
  121.7 18.5 %all-gather.3 = f32[8,1,128]{2,1,0:T(1,128)S(1)} all-gather(f32[1,1,128]{2,1,0:T(1,128)S(1)} %bitcast.52), channel_id=3, replica_groups=mesh['dp'=4,'vocab'=8] {'vocab'}, dimensions={0}, use_global_device_ids=true | all-gather | bytes 4608 | tf_op jit(solution)/shard_map/all_gather | solution.py:15
  140.2 16.3 %all-gather.2 = f32[8,1,128]{2,1,0:T(1,128)S(1)} all-gather(f32[1,1,128]{2,1,0:T(1,128)S(1)} %bitcast.51), channel_id=2, replica_groups=mesh['dp'=4,'vocab'=8] {'vocab'}, dimensions={0}, use_global_device_ids=true | all-gather | bytes 4608 | tf_op jit(solution)/shard_map/all_gather | solution.py:15
  156.5 0.3 while.17
  156.8 1.1 fusion.7
  157.9 19.7 %all-reduce = (f32[128]{0:T(128)S(1)}, f32[128]{0:T(128)}) all-reduce(f32[128]{0:T(128)S(1)} %get-tuple-element.140, f32[128]{0:T(128)S(1)} %get-tuple-element.139), channel_id=1, replica_groups=mesh['dp'=4,'vocab'=8] {'vocab'}, use_global_device_ids=true, to_apply=%region_12.13 | all-reduce | flops 256 | bytes 2048 | tf_op jit(solution)/shard_map/psum | solution.py:70
  177.6 0.6 multiply_reduce_fusion
  178.2 6.3 %all-reduce.1 = (f32[]{:T(128)}, f32[]{:T(128)}) all-reduce(f32[]{:T(128)} %get-tuple-element.142, f32[]{:T(128)} %get-tuple-element.141), channel_id=1, replica_groups=mesh['dp'=4,'vocab'=8] {'dp'}, use_global_device_ids=true, to_apply=%region_1.2 | all-reduce | flops 2 | bytes 16 | tf_op jit(solution)/shard_map/psum | solution.py:45
  184.4 0.6 convert_divide_fusion
  185.1 8.2 %fusion.10 = f32[128,2048]{1,0:T(8,128)} fusion(bf16[2048,2432]{1,0:T(8,128)(2,1)} %bitcast.47, bf16[128,2432]{0,1:T(8,128)(2,1)S(1)} %copy.10, f32[2432,128]{1,0:T(8,128)S(1)} %get-tuple-element.162, f32[128]{0:T(128)S(1)} %log.7, f32[128]{0:T(128)S(1)} %pmax.7, f32[128]{0:T(128)S(1)} %log.6, f32[128]{0:T(128)S(1)} %get-tuple-element.137, ...), kind=kOutput, calls=%fused_computation.23 | convolution fusion | flops 1277558784 | bytes 12880384 | tf_op jit(solution)/shard_map/dot_general | solution.py:74
  194.7 61.0 %reduce-scatter.2.cloned.1.call-done = f32[128,256]{1,0:T(8,128)} async-done(((f32[128,2048]{1,0:T(8,128)}), f32[128,256]{1,0:T(8,128)}) %reduce-scatter.2.cloned.1.call-update) | async-done | bytes 131088 | tf_op jit(solution)/shard_map/reduce_scatter | solution.py:77
  255.7 1.5 convert_element_type.16
  (26 shorter events, 0.3 us)
Async XLA Ops:
  7.2 107.5 %all-gather.6.cloned.1.call-start = ((), (), s32[]{:S(2)}) async-start(), calls=%async_computation.1 | async-start | bytes 12451840 | tf_op jit(solution)/shard_map/all_gather | solution.py:54
  10.1 30.5 %collective-permute-start = (bf16[256,2432]{1,0:T(8,128)(2,1)}, bf16[256,2432]{1,0:T(8,128)(2,1)S(1)}, u32[]{:S(2)}, u32[]{:S(2)}) collective-permute-start(bf16[256,2432]{1,0:T(8,128)(2,1)} %get-tuple-element.160), channel_id=1, source_target_pairs={{0,1},{1,0},{2,3},{3,2},{4,5},{5,4},{6,7},{7,6},{8,9},{9,8},{10,11... | collective-permute-start | bytes 3735560 | tf_op jit(solution)/shard_map/ppermute | solution.py:11
  42.5 1.1 copy-start
  42.5 213.1 %reduce-scatter.2.cloned.1.call-start = ((), (), s32[]{:S(2)}) async-start(), calls=%async_computation.2 | async-start | bytes 1179648 | tf_op jit(solution)/shard_map/reduce_scatter | solution.py:77
  43.6 39.9 %copy-start.1 = (bf16[128,256]{1,0:T(8,128)(2,1)S(1)}, bf16[128,256]{1,0:T(8,128)(2,1)}, u32[]{:S(2)}) copy-start(bf16[128,256]{1,0:T(8,128)(2,1)} %param.7) | copy-start | bytes 196612
  121.4 35.4 %copy-start.2 = (s32[128]{0:T(128)S(1)}, s32[128]{0:T(128)}, u32[]{:S(2)}) copy-start(s32[128]{0:T(128)} %param.10) | copy-start | bytes 1540
  121.7 55.9 %copy-start.3 = (s32[128]{0:T(128)S(1)}, s32[128]{0:T(128)}, u32[]{:S(2)}) copy-start(s32[128]{0:T(128)} %param.11) | copy-start | bytes 1540
  177.6 15.8 %copy-start.4 = (f32[128]{0:T(128)}, f32[128]{0:T(128)S(1)}, u32[]{:S(2)}) copy-start(f32[128]{0:T(128)S(1)} %get-tuple-element.153) | copy-start | bytes 1540
Sparse Core Ops, SparseCore 0:
  42.6 68.6 all-gather.5
  193.5 62.1 reduce-scatter.1
where the time goes:
time: 266 us; the launch traced here: 265 us
  blocking collectives  131 us (49%)
  waiting for transfers between devices  88.6 us (33%)
  between operations  16.6 us (6%)
  matrix products  14.9 us (6%)
  other arithmetic  6.81 us (3%)
  local copies, waits for them, and re-layouts  4.23 us (2%)
  starting transfers between devices  3.05 us (1%)
    reduce_scatter x1, waiting for transfers between devices, on_device(): lax.psum_scatter(term, 'vocab', scatter_dimension=1, tiled=True)  61 us
    all_gather x2, blocking collectives, combined_all(): gathered = jax.tree.map(lambda a: lax.all_gather(a, axis), part)  34.7 us
    all_gather x1, blocking collectives, on_device(): gathered = lax.all_gather(student_hidden, 'vocab', axis=1, tiled=True)  31.2 us
    ppermute x1, waiting for transfers between devices, swapped(): lax.ppermute(shard, axis, [(i, i ^ 1 << stride) for i in range(lax.axis_s...  27.6 us
    pmax x1, blocking collectives, on_device(): teacher_max = lax.pmax(jnp.max(teacher_full, axis=1), 'vocab')  21.9 us
    psum x1, blocking collectives, on_device(): token_kl, sampled = lax.psum((kl_part, sampled_part), 'vocab')  19.7 us
    psum x1, blocking collectives, on_device(): lax.psum(jnp.sum(jnp.exp(teacher_full - teacher_max[:, None]), axis=1), '...  17.1 us
    dot_general x1, matrix products, on_device(): lax.dot_general(dlogits, weight, (((1,), (1,)), ((), ())), preferred_elem...  8.22 us
  transfers between devices with their start and end apart: 3, of which 2 were waited for; matrix products, arithmetic and copies ran while one was open for 0% of the time, Pallas kernels for 0%

commit v1 on v0

v1 whole, which is shorter than its diff:
```python
import math

import jax
import jax.numpy as jnp
from jax import lax
from jax.sharding import Mesh, PartitionSpec as P

LANES = 128


def exchanged(array, **flips):
    axes = tuple(flips)
    sizes = [lax.axis_size(axis) for axis in axes]
    pairs = []
    for source in range(math.prod(sizes)):
        rest, target, stride = source, 0, 1
        for axis, size in reversed(list(zip(axes, sizes))):
            target += (rest % size ^ flips[axis]) * stride
            rest, stride = rest // size, stride * size
        pairs.append((source, target))
    return lax.ppermute(array, axes, pairs)


def cube_sum(value, axes):
    for axis in axes:
        for bit in range(lax.axis_size(axis).bit_length() - 1):
            value = value + exchanged(value, **{axis: 1 << bit})
    return value


def on_device(student_hidden, student_blocks, teacher_logits, token_ids, loss_mask):
    row_g, core, slab, half = (lax.axis_index(axis) for axis in ("g", "c", "s", "h"))
    n_g, n_s = lax.axis_size("g"), lax.axis_size("s")
    n_blocks = 4 * n_g
    tokens, feature = student_hidden.shape
    piece = student_blocks[0]
    rows = piece.shape[0]
    vt = piece.shape[1] // 2
    tiles = vt // LANES
    wide_tiles = -(-tiles // n_g)
    width = wide_tiles * LANES

    def offset(g):
        return (g * (tiles - wide_tiles)) // max(n_g - 1, 1) * LANES

    plane = [(mg, mh) for mg in range(n_g) for mh in range(2)]
    far_first = sorted(plane[1:], key=lambda m: (-(m[0] != 0) - m[1], m))

    hidden_plane = {(0, 0): student_hidden}
    for mg, mh in far_first:
        hidden_plane[mg, mh] = exchanged(student_hidden, g=mg, h=mh)

    def columns_of(g, h):
        start = pl_multiple(h * vt + offset(g))
        return lax.dynamic_slice_in_dim(piece, start, width, 1)

    blocks = {(0, 0, 0): columns_of(row_g, half)}
    for mg, mh in far_first:
        blocks[mg, mh, 0] = exchanged(columns_of(row_g ^ mg, half ^ mh), g=mg, h=mh)
    for mg, mh in [(0, 0)] + far_first:
        blocks[mg, mh, 1] = exchanged(blocks[mg, mh, 0], c=1)

    small = jnp.stack([token_ids, loss_mask])
    smalls = [small] + [exchanged(small, g=mg) for mg in range(1, n_g)]
    ids = jnp.concatenate([part[0] for part in smalls])
    mask_float = jnp.concatenate([part[1] for part in smalls]).astype(jnp.float32)
    core_total = jnp.full((8, LANES), jnp.sum(mask_float))
    mask_total = (core_total + exchanged(core_total, c=1))[0, 0]

    sides = [jnp.concatenate([hidden_plane[mg, mh] for mg in range(n_g)]) for mh in range(2)]
    plane_hidden = jnp.where(
        half == 0, jnp.concatenate(sides, axis=1), jnp.concatenate(sides[::-1], axis=1)
    )
    gathered = [plane_hidden] + [exchanged(plane_hidden, s=ms) for ms in range(1, n_s)]
    hidden = jnp.stack(gathered)

    def block_index(mg, mh, mc):
        return (half ^ mh) * 2 * n_g + 2 * (row_g ^ mg) + (core ^ mc)

    def hidden_of(index):
        pair = lax.dynamic_index_in_dim(hidden, slab ^ (index // 2), 0, False)
        return lax.dynamic_slice_in_dim(pair, index % 2 * feature, feature, 1)

    teacher = jnp.concatenate(
        [lax.dynamic_slice_in_dim(teacher_logits, offset(row_g), width, 1)]
        + [
            exchanged(lax.dynamic_slice_in_dim(teacher_logits, offset(row_g ^ mg), width, 1), g=mg)
            for mg in range(1, n_g)
        ]
    ).astype(jnp.float32)

    logits = None
    weight = jnp.zeros((n_blocks, rows, width), piece.dtype)
    for mg, mh in [(0, 0)] + far_first:
        for mc in range(2):
            block = blocks[mg, mh, mc]
            index = block_index(mg, mh, mc)
            if logits is not None:
                block, logits = lax.optimization_barrier((block, logits))
            term = jnp.dot(hidden_of(index), block, preferred_element_type=jnp.float32)
            logits = term if logits is None else logits + term
            place = index % 2 * n_s + index // 2
            weight = lax.dynamic_update_index_in_dim(weight, block, place, 0)

    local_column = lax.broadcasted_iota(jnp.int32, (1, width), 1)
    shared = jnp.where(row_g > 0, offset(row_g - 1) + width - offset(row_g), 0)
    mine = local_column >= shared
    low = jnp.float32(-3e38)
    student_max = jnp.max(jnp.where(mine, logits, low), axis=1)
    teacher_max = jnp.max(jnp.where(mine, teacher, low), axis=1)
    student_shift = logits - student_max[:, None]
    teacher_shift = teacher - teacher_max[:, None]
    student_sum = jnp.sum(jnp.where(mine, jnp.exp(student_shift), 0.0), axis=1)
    teacher_exp = jnp.where(mine, jnp.exp(teacher_shift), 0.0)
    teacher_sum = jnp.sum(teacher_exp, axis=1)
    cross = jnp.sum(teacher_exp * jnp.where(mine, teacher_shift - student_shift, 0.0), axis=1)
    column = local_column + (slab * 2 + half) * vt + offset(row_g)
    hit = (column == ids[:, None]) & mine
    picked = jnp.sum(jnp.where(hit, logits, 0.0), axis=1)

    stats = jnp.stack([student_max, student_sum, teacher_max, teacher_sum, cross, picked])
    stats = stats.reshape(6, n_g, tokens)

    def group(g):
        return lax.dynamic_index_in_dim(stats, g, 1, False)

    in_order = jnp.stack([group(row_g ^ g) for g in range(n_g)], 1)
    sent = jnp.broadcast_to(in_order, (n_g * n_s * 2,) + in_order.shape)
    every = lax.all_to_all(sent, ("g", "s", "h"), 0, 0, tiled=True)
    every = jnp.stack(
        [lax.dynamic_index_in_dim(every, row_g ^ mg, 2, False) for mg in range(n_g)], 2
    ).reshape(-1, 6, n_g * tokens)
    maxes, sums, t_maxes, t_sums, crosses, picks = (every[:, k] for k in range(6))
    top = jnp.max(maxes, axis=0)
    total = jnp.log(jnp.sum(sums * jnp.exp(maxes - top), axis=0))
    t_top = jnp.max(t_maxes, axis=0)
    t_scale = jnp.exp(t_maxes - t_top)
    t_total = jnp.sum(t_sums * t_scale, axis=0)
    t_log = jnp.log(t_total)

    student_logp = logits - top[:, None] - total[:, None]
    teacher_logp = teacher - t_top[:, None] - t_log[:, None]
    factor = (mask_float / mask_total)[:, None]
    delta = factor * (jnp.exp(student_logp) - jnp.exp(teacher_logp))
    dlogits = jnp.where(mine, delta, 0.0).astype(jnp.bfloat16)
    grads = lax.dot_general(
        dlogits,
        weight.reshape(n_blocks * rows, width),
        (((1,), (1,)), ((), ())),
        preferred_element_type=jnp.float32,
    )

    own = slice(0, tokens)
    gap = (t_maxes - t_top - t_log) - (maxes - top - total)
    token_kl = jnp.sum((t_scale * (crosses + t_sums * gap))[:, own], axis=0) / t_total[own]
    sampled = jnp.sum(picks[:, own], axis=0) - top[own] - total[own]
    loss_part = jnp.full((8, LANES), jnp.sum(mask_float[own] * token_kl))
    loss = cube_sum(loss_part, ("g", "c"))[0, 0] / mask_total

    def for_half(mg, h):
        group_rows = grads[mg * tokens : (mg + 1) * tokens]
        return lax.dynamic_slice_in_dim(group_rows, h * n_s * feature, n_s * feature, 1)

    partial = for_half(0, half)
    arrived = [
        exchanged(for_half(mg, half ^ mh).astype(jnp.bfloat16), g=mg, h=mh) for mg, mh in far_first
    ]
    for part in arrived:
        partial = partial + part.astype(jnp.float32)

    def for_slab(s):
        return lax.dynamic_slice_in_dim(partial, s * feature, feature, 1)

    result = for_slab(slab)
    arrived = [
        exchanged(for_slab(slab ^ ms).astype(jnp.bfloat16), s=ms) for ms in range(1, n_s)
    ]
    for part in arrived:
        result = result + part.astype(jnp.float32)
    return (result.astype(jnp.bfloat16), token_kl, sampled, loss)


def pl_multiple(start):
    return start // LANES * LANES


def solution(mesh):
    n_dp, n_vocab = mesh.devices.shape
    split = Mesh(mesh.devices.reshape(n_dp // 2, 2, n_vocab // 2, 2), ("g", "c", "s", "h"))
    dp, vocab = ("g", "c"), ("s", "h")
    return jax.shard_map(
        on_device,
        mesh=split,
        in_specs=(P(dp, vocab), P(vocab, dp, None), P(dp, vocab), P(dp), P(dp)),
        out_specs=(P(dp, vocab), P(dp), P(dp), P()),
        check_vma=False,
    )
```

time: 266 us -> 109 us (0.41)
  blocking collectives: 131 us -> 0 us
  waiting for transfers between devices: 88.6 us -> 41.3 us
  starting transfers between devices: 3.05 us -> 30 us
  between operations: 16.6 us -> 4.06 us
  local copies, waits for them, and re-layouts: 4.23 us -> 16.5 us
  matrix products: 14.9 us -> 8.59 us
    all_gather x3 -> x0, blocking collectives: 66 us -> none  [the longest x2 34.7 us: combined_all(): gathered = jax.tree.map(lambda a: lax.all_gather(a, axis), part)]
    reduce_scatter x1 -> x0, waiting for transfers between devices: 61 us -> none  [on_device(): lax.psum_scatter(term, 'vocab', scatter_dimension=1, tiled=True)]
    psum x3 -> x0, blocking collectives: 43 us -> none  [the longest x1 19.7 us: on_device(): token_kl, sampled = lax.psum((kl_part, sampled_part), 'vocab')]
    ppermute x1 -> x24, starting transfers between devices: 2.97 us -> 26.1 us  [exchanged(): return lax.ppermute(array, axes, pairs)]
    pmax x1 -> x0, blocking collectives: 21.9 us -> none  [on_device(): teacher_max = lax.pmax(jnp.max(teacher_full, axis=1), 'vocab')]
    ppermute x1 -> x24, waiting for transfers between devices: 27.6 us -> 39.3 us  [exchanged(): return lax.ppermute(array, axes, pairs)]
    dynamic_update_slice x0 -> x7, local copies, waits for them, and re-layouts: none -> 7.39 us  [on_device(): weight = lax.dynamic_update_index_in_dim(weight, block, place, 0)]
    dot_general x2 -> x9, matrix products: 14.9 us -> 8.59 us  [the longest x1 4.34 us: on_device(): lax.dot_general(dlogits, weight.reshape(n_blocks * rows, width), (((1,),...]
  transfers between devices with their start and end apart: 3 -> 25, of which waited for: 2 -> 9; matrix products, arithmetic and copies ran while one was open for 0% -> 23% of each run, Pallas kernels for 0% -> 0%
where the time goes in v1:
time: 109 us
  waiting for transfers between devices  41.3 us (38%)
  starting transfers between devices  30 us (28%)
  local copies, waits for them, and re-layouts  16.5 us (15%)
  matrix products  8.59 us (8%)
  other arithmetic  8.5 us (8%)
  between operations  4.06 us (4%)
    ppermute x24, waiting for transfers between devices, exchanged(): return lax.ppermute(array, axes, pairs)  39.3 us
    ppermute x24, starting transfers between devices, exchanged(): return lax.ppermute(array, axes, pairs)  26.1 us
    dynamic_update_slice x7, local copies, waits for them, and re-layouts, on_device(): weight = lax.dynamic_update_index_in_dim(weight, block, place, 0)  7.39 us
    dot_general x1, matrix products, on_device(): lax.dot_general(dlogits, weight.reshape(n_blocks * rows, width), (((1,),...  4.34 us
    dot_general x8, matrix products, on_device(): term = jnp.dot(hidden_of(index), block, preferred_element_type=jnp.float32)  4.25 us
    all_to_all x1, starting transfers between devices, on_device(): every = lax.all_to_all(sent, ('g', 's', 'h'), 0, 0, tiled=True)  3.86 us
    broadcast_in_dim x1, local copies, waits for them, and re-layouts, on_device(): weight = jnp.zeros((n_blocks, rows, width), piece.dtype)  2.64 us
  transfers between devices with their start and end apart: 25, of which 9 were waited for; matrix products, arithmetic and copies ran while one was open for 23% of the time, Pallas kernels for 0%

profile of v1, /device:TPU:0, one launch (start us, length us, event | category | flops | bytes accessed | tf_op | source)
XLA Modules:
  0.0 109.0 jit_solution(9990712080574957215)
XLA Ops:
  0.6 3.0 %collective-permute-start.10 = (bf16[128,256]{1,0:T(8,128)(2,1)}, bf16[128,256]{1,0:T(8,128)(2,1)S(1)}, u32[]{:S(2)}, u32[]{:S(2)}) collective-permute-start(bf16[128,256]{1,0:T(8,128)(2,1)} %param.5), channel_id=1, source_target_pairs={{0,1},{1,0},{16,17},{17,16},{2,3},{3,2},{18,19},{19,18},{4,5},{5,4... | collective-permute-start | bytes 196616 | tf_op jit(solution)/shard_map/ppermute | solution.py:21
  3.7 1.5 %collective-permute-start.11 = (bf16[128,256]{1,0:T(8,128)(2,1)}, bf16[128,256]{1,0:T(8,128)(2,1)S(1)}, u32[]{:S(2)}, u32[]{:S(2)}) collective-permute-start(bf16[128,256]{1,0:T(8,128)(2,1)} %param.5), channel_id=1, source_target_pairs={{0,17},{1,16},{16,1},{17,0},{2,19},{3,18},{18,3},{19,2},{4,21},{5,... | collective-permute-start | bytes 196616 | tf_op jit(solution)/shard_map/ppermute | solution.py:21
  5.2 2.6 %broadcast_in_dim.94 = bf16[8,256,1280]{2,1,0:T(8,128)(2,1)} broadcast(bf16[]{:T(256)} %constant.430.clone.1), dimensions={} | broadcast | bytes 5242882 | tf_op jit(solution)/shard_map/broadcast_in_dim | solution.py:93
  7.9 1.8 %dynamic-slice_bitcast_fusion.2 = (bf16[256,1280]{1,0:T(8,128)(2,1)}, bf16[8,256,1280]{2,1,0:T(8,128)(2,1)}, bf16[256,1280]{1,0:T(8,128)(2,1)}, bf16[256,1280]{1,0:T(8,128)(2,1)}, bf16[256,1280]{1,0:T(8,128)(2,1)}) fusion(bf16[1,256,4864]{2,1,0:T(8,128)(2,1)S(1)} %copy-done, s32[]{:T(128)S(6)} %select_n.308, bf16[8,256,1280]{2,1,0:T(8,128)(2,1)} %broadcast_in_dim.94, ...), kind=kLoop, calls=%fused_computation.37 | loop fusion | bytes 5898260 | tf_op jit(solution)/shard_map/dynamic_slice | solution.py:55
  9.7 2.0 %collective-permute-start = (s32[2,128]{1,0:T(2,128)S(1)}, s32[2,128]{1,0:T(2,128)S(1)}, u32[]{:S(2)}, u32[]{:S(2)}) collective-permute-start(s32[2,128]{1,0:T(2,128)S(1)} %pad_add_fusion), channel_id=1, source_target_pairs={{0,16},{16,0},{1,17},{17,1},{2,18},{18,2},{3,19},{19,3},{4,20},{20... | collective-permute-start | bytes 3080 | tf_op jit(solution)/shard_map/ppermute | solution.py:21
  13.3 2.9 %collective-permute-start.6 = (bf16[256,1280]{1,0:T(8,128)(2,1)}, bf16[256,1280]{1,0:T(8,128)(2,1)S(1)}, u32[]{:S(2)}, u32[]{:S(2)}) collective-permute-start(bf16[256,1280]{1,0:T(8,128)(2,1)} %get-tuple-element.52), channel_id=1, source_target_pairs={{0,17},{1,16},{16,1},{17,0},{2,19},{3,18},{18,3},{19,2},{4,21},{5,... | collective-permute-start | bytes 1966088 | tf_op jit(solution)/shard_map/ppermute | solution.py:21
  17.8 3.7 %collective-permute-start.14 = (bf16[256,512]{1,0:T(8,128)(2,1)S(1)}, bf16[256,512]{1,0:T(8,128)(2,1)S(1)}, u32[]{:S(2)}, u32[]{:S(2)}) collective-permute-start(bf16[256,512]{1,0:T(8,128)(2,1)S(1)} %maximum_select_fusion.1), channel_id=1, source_target_pairs={{0,6},{2,4},{4,2},{6,0},{1,7},{3,5},{5,3},{7,1},{8,14},{10,12},{12... | collective-permute-start | bytes 786440 | tf_op jit(solution)/shard_map/ppermute | solution.py:21
  24.2 4.8 %collective-permute-done.14 = bf16[256,512]{1,0:T(8,128)(2,1)S(1)} collective-permute-done((bf16[256,512]{1,0:T(8,128)(2,1)S(1)}, bf16[256,512]{1,0:T(8,128)(2,1)S(1)}, u32[]{:S(2)}, u32[]{:S(2)}) %collective-permute-start.14) | collective-permute-done | bytes 262176 | tf_op jit(solution)/shard_map/ppermute | solution.py:21
  29.5 14.9 %collective-permute-done.13 = bf16[256,512]{1,0:T(8,128)(2,1)S(1)} collective-permute-done((bf16[256,512]{1,0:T(8,128)(2,1)S(1)}, bf16[256,512]{1,0:T(8,128)(2,1)S(1)}, u32[]{:S(2)}, u32[]{:S(2)}) %collective-permute-start.13) | collective-permute-done | bytes 262176 | tf_op jit(solution)/shard_map/ppermute | solution.py:21
  45.0 1.5 %collective-permute-start.15 = (bf16[128,1280]{1,0:T(8,128)(2,1)S(1)}, bf16[128,1280]{1,0:T(8,128)(2,1)S(1)}, u32[]{:S(2)}, u32[]{:S(2)}) collective-permute-start(bf16[128,1280]{1,0:T(8,128)(2,1)S(1)} %copy-done.7), channel_id=1, source_target_pairs={{0,16},{16,0},{1,17},{17,1},{2,18},{18,2},{3,19},{19,3},{4,20},{20... | collective-permute-start | bytes 983048 | tf_op jit(solution)/shard_map/ppermute | solution.py:21
  46.6 1.5 %fusion.37 = f32[256,1280]{1,0:T(8,128)S(1)} fusion(bf16[256,1280]{1,0:T(8,128)(2,1)} %get-tuple-element.51, bf16[4,256,512]{2,1,0:T(8,128)(2,1)S(1)} %pad_maximum_fusion, s32[]{:T(128)S(6)} %select_n.321, s32[]{:T(128)S(6)} %select_n.324), kind=kOutput, calls=%fused_computation.62 | convolution fusion | flops 167772160 | bytes 2097160 | tf_op jit(solution)/shard_map/dot_general | solution.py:100
  51.6 10.7 %collective-permute-done.2 = bf16[256,1280]{1,0:T(8,128)(2,1)S(1)} collective-permute-done((bf16[256,1280]{1,0:T(8,128)(2,1)}, bf16[256,1280]{1,0:T(8,128)(2,1)S(1)}, u32[]{:S(2)}, u32[]{:S(2)}) %collective-permute-start.2) | collective-permute-done | bytes 655392 | tf_op jit(solution)/shard_map/ppermute | solution.py:21
  65.2 2.7 %collective-permute-done.15 = bf16[128,1280]{1,0:T(8,128)(2,1)S(1)} collective-permute-done((bf16[128,1280]{1,0:T(8,128)(2,1)S(1)}, bf16[128,1280]{1,0:T(8,128)(2,1)S(1)}, u32[]{:S(2)}, u32[]{:S(2)}) %collective-permute-start.15) | collective-permute-done | bytes 327712 | tf_op jit(solution)/shard_map/ppermute | solution.py:21
  68.3 1.1 fusion.5
  70.1 3.9 %all-to-all-start = ((f32[16,6,2,128]{3,2,1,0:T(2,128)}), f32[16,6,2,128]{3,2,1,0:T(2,128)S(1)}, u32[]{:S(2)}, u32[]{:S(2)}) async-start(f32[16,6,2,128]{3,2,1,0:T(2,128)} %broadcast_in_dim.93), calls=%async_computation | async-start | bytes 196608 | tf_op jit(solution)/shard_map/all_to_all | solution.py:129
  74.0 2.0 %bitcast_dynamic-update-slice_fusion.4 = bf16[8,256,1280]{2,1,0:T(8,128)(2,1)} fusion(bf16[8,256,1280]{2,1,0:T(8,128)(2,1)} %bitcast_dynamic-update-slice_fusion.5, s32[]{:T(128)S(6)} %select_n.381, bf16[256,1280]{1,0:T(8,128)(2,1)} %copy-done.1), kind=kLoop, calls=%fused_computation.27 | loop fusion | bytes 1310724 | tf_op jit(solution)/shard_map/jit(dynamic_update_index_in_dim)/dynamic_update_slice | solution.py:103
  79.6 2.0 %all-to-all-done = f32[16,6,2,128]{3,2,1,0:T(2,128)S(1)} async-done(((f32[16,6,2,128]{3,2,1,0:T(2,128)}), f32[16,6,2,128]{3,2,1,0:T(2,128)S(1)}, u32[]{:S(2)}, u32[]{:S(2)}) %all-to-all-start) | async-done | bytes 98336 | tf_op jit(solution)/shard_map/all_to_all | solution.py:129
  82.1 4.3 %fusion.14 = f32[256,2048]{1,0:T(8,128)S(1)} fusion(bf16[2048,1280]{1,0:T(8,128)(2,1)} %bitcast.39, f32[256,1280]{1,0:T(8,128)S(1)} %get-tuple-element.47, f32[256]{0:T(256)S(1)} %log.23, f32[256]{0:T(256)S(1)} %get-tuple-element.63, f32[256]{0:T(256)S(1)} %log.22, f32[256]{0:T(256)S(1)} %get-tuple-element.64, f32[256]{0:T(256)S(1)} %broadcast_divide_fusion, ...), kind=kOutput, calls=%fused_computation.21 | convolution fusion | flops 1346109440 | bytes 9312512 | tf_op jit(solution)/shard_map/dot_general | solution.py:146
  88.4 2.0 %collective-permute-start.16 = (bf16[128,1024]{1,0:T(8,128)(2,1)S(1)}, bf16[128,1024]{1,0:T(8,128)(2,1)S(1)}, u32[]{:S(2)}, u32[]{:S(2)}) collective-permute-start(bf16[128,1024]{1,0:T(8,128)(2,1)S(1)} %get-tuple-element.58), channel_id=1, source_target_pairs={{0,17},{1,16},{16,1},{17,0},{2,19},{3,18},{18,3},{19,2},{4,21},{5,... | collective-permute-start | bytes 786440 | tf_op jit(solution)/shard_map/ppermute | solution.py:21
  90.9 1.1 %multiply_reduce_fusion.1 = (f32[]{:T(128)}, f32[128]{0:T(128)}) fusion(f32[256]{0:T(256)S(1)} %add_convert_fusion.1, f32[128]{0:T(128)S(1)} %fusion.57, f32[256]{0:T(256)S(1)} %get-tuple-element.37), kind=kLoop, calls=%fused_computation.128 | loop fusion | flops 383 | bytes 2052 | tf_op jit(solution)/shard_map/reduce_sum | solution.py:157
  93.5 2.8 %collective-permute-done.22 = f32[8,128]{1,0:T(8,128)S(1)} collective-permute-done((f32[8,128]{1,0:T(8,128)S(1)}, f32[8,128]{1,0:T(8,128)S(1)}, u32[]{:S(2)}, u32[]{:S(2)}) %collective-permute-start.22) | collective-permute-done | bytes 4128 | tf_op jit(solution)/shard_map/ppermute | solution.py:21
  97.1 2.1 %collective-permute-done.16 = bf16[128,1024]{1,0:T(8,128)(2,1)S(1)} collective-permute-done((bf16[128,1024]{1,0:T(8,128)(2,1)S(1)}, bf16[128,1024]{1,0:T(8,128)(2,1)S(1)}, u32[]{:S(2)}, u32[]{:S(2)}) %collective-permute-start.16) | collective-permute-done | bytes 262176 | tf_op jit(solution)/shard_map/ppermute | solution.py:21
  99.4 2.6 %collective-permute-start.21 = (bf16[128,256]{1,0:T(8,128)(2,1)S(1)}, bf16[128,256]{1,0:T(8,128)(2,1)S(1)}, u32[]{:S(2)}, u32[]{:S(2)}) collective-permute-start(bf16[128,256]{1,0:T(8,128)(2,1)S(1)} %get-tuple-element.56), channel_id=1, source_target_pairs={{0,6},{2,4},{4,2},{6,0},{1,7},{3,5},{5,3},{7,1},{8,14},{10,12},{12... | collective-permute-start | bytes 196616 | tf_op jit(solution)/shard_map/ppermute | solution.py:21
  102.0 1.9 %collective-permute-start.19 = (bf16[128,256]{1,0:T(8,128)(2,1)S(1)}, bf16[128,256]{1,0:T(8,128)(2,1)S(1)}, u32[]{:S(2)}, u32[]{:S(2)}) collective-permute-start(bf16[128,256]{1,0:T(8,128)(2,1)S(1)} %get-tuple-element.55), channel_id=1, source_target_pairs={{0,2},{2,0},{4,6},{6,4},{1,3},{3,1},{5,7},{7,5},{8,10},{10,8},{12,... | collective-permute-start | bytes 196616 | tf_op jit(solution)/shard_map/ppermute | solution.py:21
  (130 shorter events, 25.3 us)
Async XLA Ops:
  0.6 16.2 %collective-permute-start.10 = (bf16[128,256]{1,0:T(8,128)(2,1)}, bf16[128,256]{1,0:T(8,128)(2,1)S(1)}, u32[]{:S(2)}, u32[]{:S(2)}) collective-permute-start(bf16[128,256]{1,0:T(8,128)(2,1)} %param.5), channel_id=1, source_target_pairs={{0,1},{1,0},{16,17},{17,16},{2,3},{3,2},{18,19},{19,18},{4,5},{5,4... | collective-permute-start | bytes 196616 | tf_op jit(solution)/shard_map/ppermute | solution.py:21
  3.7 14.0 %collective-permute-start.11 = (bf16[128,256]{1,0:T(8,128)(2,1)}, bf16[128,256]{1,0:T(8,128)(2,1)S(1)}, u32[]{:S(2)}, u32[]{:S(2)}) collective-permute-start(bf16[128,256]{1,0:T(8,128)(2,1)} %param.5), channel_id=1, source_target_pairs={{0,17},{1,16},{16,1},{17,0},{2,19},{3,18},{18,3},{19,2},{4,21},{5,... | collective-permute-start | bytes 196616 | tf_op jit(solution)/shard_map/ppermute | solution.py:21
  5.2 12.5 %collective-permute-start.9 = (bf16[128,256]{1,0:T(8,128)(2,1)}, bf16[128,256]{1,0:T(8,128)(2,1)S(1)}, u32[]{:S(2)}, u32[]{:S(2)}) collective-permute-start(bf16[128,256]{1,0:T(8,128)(2,1)} %param.5), channel_id=1, source_target_pairs={{0,16},{1,17},{16,0},{17,1},{2,18},{3,19},{18,2},{19,3},{4,20},{5,... | collective-permute-start | bytes 196616 | tf_op jit(solution)/shard_map/ppermute | solution.py:21
  9.7 38.4 %collective-permute-start.8 = (bf16[256,1280]{1,0:T(8,128)(2,1)}, bf16[256,1280]{1,0:T(8,128)(2,1)S(1)}, u32[]{:S(2)}, u32[]{:S(2)}) collective-permute-start(bf16[256,1280]{1,0:T(8,128)(2,1)} %get-tuple-element.51), channel_id=1, source_target_pairs={{0,8},{8,0},{1,9},{9,1},{2,10},{10,2},{3,11},{11,3},{4,12},{12,4},... | collective-permute-start | bytes 1966088 | tf_op jit(solution)/shard_map/ppermute | solution.py:21
  9.7 3.6 %collective-permute-start = (s32[2,128]{1,0:T(2,128)S(1)}, s32[2,128]{1,0:T(2,128)S(1)}, u32[]{:S(2)}, u32[]{:S(2)}) collective-permute-start(s32[2,128]{1,0:T(2,128)S(1)} %pad_add_fusion), channel_id=1, source_target_pairs={{0,16},{16,0},{1,17},{17,1},{2,18},{18,2},{3,19},{19,3},{4,20},{20... | collective-permute-start | bytes 3080 | tf_op jit(solution)/shard_map/ppermute | solution.py:21
  13.3 35.3 %collective-permute-start.6 = (bf16[256,1280]{1,0:T(8,128)(2,1)}, bf16[256,1280]{1,0:T(8,128)(2,1)S(1)}, u32[]{:S(2)}, u32[]{:S(2)}) collective-permute-start(bf16[256,1280]{1,0:T(8,128)(2,1)} %get-tuple-element.52), channel_id=1, source_target_pairs={{0,17},{1,16},{16,1},{17,0},{2,19},{3,18},{18,3},{19,2},{4,21},{5,... | collective-permute-start | bytes 1966088 | tf_op jit(solution)/shard_map/ppermute | solution.py:21
  17.5 3.9 %collective-permute-start.1 = (f32[8,128]{1,0:T(8,128)S(1)}, f32[8,128]{1,0:T(8,128)S(1)}, u32[]{:S(2)}, u32[]{:S(2)}) collective-permute-start(f32[8,128]{1,0:T(8,128)S(1)} %broadcast_in_dim.90), channel_id=1, source_target_pairs={{0,8},{8,0},{1,9},{9,1},{2,10},{10,2},{3,11},{11,3},{4,12},{12,4},... | collective-permute-start | bytes 12296 | tf_op jit(solution)/shard_map/ppermute | solution.py:21
  17.8 11.2 %collective-permute-start.14 = (bf16[256,512]{1,0:T(8,128)(2,1)S(1)}, bf16[256,512]{1,0:T(8,128)(2,1)S(1)}, u32[]{:S(2)}, u32[]{:S(2)}) collective-permute-start(bf16[256,512]{1,0:T(8,128)(2,1)S(1)} %maximum_select_fusion.1), channel_id=1, source_target_pairs={{0,6},{2,4},{4,2},{6,0},{1,7},{3,5},{5,3},{7,1},{8,14},{10,12},{12... | collective-permute-start | bytes 786440 | tf_op jit(solution)/shard_map/ppermute | solution.py:21
  21.5 23.0 %collective-permute-start.13 = (bf16[256,512]{1,0:T(8,128)(2,1)S(1)}, bf16[256,512]{1,0:T(8,128)(2,1)S(1)}, u32[]{:S(2)}, u32[]{:S(2)}) collective-permute-start(bf16[256,512]{1,0:T(8,128)(2,1)S(1)} %maximum_select_fusion.1), channel_id=1, source_target_pairs={{0,4},{2,6},{4,0},{6,2},{1,5},{3,7},{5,1},{7,3},{8,12},{10,14},{12... | collective-permute-start | bytes 786440 | tf_op jit(solution)/shard_map/ppermute | solution.py:21
  21.5 23.5 %collective-permute-start.12 = (bf16[256,512]{1,0:T(8,128)(2,1)S(1)}, bf16[256,512]{1,0:T(8,128)(2,1)S(1)}, u32[]{:S(2)}, u32[]{:S(2)}) collective-permute-start(bf16[256,512]{1,0:T(8,128)(2,1)S(1)} %maximum_select_fusion.1), channel_id=1, source_target_pairs={{0,2},{2,0},{4,6},{6,4},{1,3},{3,1},{5,7},{7,5},{8,10},{10,8},{12,... | collective-permute-start | bytes 786440 | tf_op jit(solution)/shard_map/ppermute | solution.py:21
  29.0 20.6 %collective-permute-start.4 = (bf16[256,1280]{1,0:T(8,128)(2,1)}, bf16[256,1280]{1,0:T(8,128)(2,1)S(1)}, u32[]{:S(2)}, u32[]{:S(2)}) collective-permute-start(bf16[256,1280]{1,0:T(8,128)(2,1)} %get-tuple-element.50), channel_id=1, source_target_pairs={{0,1},{1,0},{16,17},{17,16},{2,3},{3,2},{18,19},{19,18},{4,5},{5,4... | collective-permute-start | bytes 1966088 | tf_op jit(solution)/shard_map/ppermute | solution.py:21
  44.4 17.8 %collective-permute-start.2 = (bf16[256,1280]{1,0:T(8,128)(2,1)}, bf16[256,1280]{1,0:T(8,128)(2,1)S(1)}, u32[]{:S(2)}, u32[]{:S(2)}) collective-permute-start(bf16[256,1280]{1,0:T(8,128)(2,1)} %get-tuple-element.48), channel_id=1, source_target_pairs={{0,16},{1,17},{16,0},{17,1},{2,18},{3,19},{18,2},{19,3},{4,20},{5,... | collective-permute-start | bytes 1966088 | tf_op jit(solution)/shard_map/ppermute | solution.py:21
  45.0 23.0 %collective-permute-start.15 = (bf16[128,1280]{1,0:T(8,128)(2,1)S(1)}, bf16[128,1280]{1,0:T(8,128)(2,1)S(1)}, u32[]{:S(2)}, u32[]{:S(2)}) collective-permute-start(bf16[128,1280]{1,0:T(8,128)(2,1)S(1)} %copy-done.7), channel_id=1, source_target_pairs={{0,16},{16,0},{1,17},{17,1},{2,18},{18,2},{3,19},{19,3},{4,20},{20... | collective-permute-start | bytes 983048 | tf_op jit(solution)/shard_map/ppermute | solution.py:21
  48.7 13.6 %collective-permute-start.7 = (bf16[256,1280]{1,0:T(8,128)(2,1)S(1)}, bf16[256,1280]{1,0:T(8,128)(2,1)S(1)}, u32[]{:S(2)}, u32[]{:S(2)}) collective-permute-start(bf16[256,1280]{1,0:T(8,128)(2,1)S(1)} %collective-permute-done.6), channel_id=1, source_target_pairs={{0,8},{8,0},{1,9},{9,1},{2,10},{10,2},{3,11},{11,3},{4,12},{12,4},... | collective-permute-start | bytes 1966088 | tf_op jit(solution)/shard_map/ppermute | solution.py:21
  49.6 13.7 %collective-permute-start.5 = (bf16[256,1280]{1,0:T(8,128)(2,1)S(1)}, bf16[256,1280]{1,0:T(8,128)(2,1)S(1)}, u32[]{:S(2)}, u32[]{:S(2)}) collective-permute-start(bf16[256,1280]{1,0:T(8,128)(2,1)S(1)} %collective-permute-done.4), channel_id=1, source_target_pairs={{0,8},{8,0},{1,9},{9,1},{2,10},{10,2},{3,11},{11,3},{4,12},{12,4},... | collective-permute-start | bytes 1966088 | tf_op jit(solution)/shard_map/ppermute | solution.py:21
  70.1 11.5 %all-to-all-start = ((f32[16,6,2,128]{3,2,1,0:T(2,128)}), f32[16,6,2,128]{3,2,1,0:T(2,128)S(1)}, u32[]{:S(2)}, u32[]{:S(2)}) async-start(f32[16,6,2,128]{3,2,1,0:T(2,128)} %broadcast_in_dim.93), calls=%async_computation | async-start | bytes 196608 | tf_op jit(solution)/shard_map/all_to_all | solution.py:129
  86.7 10.4 %collective-permute-start.18 = (bf16[128,1024]{1,0:T(8,128)(2,1)S(1)}, bf16[128,1024]{1,0:T(8,128)(2,1)S(1)}, u32[]{:S(2)}, u32[]{:S(2)}) collective-permute-start(bf16[128,1024]{1,0:T(8,128)(2,1)S(1)} %get-tuple-element.59), channel_id=1, source_target_pairs={{0,16},{1,17},{16,0},{17,1},{2,18},{3,19},{18,2},{19,3},{4,20},{5,... | collective-permute-start | bytes 786440 | tf_op jit(solution)/shard_map/ppermute | solution.py:21
  87.5 9.5 %collective-permute-start.17 = (bf16[128,1024]{1,0:T(8,128)(2,1)S(1)}, bf16[128,1024]{1,0:T(8,128)(2,1)S(1)}, u32[]{:S(2)}, u32[]{:S(2)}) collective-permute-start(bf16[128,1024]{1,0:T(8,128)(2,1)S(1)} %dynamic-slice_convert_fusion.1), channel_id=1, source_target_pairs={{0,1},{1,0},{16,17},{17,16},{2,3},{3,2},{18,19},{19,18},{4,5},{5,4... | collective-permute-start | bytes 786440 | tf_op jit(solution)/shard_map/ppermute | solution.py:21
  88.4 10.9 %collective-permute-start.16 = (bf16[128,1024]{1,0:T(8,128)(2,1)S(1)}, bf16[128,1024]{1,0:T(8,128)(2,1)S(1)}, u32[]{:S(2)}, u32[]{:S(2)}) collective-permute-start(bf16[128,1024]{1,0:T(8,128)(2,1)S(1)} %get-tuple-element.58), channel_id=1, source_target_pairs={{0,17},{1,16},{16,1},{17,0},{2,19},{3,18},{18,3},{19,2},{4,21},{5,... | collective-permute-start | bytes 786440 | tf_op jit(solution)/shard_map/ppermute | solution.py:21
  92.7 3.7 %collective-permute-start.22 = (f32[8,128]{1,0:T(8,128)S(1)}, f32[8,128]{1,0:T(8,128)S(1)}, u32[]{:S(2)}, u32[]{:S(2)}) collective-permute-start(f32[8,128]{1,0:T(8,128)S(1)} %broadcast_in_dim.102), channel_id=1, source_target_pairs={{0,16},{16,0},{1,17},{17,1},{2,18},{18,2},{3,19},{19,3},{4,20},{20... | collective-permute-start | bytes 12296 | tf_op jit(solution)/shard_map/ppermute | solution.py:21
  97.0 6.9 %collective-permute-start.23 = (f32[8,128]{1,0:T(8,128)S(1)}, f32[8,128]{1,0:T(8,128)S(1)}, u32[]{:S(2)}, u32[]{:S(2)}) collective-permute-start(f32[8,128]{1,0:T(8,128)S(1)} %broadcast_add_fusion), channel_id=1, source_target_pairs={{0,8},{8,0},{1,9},{9,1},{2,10},{10,2},{3,11},{11,3},{4,12},{12,4},... | collective-permute-start | bytes 12296 | tf_op jit(solution)/shard_map/ppermute | solution.py:21
  99.4 7.0 %collective-permute-start.21 = (bf16[128,256]{1,0:T(8,128)(2,1)S(1)}, bf16[128,256]{1,0:T(8,128)(2,1)S(1)}, u32[]{:S(2)}, u32[]{:S(2)}) collective-permute-start(bf16[128,256]{1,0:T(8,128)(2,1)S(1)} %get-tuple-element.56), channel_id=1, source_target_pairs={{0,6},{2,4},{4,2},{6,0},{1,7},{3,5},{5,3},{7,1},{8,14},{10,12},{12... | collective-permute-start | bytes 196616 | tf_op jit(solution)/shard_map/ppermute | solution.py:21
  102.0 5.2 %collective-permute-start.20 = (bf16[128,256]{1,0:T(8,128)(2,1)S(1)}, bf16[128,256]{1,0:T(8,128)(2,1)S(1)}, u32[]{:S(2)}, u32[]{:S(2)}) collective-permute-start(bf16[128,256]{1,0:T(8,128)(2,1)S(1)} %get-tuple-element.57), channel_id=1, source_target_pairs={{0,4},{2,6},{4,0},{6,2},{1,5},{3,7},{5,1},{7,3},{8,12},{10,14},{12... | collective-permute-start | bytes 196616 | tf_op jit(solution)/shard_map/ppermute | solution.py:21
  102.0 5.2 %collective-permute-start.19 = (bf16[128,256]{1,0:T(8,128)(2,1)S(1)}, bf16[128,256]{1,0:T(8,128)(2,1)S(1)}, u32[]{:S(2)}, u32[]{:S(2)}) collective-permute-start(bf16[128,256]{1,0:T(8,128)(2,1)S(1)} %get-tuple-element.55), channel_id=1, source_target_pairs={{0,2},{2,0},{4,6},{6,4},{1,3},{3,1},{5,7},{7,5},{8,10},{10,8},{12,... | collective-permute-start | bytes 196616 | tf_op jit(solution)/shard_map/ppermute | solution.py:21
  (14 other events, 67.7 us)

commit v2 on v1

v2 whole, which is shorter than its diff:
```python
import math

import jax
import jax.numpy as jnp
from jax import lax
from jax.sharding import Mesh, PartitionSpec as P

LANES = 128


def exchanged(array, **flips):
    axes = tuple(flips)
    sizes = [lax.axis_size(axis) for axis in axes]
    pairs = []
    for source in range(math.prod(sizes)):
        rest, target, stride = source, 0, 1
        for axis, size in reversed(list(zip(axes, sizes))):
            target += (rest % size ^ flips[axis]) * stride
            rest, stride = rest // size, stride * size
        pairs.append((source, target))
    return lax.ppermute(array, axes, pairs)


def from_every(array, axes):
    return lax.all_to_all(array, axes, 0, 0, tiled=True)


def on_device(student_hidden, student_blocks, teacher_logits, token_ids, loss_mask):
    row_g, core, slab, half = (lax.axis_index(axis) for axis in ("g", "c", "s", "h"))
    n_g, n_s = lax.axis_size("g"), lax.axis_size("s")
    tokens, feature = student_hidden.shape
    piece = student_blocks[0]
    rows = piece.shape[0]
    vt = piece.shape[1] // 2
    tiles = vt // LANES
    wide_tiles = -(-tiles // n_g)
    width = wide_tiles * LANES

    def offset(g):
        return (g * (tiles - wide_tiles)) // max(n_g - 1, 1) * LANES

    plane = [(mg, mh) for mh in range(2) for mg in range(n_g)]
    far_first = sorted(plane[1:], key=lambda m: (-(m[0] != 0) - m[1], m))

    hidden_plane = {(0, 0): student_hidden}
    for mg, mh in far_first:
        hidden_plane[mg, mh] = exchanged(student_hidden, g=mg, h=mh)

    def columns_of(g, h):
        return lax.dynamic_slice_in_dim(piece, h * vt + offset(g), width, 1)

    blocks = {(0, 0, 0): columns_of(row_g, half)}
    for mg, mh in far_first:
        cut = columns_of(row_g ^ mg, half ^ mh)
        blocks[mg, mh, 0] = exchanged(cut, g=mg, h=mh)
    for mg, mh in [(0, 0)] + far_first:
        blocks[mg, mh, 1] = exchanged(blocks[mg, mh, 0], c=1)

    small = jnp.stack([token_ids, loss_mask])
    smalls = [small] + [exchanged(small, g=mg) for mg in range(1, n_g)]
    ids = jnp.concatenate([part[0] for part in smalls])
    mask_float = jnp.concatenate([part[1] for part in smalls]).astype(jnp.float32)
    core_total = jnp.full((8, LANES), jnp.sum(mask_float))
    mask_total = (core_total + exchanged(core_total, c=1))[0, 0]
    factor = (mask_float / mask_total)[:, None]

    local = teacher_logits.astype(jnp.float32)
    local_max = jnp.max(local, axis=1)
    local_sum = jnp.sum(jnp.exp(local - local_max[:, None]), axis=1)
    sent = jnp.broadcast_to(jnp.stack([local_max, local_sum]), (2 * n_s, 2, tokens))
    pairs = from_every(sent, ("s", "h"))
    t_top = jnp.max(pairs[:, 0], axis=0)
    t_log = jnp.log(jnp.sum(pairs[:, 1] * jnp.exp(pairs[:, 0] - t_top), axis=0))
    norm = jnp.stack([t_top, t_log])
    norms = [norm] + [exchanged(norm, g=mg) for mg in range(1, n_g)]
    t_top, t_log = jnp.concatenate(norms, axis=1)

    def teacher_of(g):
        return lax.dynamic_slice_in_dim(teacher_logits, offset(g), width, 1)

    teacher = jnp.concatenate(
        [teacher_of(row_g)]
        + [exchanged(teacher_of(row_g ^ mg), g=mg) for mg in range(1, n_g)]
    ).astype(jnp.float32)

    sides = [jnp.concatenate([hidden_plane[mg, mh] for mg in range(n_g)]) for mh in range(2)]
    plane_hidden = jnp.where(
        half == 0, jnp.concatenate(sides, axis=1), jnp.concatenate(sides[::-1], axis=1)
    )
    gathered = [plane_hidden]
    gathered += [exchanged(plane_hidden, s=ms) for ms in range(1, n_s)]
    hidden = jnp.stack(gathered)

    def hidden_of(mg, mh, mc):
        index = (half ^ mh) * 2 * n_g + 2 * (row_g ^ mg) + (core ^ mc)
        pair = lax.dynamic_index_in_dim(hidden, slab ^ (index // 2), 0, False)
        return lax.dynamic_slice_in_dim(pair, index % 2 * feature, feature, 1)

    logits = None
    for mg, mh in [(0, 0)] + far_first:
        for mc in range(2):
            block = blocks[mg, mh, mc]
            if logits is not None:
                block, logits = lax.optimization_barrier((block, logits))
            term = jnp.dot(hidden_of(mg, mh, mc), block, preferred_element_type=jnp.float32)
            logits = term if logits is None else logits + term

    local_column = lax.broadcasted_iota(jnp.int32, (1, width), 1)
    shared = jnp.where(row_g > 0, offset(row_g - 1) + width - offset(row_g), 0)
    mine = local_column >= shared

    def by_group(stack):
        parts = stack.reshape(stack.shape[0], n_g, tokens)
        return jnp.stack(
            [lax.dynamic_index_in_dim(parts, row_g ^ g, 1, False) for g in range(n_g)]
        )

    local_max = jnp.max(jnp.where(mine, logits, jnp.float32(-3e38)), axis=1)
    local_sum = jnp.sum(jnp.where(mine, jnp.exp(logits - local_max[:, None]), 0.0), axis=1)
    sent = by_group(jnp.stack([local_max, local_sum]))
    every = from_every(jnp.broadcast_to(sent, (2 * n_s * n_g,) + sent.shape), ("g", "s", "h"))
    every = jnp.concatenate(
        [lax.dynamic_index_in_dim(every, row_g ^ mg, 1, False) for mg in range(n_g)], 2
    )
    top = jnp.max(every[:, 0], axis=0)
    log_total = jnp.log(jnp.sum(every[:, 1] * jnp.exp(every[:, 0] - top), axis=0))

    student_logp = logits - top[:, None] - log_total[:, None]
    teacher_logp = teacher - t_top[:, None] - t_log[:, None]
    teacher_prob = jnp.exp(teacher_logp)
    delta = factor * (jnp.exp(student_logp) - teacher_prob)
    dlogits = jnp.where(mine, delta, 0.0).astype(jnp.bfloat16)

    weight = jnp.concatenate([blocks[mg, mh, mc] for mc in range(2) for mg, mh in plane])
    grads = lax.dot_general(
        dlogits, weight, (((1,), (1,)), ((), ())), preferred_element_type=jnp.float32
    )
    wide = len(plane) * rows

    def for_half(mg, mh):
        group_rows = grads[mg * tokens : (mg + 1) * tokens]
        return lax.dynamic_slice_in_dim(group_rows, (core ^ half ^ mh) * wide, wide, 1)

    partial = for_half(0, 0)
    arrived = [
        (exchanged(for_half(mg, mh).astype(jnp.bfloat16), g=mg, h=mh), mg, mh)
        for mg, mh in far_first
    ]
    for part, kg, kh in arrived:
        order = [(mh ^ kh) * n_g + (mg ^ kg) for mg, mh in plane]
        part = jnp.concatenate([part[:, j * rows : (j + 1) * rows] for j in order], axis=1)
        partial = partial + part.astype(jnp.float32)

    kl_part = jnp.sum(jnp.where(mine, teacher_prob * (teacher_logp - student_logp), 0.0), axis=1)
    column = local_column + (slab * 2 + half) * vt + offset(row_g)
    hit = (column == ids[:, None]) & mine
    picked = jnp.sum(jnp.where(hit, logits, 0.0), axis=1)
    loss_part = jnp.broadcast_to(jnp.sum(mask_float * kl_part), kl_part.shape)
    sent = by_group(jnp.stack([kl_part, picked, loss_part]))
    sent = jnp.broadcast_to(sent[:, None], (n_g, 2 * n_s) + sent.shape[1:])
    every = from_every(sent.reshape(-1, 3, tokens), ("g", "s", "h"))
    token_kl, picked, core_loss = jnp.sum(every, axis=0)
    sampled = picked - top[:tokens] - log_total[:tokens]
    core_loss = jnp.broadcast_to(core_loss, (8, LANES))
    loss = (core_loss + exchanged(core_loss, c=1))[0, 0] / mask_total

    def for_slab(s):
        index = (half ^ (s // n_g)) * n_g + (row_g ^ (s % n_g))
        return lax.dynamic_slice_in_dim(partial, index * rows, rows, 1)

    result = for_slab(slab)
    arrived = [exchanged(for_slab(slab ^ ms).astype(jnp.bfloat16), s=ms) for ms in range(1, n_s)]
    for part in arrived:
        result = result + part.astype(jnp.float32)
    return (result.astype(jnp.bfloat16), token_kl, sampled, loss)


def solution(mesh):
    n_dp, n_vocab = mesh.devices.shape
    n_g, n_s = n_dp // 2, n_vocab // 2
    split = Mesh(mesh.devices.reshape(n_g, 2, n_s, 2), ("g", "c", "s", "h"))
    dp, vocab = ("g", "c"), ("s", "h")
    return jax.shard_map(
        on_device,
        mesh=split,
        in_specs=(P(dp, vocab), P(vocab, dp, None), P(dp, vocab), P(dp), P(dp)),
        out_specs=(P(dp, vocab), P(dp), P(dp), P()),
        check_vma=False,
    )
```

time: 109 us -> 144 us (1.32)
  starting transfers between devices: 30 us -> 48.1 us
  waiting for transfers between devices: 41.3 us -> 57.3 us
  local copies, waits for them, and re-layouts: 16.5 us -> 18.6 us
    all_to_all x1 -> x3, starting transfers between devices: 3.86 us -> 21.6 us  [from_every(): return lax.all_to_all(array, axes, 0, 0, tiled=True)]
    ppermute x24, waiting for transfers between devices: 39.3 us -> 52.6 us  [exchanged(): return lax.ppermute(array, axes, pairs)]
    unnamed x31 -> x19, local copies, waits for them, and re-layouts: 0.42 us -> 8.26 us
    dynamic_update_slice x7 -> x0, local copies, waits for them, and re-layouts: 7.39 us -> none  [on_device(): weight = lax.dynamic_update_index_in_dim(weight, block, place, 0)]
    all_to_all x1 -> x3, waiting for transfers between devices: 2.04 us -> 4.73 us  [from_every(): return lax.all_to_all(array, axes, 0, 0, tiled=True)]
    broadcast_in_dim x3 -> x4, local copies, waits for them, and re-layouts: 3.95 us -> 1.85 us  [the longest x1 0.62 us: on_device(): jnp.broadcast_to(sent, (2 * n_s * n_g,) + sent.shape)]
    dynamic_slice x4 -> x3, local copies, waits for them, and re-layouts: 2.69 us -> 3.48 us  [the longest x1 2.56 us: columns_of(): return lax.dynamic_slice_in_dim(piece, h * vt + offset(g), width, 1)]
    reduce_sum x6 -> x7, other arithmetic: 2.87 us -> 3.28 us  [the longest x1 1.85 us: on_device(): jnp.sum(jnp.where(mine, teacher_prob * (teacher_logp - student_logp), 0.0...]
  transfers between devices with their start and end apart: 25 -> 27, of which waited for: 9 -> 10; matrix products, arithmetic and copies ran while one was open for 23% -> 21% of each run, Pallas kernels for 0% -> 0%
where the time goes in v2:
time: 144 us; the launch traced here: 143 us
  waiting for transfers between devices  57.3 us (40%)
  starting transfers between devices  48.1 us (33%)
  local copies, waits for them, and re-layouts  18.6 us (13%)
  other arithmetic  7.68 us (5%)
  matrix products  7.63 us (5%)
  between operations  3.98 us (3%)
    ppermute x24, waiting for transfers between devices, exchanged(): return lax.ppermute(array, axes, pairs)  52.6 us
    ppermute x24, starting transfers between devices, exchanged(): return lax.ppermute(array, axes, pairs)  26.5 us
    all_to_all x3, starting transfers between devices, from_every(): return lax.all_to_all(array, axes, 0, 0, tiled=True)  21.6 us
    unnamed x19, local copies, waits for them, and re-layouts  8.26 us
    all_to_all x3, waiting for transfers between devices, from_every(): return lax.all_to_all(array, axes, 0, 0, tiled=True)  4.73 us
    dot_general x1, matrix products, on_device(): lax.dot_general(dlogits, weight, (((1,), (1,)), ((), ())), preferred_elem...  4.47 us
    dot_general x8, matrix products, on_device(): jnp.dot(hidden_of(mg, mh, mc), block, preferred_element_type=jnp.float32)  3.15 us
  transfers between devices with their start and end apart: 27, of which 10 were waited for; matrix products, arithmetic and copies ran while one was open for 21% of the time, Pallas kernels for 0%

profile of v2, /device:TPU:0, one launch (start us, length us, event | category | flops | bytes accessed | tf_op | source)
XLA Modules:
  0.0 143.3 jit_solution(10804805810805128550)
XLA Ops:
  0.6 3.0 %collective-permute-start.10 = (bf16[128,256]{1,0:T(8,128)(2,1)}, bf16[128,256]{1,0:T(8,128)(2,1)}, u32[]{:S(2)}, u32[]{:S(2)}) collective-permute-start(bf16[128,256]{1,0:T(8,128)(2,1)} %param.5), channel_id=1, source_target_pairs={{0,1},{1,0},{16,17},{17,16},{2,3},{3,2},{18,19},{19,18},{4,5},{5,4... | collective-permute-start | bytes 196616 | tf_op jit(solution)/shard_map/ppermute | solution.py:21
  5.2 2.6 %dynamic-slice_bitcast_fusion.1 = (bf16[256,1280]{1,0:T(8,128)(2,1)S(1)}, bf16[256,1280]{1,0:T(8,128)(2,1)S(1)}, bf16[256,1280]{1,0:T(8,128)(2,1)}) fusion(bf16[1,256,4864]{2,1,0:T(8,128)(2,1)} %param.6, s32[]{:T(128)S(6)} %select_n.273, s32[]{:T(128)S(6)} %select_n.272, s32[]{:T(128)S(6)} %select_n.271), kind=kLoop, calls=%fused_computation.18 | loop fusion | bytes 3932172 | tf_op jit(solution)/shard_map/dynamic_slice | solution.py:50
  7.8 2.0 %collective-permute-start.2 = (bf16[256,1280]{1,0:T(8,128)(2,1)}, bf16[256,1280]{1,0:T(8,128)(2,1)S(1)}, u32[]{:S(2)}, u32[]{:S(2)}) collective-permute-start(bf16[256,1280]{1,0:T(8,128)(2,1)} %get-tuple-element.42), channel_id=1, source_target_pairs={{0,16},{1,17},{16,0},{17,1},{2,18},{3,19},{18,2},{19,3},{4,20},{5,... | collective-permute-start | bytes 1966088 | tf_op jit(solution)/shard_map/ppermute | solution.py:21
  10.9 5.8 %all-to-all-start.1 = ((f32[8,2,128]{2,1,0:T(2,128)}), f32[8,2,128]{2,1,0:T(2,128)S(1)}, u32[]{:S(2)}, u32[]{:S(2)}) async-start(f32[8,2,128]{2,1,0:T(2,128)} %broadcast_in_dim.63), calls=%async_computation.1 | async-start | bytes 16384 | tf_op jit(solution)/shard_map/all_to_all | solution.py:25
  17.8 2.0 %constant_dynamic-update-slice_fusion.11 = (bf16[2048,1280]{1,0:T(8,128)(2,1)}, bf16[256,1280]{1,0:T(8,128)(2,1)S(1)}) fusion(bf16[1,256,4864]{2,1,0:T(8,128)(2,1)} %param.6, s32[]{:T(128)S(6)} %select_n.274), kind=kLoop, calls=%fused_computation.70 | loop fusion | bytes 1966084
  20.8 3.2 %collective-permute-done = s32[2,128]{1,0:T(2,128)S(1)} collective-permute-done((s32[2,128]{1,0:T(2,128)S(1)}, s32[2,128]{1,0:T(2,128)S(1)}, u32[]{:S(2)}, u32[]{:S(2)}) %collective-permute-start) | collective-permute-done | bytes 1056 | tf_op jit(solution)/shard_map/ppermute | solution.py:21
  24.1 1.7 %collective-permute-start.16 = (f32[2,128]{1,0:T(2,128)S(1)}, f32[2,128]{1,0:T(2,128)S(1)}, u32[]{:S(2)}, u32[]{:S(2)}) collective-permute-start(f32[2,128]{1,0:T(2,128)S(1)} %pad_maximum_fusion.8), channel_id=1, source_target_pairs={{0,16},{16,0},{1,17},{17,1},{2,18},{18,2},{3,19},{19,3},{4,20},{20... | collective-permute-start | bytes 3080 | tf_op jit(solution)/shard_map/ppermute | solution.py:21
  25.8 1.9 %collective-permute-done.16 = f32[2,128]{1,0:T(2,128)S(1)} collective-permute-done((f32[2,128]{1,0:T(2,128)S(1)}, f32[2,128]{1,0:T(2,128)S(1)}, u32[]{:S(2)}, u32[]{:S(2)}) %collective-permute-start.16) | collective-permute-done | bytes 1056 | tf_op jit(solution)/shard_map/ppermute | solution.py:21
  29.6 3.8 %collective-permute-start.14 = (bf16[256,512]{1,0:T(8,128)(2,1)S(1)}, bf16[256,512]{1,0:T(8,128)(2,1)S(1)}, u32[]{:S(2)}, u32[]{:S(2)}) collective-permute-start(bf16[256,512]{1,0:T(8,128)(2,1)S(1)} %maximum_select_fusion.1), channel_id=1, source_target_pairs={{0,6},{2,4},{4,2},{6,0},{1,7},{3,5},{5,3},{7,1},{8,14},{10,12},{12... | collective-permute-start | bytes 786440 | tf_op jit(solution)/shard_map/ppermute | solution.py:21
  34.1 6.6 %collective-permute-done.14 = bf16[256,512]{1,0:T(8,128)(2,1)S(1)} collective-permute-done((bf16[256,512]{1,0:T(8,128)(2,1)S(1)}, bf16[256,512]{1,0:T(8,128)(2,1)S(1)}, u32[]{:S(2)}, u32[]{:S(2)}) %collective-permute-start.14) | collective-permute-done | bytes 262176 | tf_op jit(solution)/shard_map/ppermute | solution.py:21
  40.8 1.6 %collective-permute-start.4 = (bf16[256,1280]{1,0:T(8,128)(2,1)S(1)}, bf16[256,1280]{1,0:T(8,128)(2,1)S(1)}, u32[]{:S(2)}, u32[]{:S(2)}) collective-permute-start(bf16[256,1280]{1,0:T(8,128)(2,1)S(1)} %get-tuple-element.41), channel_id=1, source_target_pairs={{0,1},{1,0},{16,17},{17,16},{2,3},{3,2},{18,19},{19,18},{4,5},{5,4... | collective-permute-start | bytes 1966088 | tf_op jit(solution)/shard_map/ppermute | solution.py:21
  42.4 14.0 %collective-permute-done.13 = bf16[256,512]{1,0:T(8,128)(2,1)S(1)} collective-permute-done((bf16[256,512]{1,0:T(8,128)(2,1)S(1)}, bf16[256,512]{1,0:T(8,128)(2,1)S(1)}, u32[]{:S(2)}, u32[]{:S(2)}) %collective-permute-start.13) | collective-permute-done | bytes 262176 | tf_op jit(solution)/shard_map/ppermute | solution.py:21
  56.4 2.4 %collective-permute-start.6 = (bf16[256,1280]{1,0:T(8,128)(2,1)S(1)}, bf16[256,1280]{1,0:T(8,128)(2,1)S(1)}, u32[]{:S(2)}, u32[]{:S(2)}) collective-permute-start(bf16[256,1280]{1,0:T(8,128)(2,1)S(1)} %get-tuple-element.40), channel_id=1, source_target_pairs={{0,17},{1,16},{16,1},{17,0},{2,19},{3,18},{18,3},{19,2},{4,21},{5,... | collective-permute-start | bytes 1966088 | tf_op jit(solution)/shard_map/ppermute | solution.py:21
  60.4 13.2 %collective-permute-done.6 = bf16[256,1280]{1,0:T(8,128)(2,1)S(1)} collective-permute-done((bf16[256,1280]{1,0:T(8,128)(2,1)S(1)}, bf16[256,1280]{1,0:T(8,128)(2,1)S(1)}, u32[]{:S(2)}, u32[]{:S(2)}) %collective-permute-start.6) | collective-permute-done | bytes 655392 | tf_op jit(solution)/shard_map/ppermute | solution.py:21
  82.1 12.3 %all-to-all-start = ((f32[16,2,2,128]{3,2,1,0:T(2,128)}), f32[16,2,2,128]{3,2,1,0:T(2,128)S(1)}, u32[]{:S(2)}, u32[]{:S(2)}) async-start(f32[16,2,2,128]{3,2,1,0:T(2,128)} %broadcast_in_dim.62), calls=%async_computation | async-start | bytes 65536 | tf_op jit(solution)/shard_map/all_to_all | solution.py:25
  97.1 4.7 %all-to-all-done = f32[16,2,2,128]{3,2,1,0:T(2,128)S(1)} async-done(((f32[16,2,2,128]{3,2,1,0:T(2,128)}), f32[16,2,2,128]{3,2,1,0:T(2,128)S(1)}, u32[]{:S(2)}, u32[]{:S(2)}) %all-to-all-start) | async-done | bytes 32800 | tf_op jit(solution)/shard_map/all_to_all | solution.py:25
  101.9 1.9 %select_reduce_fusion.1 = (f32[256]{0:T(256)S(1)}, f32[256]{0:T(256)S(1)}) fusion(f32[256,1280]{1,0:T(8,128)S(1)} %get-tuple-element.37, f32[256]{0:T(256)S(1)} %bitcast.120, f32[256]{0:T(256)S(1)} %bitcast.118, f32[256]{0:T(256)S(1)} %log.20, f32[256]{0:T(256)S(1)} %fusion.48, pred[1280]{0:T(1024)(128)(4,1)S(1)} %iota_compare_fusion, ...), kind=kLoop, calls=%fused_computation.1 | loop fusion | flops 5242368 | bytes 1979648 | tf_op jit(solution)/shard_map/reduce_sum | solution.py:154
  106.6 3.5 %all-to-all-start.2 = ((f32[16,3,128]{2,1,0:T(4,128)}), f32[16,3,128]{2,1,0:T(4,128)S(1)}, u32[]{:S(2)}, u32[]{:S(2)}) async-start(f32[16,3,128]{2,1,0:T(4,128)} %bitcast.42), calls=%async_computation.2 | async-start | bytes 65536 | tf_op jit(solution)/shard_map/all_to_all | solution.py:25
  111.9 4.5 %fusion.1 = f32[256,2048]{1,0:T(8,128)S(1)} fusion(bf16[2048,1280]{1,0:T(8,128)(2,1)} %constant_dynamic-update-slice_fusion.4, f32[256,1280]{1,0:T(8,128)S(1)} %get-tuple-element.37, f32[256]{0:T(256)S(1)} %bitcast.121, f32[256]{0:T(256)S(1)} %bitcast.119, f32[256]{0:T(256)S(1)} %log.20, f32[256]{0:T(256)S(1)} %fusion.48, f32[256]{0:T(256)S(1)} %broadcast_divide_fusion, ...), kind=kOutput, calls=%fused_computation.10 | convolution fusion | flops 1346109440 | bytes 9312512 | tf_op jit(solution)/shard_map/dot_general | solution.py:135
  116.6 2.8 %collective-permute-start.17 = (bf16[128,1024]{1,0:T(8,128)(2,1)S(1)}, bf16[128,1024]{1,0:T(8,128)(2,1)S(1)}, u32[]{:S(2)}, u32[]{:S(2)}) collective-permute-start(bf16[128,1024]{1,0:T(8,128)(2,1)S(1)} %get-tuple-element.49), channel_id=1, source_target_pairs={{0,17},{1,16},{16,1},{17,0},{2,19},{3,18},{18,3},{19,2},{4,21},{5,... | collective-permute-start | bytes 786440 | tf_op jit(solution)/shard_map/ppermute | solution.py:21
  121.3 5.5 %collective-permute-done.17 = bf16[128,1024]{1,0:T(8,128)(2,1)S(1)} collective-permute-done((bf16[128,1024]{1,0:T(8,128)(2,1)S(1)}, bf16[128,1024]{1,0:T(8,128)(2,1)S(1)}, u32[]{:S(2)}, u32[]{:S(2)}) %collective-permute-start.17) | collective-permute-done | bytes 262176 | tf_op jit(solution)/shard_map/ppermute | solution.py:21
  126.8 5.2 %collective-permute-done.18 = bf16[128,1024]{1,0:T(8,128)(2,1)S(1)} collective-permute-done((bf16[128,1024]{1,0:T(8,128)(2,1)S(1)}, bf16[128,1024]{1,0:T(8,128)(2,1)S(1)}, u32[]{:S(2)}, u32[]{:S(2)}) %collective-permute-start.18) | collective-permute-done | bytes 262176 | tf_op jit(solution)/shard_map/ppermute | solution.py:21
  132.3 3.4 %collective-permute-start.22 = (bf16[128,256]{1,0:T(8,128)(2,1)S(1)}, bf16[128,256]{1,0:T(8,128)(2,1)S(1)}, u32[]{:S(2)}, u32[]{:S(2)}) collective-permute-start(bf16[128,256]{1,0:T(8,128)(2,1)S(1)} %get-tuple-element.46), channel_id=1, source_target_pairs={{0,6},{2,4},{4,2},{6,0},{1,7},{3,5},{5,3},{7,1},{8,14},{10,12},{12... | collective-permute-start | bytes 196616 | tf_op jit(solution)/shard_map/ppermute | solution.py:21
  139.0 2.5 %collective-permute-done.21 = bf16[128,256]{1,0:T(8,128)(2,1)S(1)} collective-permute-done((bf16[128,256]{1,0:T(8,128)(2,1)S(1)}, bf16[128,256]{1,0:T(8,128)(2,1)S(1)}, u32[]{:S(2)}, u32[]{:S(2)}) %collective-permute-start.21) | collective-permute-done | bytes 65568 | tf_op jit(solution)/shard_map/ppermute | solution.py:21
  (127 shorter events, 29.2 us)
Async XLA Ops:
  0.6 27.1 %collective-permute-start.10 = (bf16[128,256]{1,0:T(8,128)(2,1)}, bf16[128,256]{1,0:T(8,128)(2,1)}, u32[]{:S(2)}, u32[]{:S(2)}) collective-permute-start(bf16[128,256]{1,0:T(8,128)(2,1)} %param.5), channel_id=1, source_target_pairs={{0,1},{1,0},{16,17},{17,16},{2,3},{3,2},{18,19},{19,18},{4,5},{5,4... | collective-permute-start | bytes 196616 | tf_op jit(solution)/shard_map/ppermute | solution.py:21
  3.7 24.9 %collective-permute-start.11 = (bf16[128,256]{1,0:T(8,128)(2,1)}, bf16[128,256]{1,0:T(8,128)(2,1)}, u32[]{:S(2)}, u32[]{:S(2)}) collective-permute-start(bf16[128,256]{1,0:T(8,128)(2,1)} %param.5), channel_id=1, source_target_pairs={{0,17},{1,16},{16,1},{17,0},{2,19},{3,18},{18,3},{19,2},{4,21},{5,... | collective-permute-start | bytes 196616 | tf_op jit(solution)/shard_map/ppermute | solution.py:21
  5.2 24.3 %collective-permute-start.9 = (bf16[128,256]{1,0:T(8,128)(2,1)}, bf16[128,256]{1,0:T(8,128)(2,1)S(1)}, u32[]{:S(2)}, u32[]{:S(2)}) collective-permute-start(bf16[128,256]{1,0:T(8,128)(2,1)} %param.5), channel_id=1, source_target_pairs={{0,16},{1,17},{16,0},{17,1},{2,18},{3,19},{18,2},{19,3},{4,20},{5,... | collective-permute-start | bytes 196616 | tf_op jit(solution)/shard_map/ppermute | solution.py:21
  7.8 65.9 %collective-permute-start.2 = (bf16[256,1280]{1,0:T(8,128)(2,1)}, bf16[256,1280]{1,0:T(8,128)(2,1)S(1)}, u32[]{:S(2)}, u32[]{:S(2)}) collective-permute-start(bf16[256,1280]{1,0:T(8,128)(2,1)} %get-tuple-element.42), channel_id=1, source_target_pairs={{0,16},{1,17},{16,0},{17,1},{2,18},{3,19},{18,2},{19,3},{4,20},{5,... | collective-permute-start | bytes 1966088 | tf_op jit(solution)/shard_map/ppermute | solution.py:21
  10.9 13.1 %all-to-all-start.1 = ((f32[8,2,128]{2,1,0:T(2,128)}), f32[8,2,128]{2,1,0:T(2,128)S(1)}, u32[]{:S(2)}, u32[]{:S(2)}) async-start(f32[8,2,128]{2,1,0:T(2,128)} %broadcast_in_dim.63), calls=%async_computation.1 | async-start | bytes 16384 | tf_op jit(solution)/shard_map/all_to_all | solution.py:25
  16.7 7.2 %collective-permute-start = (s32[2,128]{1,0:T(2,128)S(1)}, s32[2,128]{1,0:T(2,128)S(1)}, u32[]{:S(2)}, u32[]{:S(2)}) collective-permute-start(s32[2,128]{1,0:T(2,128)S(1)} %pad_add_fusion), channel_id=1, source_target_pairs={{0,16},{16,0},{1,17},{17,1},{2,18},{18,2},{3,19},{19,3},{4,20},{20... | collective-permute-start | bytes 3080 | tf_op jit(solution)/shard_map/ppermute | solution.py:21
  27.7 32.1 %collective-permute-start.8 = (bf16[256,1280]{1,0:T(8,128)(2,1)S(1)}, bf16[256,1280]{1,0:T(8,128)(2,1)S(1)}, u32[]{:S(2)}, u32[]{:S(2)}) collective-permute-start(bf16[256,1280]{1,0:T(8,128)(2,1)S(1)} %get-tuple-element.39), channel_id=1, source_target_pairs={{0,8},{8,0},{1,9},{9,1},{2,10},{10,2},{3,11},{11,3},{4,12},{12,4},... | collective-permute-start | bytes 1966088 | tf_op jit(solution)/shard_map/ppermute | solution.py:21
  29.6 11.2 %collective-permute-start.14 = (bf16[256,512]{1,0:T(8,128)(2,1)S(1)}, bf16[256,512]{1,0:T(8,128)(2,1)S(1)}, u32[]{:S(2)}, u32[]{:S(2)}) collective-permute-start(bf16[256,512]{1,0:T(8,128)(2,1)S(1)} %maximum_select_fusion.1), channel_id=1, source_target_pairs={{0,6},{2,4},{4,2},{6,0},{1,7},{3,5},{5,3},{7,1},{8,14},{10,12},{12... | collective-permute-start | bytes 786440 | tf_op jit(solution)/shard_map/ppermute | solution.py:21
  33.4 23.0 %collective-permute-start.13 = (bf16[256,512]{1,0:T(8,128)(2,1)S(1)}, bf16[256,512]{1,0:T(8,128)(2,1)S(1)}, u32[]{:S(2)}, u32[]{:S(2)}) collective-permute-start(bf16[256,512]{1,0:T(8,128)(2,1)S(1)} %maximum_select_fusion.1), channel_id=1, source_target_pairs={{0,4},{2,6},{4,0},{6,2},{1,5},{3,7},{5,1},{7,3},{8,12},{10,14},{12... | collective-permute-start | bytes 786440 | tf_op jit(solution)/shard_map/ppermute | solution.py:21
  33.4 25.4 %collective-permute-start.12 = (bf16[256,512]{1,0:T(8,128)(2,1)S(1)}, bf16[256,512]{1,0:T(8,128)(2,1)S(1)}, u32[]{:S(2)}, u32[]{:S(2)}) collective-permute-start(bf16[256,512]{1,0:T(8,128)(2,1)S(1)} %maximum_select_fusion.1), channel_id=1, source_target_pairs={{0,2},{2,0},{4,6},{6,4},{1,3},{3,1},{5,7},{7,5},{8,10},{10,8},{12,... | collective-permute-start | bytes 786440 | tf_op jit(solution)/shard_map/ppermute | solution.py:21
  40.8 34.3 %collective-permute-start.4 = (bf16[256,1280]{1,0:T(8,128)(2,1)S(1)}, bf16[256,1280]{1,0:T(8,128)(2,1)S(1)}, u32[]{:S(2)}, u32[]{:S(2)}) collective-permute-start(bf16[256,1280]{1,0:T(8,128)(2,1)S(1)} %get-tuple-element.41), channel_id=1, source_target_pairs={{0,1},{1,0},{16,17},{17,16},{2,3},{3,2},{18,19},{19,18},{4,5},{5,4... | collective-permute-start | bytes 1966088 | tf_op jit(solution)/shard_map/ppermute | solution.py:21
  56.4 17.3 %collective-permute-start.6 = (bf16[256,1280]{1,0:T(8,128)(2,1)S(1)}, bf16[256,1280]{1,0:T(8,128)(2,1)S(1)}, u32[]{:S(2)}, u32[]{:S(2)}) collective-permute-start(bf16[256,1280]{1,0:T(8,128)(2,1)S(1)} %get-tuple-element.40), channel_id=1, source_target_pairs={{0,17},{1,16},{16,1},{17,0},{2,19},{3,18},{18,3},{19,2},{4,21},{5,... | collective-permute-start | bytes 1966088 | tf_op jit(solution)/shard_map/ppermute | solution.py:21
  58.8 43.1 %collective-permute-start.15 = (bf16[128,1280]{1,0:T(8,128)(2,1)}, bf16[128,1280]{1,0:T(8,128)(2,1)}, u32[]{:S(2)}, u32[]{:S(2)}) collective-permute-start(bf16[128,1280]{1,0:T(8,128)(2,1)} %get-tuple-element.44), channel_id=1, source_target_pairs={{0,16},{16,0},{1,17},{17,1},{2,18},{18,2},{3,19},{19,3},{4,20},{20... | collective-permute-start | bytes 983048 | tf_op jit(solution)/shard_map/ppermute | solution.py:21
  73.6 6.8 %collective-permute-start.3 = (bf16[256,1280]{1,0:T(8,128)(2,1)S(1)}, bf16[256,1280]{1,0:T(8,128)(2,1)S(1)}, u32[]{:S(2)}, u32[]{:S(2)}) collective-permute-start(bf16[256,1280]{1,0:T(8,128)(2,1)S(1)} %collective-permute-done.2), channel_id=1, source_target_pairs={{0,8},{8,0},{1,9},{9,1},{2,10},{10,2},{3,11},{11,3},{4,12},{12,4},... | collective-permute-start | bytes 1966088 | tf_op jit(solution)/shard_map/ppermute | solution.py:21
  82.1 19.7 %all-to-all-start = ((f32[16,2,2,128]{3,2,1,0:T(2,128)}), f32[16,2,2,128]{3,2,1,0:T(2,128)S(1)}, u32[]{:S(2)}, u32[]{:S(2)}) async-start(f32[16,2,2,128]{3,2,1,0:T(2,128)} %broadcast_in_dim.62), calls=%async_computation | async-start | bytes 65536 | tf_op jit(solution)/shard_map/all_to_all | solution.py:25
  105.0 5.0 %collective-permute-start.1 = (f32[8,128]{1,0:T(8,128)S(1)}, f32[8,128]{1,0:T(8,128)S(1)}, u32[]{:S(2)}, u32[]{:S(2)}) collective-permute-start(f32[8,128]{1,0:T(8,128)S(1)} %broadcast_in_dim.59), channel_id=1, source_target_pairs={{0,8},{8,0},{1,9},{9,1},{2,10},{10,2},{3,11},{11,3},{4,12},{12,4},... | collective-permute-start | bytes 12296 | tf_op jit(solution)/shard_map/ppermute | solution.py:21
  106.6 13.7 %all-to-all-start.2 = ((f32[16,3,128]{2,1,0:T(4,128)}), f32[16,3,128]{2,1,0:T(4,128)S(1)}, u32[]{:S(2)}, u32[]{:S(2)}) async-start(f32[16,3,128]{2,1,0:T(4,128)} %bitcast.42), calls=%async_computation.2 | async-start | bytes 65536 | tf_op jit(solution)/shard_map/all_to_all | solution.py:25
  116.6 10.2 %collective-permute-start.17 = (bf16[128,1024]{1,0:T(8,128)(2,1)S(1)}, bf16[128,1024]{1,0:T(8,128)(2,1)S(1)}, u32[]{:S(2)}, u32[]{:S(2)}) collective-permute-start(bf16[128,1024]{1,0:T(8,128)(2,1)S(1)} %get-tuple-element.49), channel_id=1, source_target_pairs={{0,17},{1,16},{16,1},{17,0},{2,19},{3,18},{18,3},{19,2},{4,21},{5,... | collective-permute-start | bytes 786440 | tf_op jit(solution)/shard_map/ppermute | solution.py:21
  119.5 12.6 %collective-permute-start.18 = (bf16[128,1024]{1,0:T(8,128)(2,1)S(1)}, bf16[128,1024]{1,0:T(8,128)(2,1)S(1)}, u32[]{:S(2)}, u32[]{:S(2)}) collective-permute-start(bf16[128,1024]{1,0:T(8,128)(2,1)S(1)} %dynamic-slice_convert_fusion.1), channel_id=1, source_target_pairs={{0,1},{1,0},{16,17},{17,16},{2,3},{3,2},{18,19},{19,18},{4,5},{5,4... | collective-permute-start | bytes 786440 | tf_op jit(solution)/shard_map/ppermute | solution.py:21
  120.1 12.0 %collective-permute-start.19 = (bf16[128,1024]{1,0:T(8,128)(2,1)S(1)}, bf16[128,1024]{1,0:T(8,128)(2,1)S(1)}, u32[]{:S(2)}, u32[]{:S(2)}) collective-permute-start(bf16[128,1024]{1,0:T(8,128)(2,1)S(1)} %get-tuple-element.48), channel_id=1, source_target_pairs={{0,16},{1,17},{16,0},{17,1},{2,18},{3,19},{18,2},{19,3},{4,20},{5,... | collective-permute-start | bytes 786440 | tf_op jit(solution)/shard_map/ppermute | solution.py:21
  121.3 15.4 %collective-permute-start.23 = (f32[8,128]{1,0:T(8,128)S(1)}, f32[8,128]{1,0:T(8,128)S(1)}, u32[]{:S(2)}, u32[]{:S(2)}) collective-permute-start(f32[8,128]{1,0:T(8,128)S(1)} %broadcast_in_dim.65), channel_id=1, source_target_pairs={{0,8},{8,0},{1,9},{9,1},{2,10},{10,2},{3,11},{11,3},{4,12},{12,4},... | collective-permute-start | bytes 12296 | tf_op jit(solution)/shard_map/ppermute | solution.py:21
  132.3 6.7 %collective-permute-start.22 = (bf16[128,256]{1,0:T(8,128)(2,1)S(1)}, bf16[128,256]{1,0:T(8,128)(2,1)S(1)}, u32[]{:S(2)}, u32[]{:S(2)}) collective-permute-start(bf16[128,256]{1,0:T(8,128)(2,1)S(1)} %get-tuple-element.46), channel_id=1, source_target_pairs={{0,6},{2,4},{4,2},{6,0},{1,7},{3,5},{5,3},{7,1},{8,14},{10,12},{12... | collective-permute-start | bytes 196616 | tf_op jit(solution)/shard_map/ppermute | solution.py:21
  135.7 5.8 %collective-permute-start.21 = (bf16[128,256]{1,0:T(8,128)(2,1)S(1)}, bf16[128,256]{1,0:T(8,128)(2,1)S(1)}, u32[]{:S(2)}, u32[]{:S(2)}) collective-permute-start(bf16[128,256]{1,0:T(8,128)(2,1)S(1)} %get-tuple-element.47), channel_id=1, source_target_pairs={{0,4},{2,6},{4,0},{6,2},{1,5},{3,7},{5,1},{7,3},{8,12},{10,14},{12... | collective-permute-start | bytes 196616 | tf_op jit(solution)/shard_map/ppermute | solution.py:21
  135.7 5.8 %collective-permute-start.20 = (bf16[128,256]{1,0:T(8,128)(2,1)S(1)}, bf16[128,256]{1,0:T(8,128)(2,1)S(1)}, u32[]{:S(2)}, u32[]{:S(2)}) collective-permute-start(bf16[128,256]{1,0:T(8,128)(2,1)S(1)} %get-tuple-element.45), channel_id=1, source_target_pairs={{0,2},{2,0},{4,6},{6,4},{1,3},{3,1},{5,7},{7,5},{8,10},{10,8},{12,... | collective-permute-start | bytes 196616 | tf_op jit(solution)/shard_map/ppermute | solution.py:21
  (8 other events, 56.3 us)

commit v3 on v2

v3 whole, which is shorter than its diff:
```python
import math

import jax
import jax.numpy as jnp
from jax import lax
from jax.sharding import Mesh, PartitionSpec as P

LANES = 128


def exchanged(array, **flips):
    axes = tuple(flips)
    sizes = [lax.axis_size(axis) for axis in axes]
    pairs = []
    for source in range(math.prod(sizes)):
        rest, target, stride = source, 0, 1
        for axis, size in reversed(list(zip(axes, sizes))):
            target += (rest % size ^ flips[axis]) * stride
            rest, stride = rest // size, stride * size
        pairs.append((source, target))
    return lax.ppermute(array, axes, pairs)


def from_every(array, axes):
    return lax.all_to_all(array, axes, 0, 0, tiled=True)


def on_device(student_hidden, student_blocks, teacher_logits, token_ids, loss_mask):
    row_g, core, slab, half = (lax.axis_index(axis) for axis in ("g", "c", "s", "h"))
    n_g, n_s = lax.axis_size("g"), lax.axis_size("s")
    tokens, feature = student_hidden.shape
    piece = student_blocks[0]
    rows = piece.shape[0]
    vt = piece.shape[1] // 2
    tiles = vt // LANES
    wide_tiles = -(-tiles // n_g)
    width = wide_tiles * LANES

    def offset(g):
        return (g * (tiles - wide_tiles)) // max(n_g - 1, 1) * LANES

    plane = [(mg, mh) for mh in range(2) for mg in range(n_g)]
    others = sorted(plane[1:], key=lambda m: (m[0].bit_count() + m[1], m))

    hidden_plane = {(0, 0): student_hidden}
    for mg, mh in others:
        hidden_plane[mg, mh] = exchanged(student_hidden, g=mg, h=mh)

    def columns_of(g, h):
        return lax.dynamic_slice_in_dim(piece, h * vt + offset(g), width, 1)

    blocks = {(0, 0, 0): columns_of(row_g, half)}
    for mg, mh in others:
        cut = columns_of(row_g ^ mg, half ^ mh)
        blocks[mg, mh, 0] = exchanged(cut, g=mg, h=mh)
    for mg, mh in [(0, 0)] + others:
        blocks[mg, mh, 1] = exchanged(blocks[mg, mh, 0], c=1)

    local = teacher_logits.astype(jnp.float32)
    local_max = jnp.max(local, axis=1)
    local_sum = jnp.sum(jnp.exp(local - local_max[:, None]), axis=1)
    own_mask = loss_mask.astype(jnp.float32)
    own_count = jnp.full((8, LANES), jnp.sum(own_mask))
    chip_count = own_count + exchanged(own_count, c=1)
    own_parts = jnp.stack(
        [local_max, local_sum, own_mask + 2.0 * chip_count[0, 0], token_ids.astype(jnp.float32)]
    )

    def teacher_of(g):
        return lax.dynamic_slice_in_dim(teacher_logits, offset(g), width, 1)

    teacher = [teacher_of(row_g)] + [
        exchanged(teacher_of(row_g ^ mg), g=mg) for mg in range(1, n_g)
    ]

    sides = [jnp.concatenate([hidden_plane[mg, mh] for mg in range(n_g)]) for mh in range(2)]
    plane_hidden = jnp.where(
        half == 0, jnp.concatenate(sides, axis=1), jnp.concatenate(sides[::-1], axis=1)
    )
    gathered = [plane_hidden]
    gathered += [exchanged(plane_hidden, s=ms) for ms in range(1, n_s)]

    def hidden_of(mg, mh, mc):
        index = (half ^ mh) * n_g + (row_g ^ mg)
        pair = lax.select_n(slab ^ index, *gathered)
        return jnp.where((core ^ mc) == 0, pair[:, :feature], pair[:, feature:])

    logits = None
    for mg, mh in [(0, 0)] + others:
        for mc in range(2):
            block = blocks[mg, mh, mc]
            if logits is not None:
                block, logits = lax.optimization_barrier((block, logits))
            term = jnp.dot(hidden_of(mg, mh, mc), block, preferred_element_type=jnp.float32)
            logits = term if logits is None else logits + term

    local_column = lax.broadcasted_iota(jnp.int32, (1, width), 1)
    shared = jnp.where(row_g > 0, offset(row_g - 1) + width - offset(row_g), 0)
    mine = local_column >= shared

    def by_group(stack):
        parts = stack.reshape(stack.shape[0], n_g, tokens)
        return jnp.stack(
            [lax.dynamic_index_in_dim(parts, row_g ^ g, 1, False) for g in range(n_g)]
        )

    local_max = jnp.max(jnp.where(mine, logits, jnp.float32(-3e38)), axis=1)
    local_sum = jnp.sum(jnp.where(mine, jnp.exp(logits - local_max[:, None]), 0.0), axis=1)
    sent = by_group(jnp.stack([local_max, local_sum])).reshape(2 * n_g, tokens)
    sent = jnp.concatenate([sent, own_parts])
    every = from_every(jnp.broadcast_to(sent, (2 * n_s * n_g,) + sent.shape), ("g", "s", "h"))
    teacher, _ = lax.optimization_barrier((teacher, every))
    teacher = jnp.concatenate(teacher).astype(jnp.float32)
    student_parts = every[:, : 2 * n_g].reshape(2 * n_s * n_g, n_g, 2, tokens)
    student_parts = jnp.concatenate(
        [lax.dynamic_index_in_dim(student_parts, row_g ^ mg, 1, False) for mg in range(n_g)], 2
    )
    teacher_parts = every[:, 2 * n_g :].reshape(n_g, 2 * n_s, 4, tokens)
    teacher_parts = jnp.concatenate(
        [lax.dynamic_index_in_dim(teacher_parts, row_g ^ mg, 0, False) for mg in range(n_g)], 2
    )

    def normalizer(maxes, sums):
        top = jnp.max(maxes, axis=0)
        return top, jnp.log(jnp.sum(sums * jnp.exp(maxes - top), axis=0))

    top, log_total = normalizer(student_parts[:, 0], student_parts[:, 1])
    t_top, t_log = normalizer(teacher_parts[:, 0], teacher_parts[:, 1])
    coded, ids = teacher_parts[0, 2], teacher_parts[0, 3].astype(jnp.int32)
    chip_counts = jnp.floor(coded * 0.5)
    mask_float = coded - 2.0 * chip_counts
    mask_total = jnp.sum(chip_counts.reshape(n_g, tokens)[:, 0])
    factor = (mask_float / mask_total)[:, None]

    def log_probs(logits, teacher):
        student_logp = logits - top[:, None] - log_total[:, None]
        return student_logp, teacher - t_top[:, None] - t_log[:, None]

    student_logp, teacher_logp = log_probs(logits, teacher)
    delta = factor * (jnp.exp(student_logp) - jnp.exp(teacher_logp))
    dlogits = jnp.where(mine, delta, 0.0).astype(jnp.bfloat16)

    def features_of(mc, mg, mh):
        block = blocks[mg, mh, mc]
        return lax.dot_general(
            dlogits, block, (((1,), (1,)), ((), ())), preferred_element_type=jnp.float32
        )

    grads = [[features_of(mc, mg, mh) for mg, mh in plane] for mc in range(2)]
    crossed = (core ^ half) == 1

    def for_half(mg, mh):
        picks = [jnp.where(crossed, b, a) for a, b in zip(grads[mh], grads[1 - mh])]
        return jnp.concatenate([p[mg * tokens : (mg + 1) * tokens] for p in picks], axis=1)

    partial = for_half(0, 0)
    terms = [for_half(mg, mh).astype(jnp.bfloat16) for mg, mh in others]
    arrived = [(exchanged(term, g=mg, h=mh), mg, mh) for term, (mg, mh) in zip(terms, others)]
    for part, kg, kh in arrived:
        order = [(mh ^ kh) * n_g + (mg ^ kg) for mg, mh in plane]
        part = jnp.concatenate([part[:, j * rows : (j + 1) * rows] for j in order], axis=1)
        partial = partial + part.astype(jnp.float32)

    _, logits, teacher = lax.optimization_barrier((terms, logits, teacher))
    student_logp, teacher_logp = log_probs(logits, teacher)
    gap = jnp.exp(teacher_logp) * (teacher_logp - student_logp)
    kl_part = jnp.sum(jnp.where(mine, gap, 0.0), axis=1)
    column = local_column + (slab * 2 + half) * vt + offset(row_g)
    hit = (column == ids[:, None]) & mine
    picked = jnp.sum(jnp.where(hit, logits, 0.0), axis=1)
    loss_part = jnp.broadcast_to(jnp.sum(mask_float * kl_part), kl_part.shape)
    sent = by_group(jnp.stack([kl_part, picked, loss_part]))
    sent = jnp.broadcast_to(sent[:, None], (n_g, 2 * n_s) + sent.shape[1:])
    every = from_every(sent.reshape(-1, 3, tokens), ("g", "s", "h"))

    def for_slab(s):
        index = (half ^ (s // n_g)) * n_g + (row_g ^ (s % n_g))
        return lax.dynamic_slice_in_dim(partial, index * rows, rows, 1)

    result = for_slab(slab)
    slab_terms = [for_slab(slab ^ ms).astype(jnp.bfloat16) for ms in range(1, n_s)]
    arrived = [exchanged(term, s=ms) for ms, term in enumerate(slab_terms, 1)]
    every, _ = lax.optimization_barrier((every, slab_terms))
    token_kl, picked, core_loss = jnp.sum(every, axis=0)
    sampled = picked - top[:tokens] - log_total[:tokens]
    core_loss = jnp.broadcast_to(core_loss, (8, LANES))
    loss = (core_loss + exchanged(core_loss, c=1))[0, 0] / mask_total

    for part in arrived:
        result = result + part.astype(jnp.float32)
    return (result.astype(jnp.bfloat16), token_kl, sampled, loss)


def solution(mesh):
    n_dp, n_vocab = mesh.devices.shape
    n_g, n_s = n_dp // 2, n_vocab // 2
    split = Mesh(mesh.devices.reshape(n_g, 2, n_s, 2), ("g", "c", "s", "h"))
    dp, vocab = ("g", "c"), ("s", "h")
    return jax.shard_map(
        on_device,
        mesh=split,
        in_specs=(P(dp, vocab), P(vocab, dp, None), P(dp, vocab), P(dp), P(dp)),
        out_specs=(P(dp, vocab), P(dp), P(dp), P()),
        check_vma=False,
    )
```

time: 144 us -> 123 us (0.85)
  starting transfers between devices: 48.1 us -> 36.3 us
  waiting for transfers between devices: 57.3 us -> 53 us
  local copies, waits for them, and re-layouts: 18.6 us -> 14.9 us
  matrix products: 7.63 us -> 5.67 us
    all_to_all x3 -> x2, starting transfers between devices: 21.6 us -> 12.6 us  [from_every(): return lax.all_to_all(array, axes, 0, 0, tiled=True)]
    ppermute x24 -> x22, waiting for transfers between devices: 52.6 us -> 47 us  [exchanged(): return lax.ppermute(array, axes, pairs)]
    unnamed x19 -> x42, local copies, waits for them, and re-layouts: 8.26 us -> 5.12 us
    ppermute x24 -> x22, starting transfers between devices: 26.5 us -> 23.7 us  [exchanged(): return lax.ppermute(array, axes, pairs)]
    dot_general x1 -> x8, matrix products: 4.47 us -> 2.94 us  [features_of(): lax.dot_general(dlogits, block, (((1,), (1,)), ((), ())), preferred_eleme...]
    all_to_all x3 -> x2, waiting for transfers between devices: 4.73 us -> 5.98 us  [from_every(): return lax.all_to_all(array, axes, 0, 0, tiled=True)]
  transfers between devices with their start and end apart: 27 -> 24, of which waited for: 10 -> 7; matrix products, arithmetic and copies ran while one was open for 21% -> 14% of each run, Pallas kernels for 0% -> 0%
where the time goes in v3:
time: 123 us; the launch traced here: 122 us
  waiting for transfers between devices  53 us (43%)
  starting transfers between devices  36.3 us (30%)
  local copies, waits for them, and re-layouts  14.9 us (12%)
  other arithmetic  8.07 us (7%)
  matrix products  5.67 us (5%)
  between operations  4.54 us (4%)
    ppermute x22, waiting for transfers between devices, exchanged(): return lax.ppermute(array, axes, pairs)  47 us
    ppermute x22, starting transfers between devices, exchanged(): return lax.ppermute(array, axes, pairs)  23.7 us
    all_to_all x2, starting transfers between devices, from_every(): return lax.all_to_all(array, axes, 0, 0, tiled=True)  12.6 us
    all_to_all x2, waiting for transfers between devices, from_every(): return lax.all_to_all(array, axes, 0, 0, tiled=True)  5.98 us
    unnamed x42, local copies, waits for them, and re-layouts  5.12 us
    dynamic_slice x1, local copies, waits for them, and re-layouts, columns_of(): return lax.dynamic_slice_in_dim(piece, h * vt + offset(g), width, 1)  2.99 us
    dot_general x8, matrix products, features_of(): lax.dot_general(dlogits, block, (((1,), (1,)), ((), ())), preferred_eleme...  2.94 us
    dot_general x8, matrix products, on_device(): jnp.dot(hidden_of(mg, mh, mc), block, preferred_element_type=jnp.float32)  2.73 us
  transfers between devices with their start and end apart: 24, of which 7 were waited for; matrix products, arithmetic and copies ran while one was open for 14% of the time, Pallas kernels for 0%

profile of v3, /device:TPU:0, one launch (start us, length us, event | category | flops | bytes accessed | tf_op | source)
XLA Modules:
  0.0 122.5 jit_solution(2378311803221338579)
XLA Ops:
  0.6 3.0 %collective-permute-start.8 = (bf16[128,256]{1,0:T(8,128)(2,1)}, bf16[128,256]{1,0:T(8,128)(2,1)}, u32[]{:S(2)}, u32[]{:S(2)}) collective-permute-start(bf16[128,256]{1,0:T(8,128)(2,1)} %param.5), channel_id=1, source_target_pairs={{0,1},{1,0},{16,17},{17,16},{2,3},{3,2},{18,19},{19,18},{4,5},{5,4... | collective-permute-start | bytes 196616 | tf_op jit(solution)/shard_map/ppermute | solution.py:21
  3.7 1.5 %collective-permute-start.9 = (bf16[128,256]{1,0:T(8,128)(2,1)}, bf16[128,256]{1,0:T(8,128)(2,1)}, u32[]{:S(2)}, u32[]{:S(2)}) collective-permute-start(bf16[128,256]{1,0:T(8,128)(2,1)} %param.5), channel_id=1, source_target_pairs={{0,17},{1,16},{16,1},{17,0},{2,19},{3,18},{18,3},{19,2},{4,21},{5,... | collective-permute-start | bytes 196616 | tf_op jit(solution)/shard_map/ppermute | solution.py:21
  5.2 3.0 %dynamic-slice_bitcast_fusion = (bf16[256,1280]{1,0:T(8,128)(2,1)S(1)}, bf16[256,1280]{1,0:T(8,128)(2,1)}, bf16[256,1280]{1,0:T(8,128)(2,1)S(1)}, bf16[256,1280]{1,0:T(8,128)(2,1)}) fusion(bf16[1,256,4864]{2,1,0:T(8,128)(2,1)} %param.6, s32[]{:T(128)S(6)} %select_n.356, s32[]{:T(128)S(6)} %select_n.354, s32[]{:T(128)S(6)} %select_n.353, s32[]{:T(128)S(6)} %select_n.355), kind=kLoop, calls=%fused_computation.7 | loop fusion | bytes 5242896 | tf_op jit(solution)/shard_map/dynamic_slice | solution.py:50
  8.2 1.9 %collective-permute-start.4 = (bf16[256,1280]{1,0:T(8,128)(2,1)}, bf16[256,1280]{1,0:T(8,128)(2,1)S(1)}, u32[]{:S(2)}, u32[]{:S(2)}) collective-permute-start(bf16[256,1280]{1,0:T(8,128)(2,1)} %get-tuple-element.67), channel_id=1, source_target_pairs={{0,1},{1,0},{16,17},{17,16},{2,3},{3,2},{18,19},{19,18},{4,5},{5,4... | collective-permute-start | bytes 1966088 | tf_op jit(solution)/shard_map/ppermute | solution.py:21
  12.7 0.8 constant_dynamic-update-slice_fusion.3
  13.5 0.8 constant_dynamic-update-slice_fusion.2
  14.5 2.7 %collective-permute-start.11 = (bf16[256,512]{1,0:T(8,128)(2,1)S(1)}, bf16[256,512]{1,0:T(8,128)(2,1)S(1)}, u32[]{:S(2)}, u32[]{:S(2)}) collective-permute-start(bf16[256,512]{1,0:T(8,128)(2,1)S(1)} %maximum_select_fusion), channel_id=1, source_target_pairs={{0,4},{2,6},{4,0},{6,2},{1,5},{3,7},{5,1},{7,3},{8,12},{10,14},{12... | collective-permute-start | bytes 786440 | tf_op jit(solution)/shard_map/ppermute | solution.py:21
  17.1 1.3 %collective-permute-start.12 = (bf16[256,512]{1,0:T(8,128)(2,1)S(1)}, bf16[256,512]{1,0:T(8,128)(2,1)S(1)}, u32[]{:S(2)}, u32[]{:S(2)}) collective-permute-start(bf16[256,512]{1,0:T(8,128)(2,1)S(1)} %maximum_select_fusion), channel_id=1, source_target_pairs={{0,6},{2,4},{4,2},{6,0},{1,7},{3,5},{5,3},{7,1},{8,14},{10,12},{12... | collective-permute-start | bytes 786440 | tf_op jit(solution)/shard_map/ppermute | solution.py:21
  20.6 15.4 %collective-permute-done.11 = bf16[256,512]{1,0:T(8,128)(2,1)S(1)} collective-permute-done((bf16[256,512]{1,0:T(8,128)(2,1)S(1)}, bf16[256,512]{1,0:T(8,128)(2,1)S(1)}, u32[]{:S(2)}, u32[]{:S(2)}) %collective-permute-start.11) | collective-permute-done | bytes 262176 | tf_op jit(solution)/shard_map/ppermute | solution.py:21
  35.9 1.5 %collective-permute-start = (bf16[256,1280]{1,0:T(8,128)(2,1)S(1)}, bf16[256,1280]{1,0:T(8,128)(2,1)S(1)}, u32[]{:S(2)}, u32[]{:S(2)}) collective-permute-start(bf16[256,1280]{1,0:T(8,128)(2,1)S(1)} %get-tuple-element.66), channel_id=1, source_target_pairs={{0,17},{1,16},{16,1},{17,0},{2,19},{3,18},{18,3},{19,2},{4,21},{5,... | collective-permute-start | bytes 1966088 | tf_op jit(solution)/shard_map/ppermute | solution.py:21
  39.0 26.7 %collective-permute-done.2 = bf16[256,1280]{1,0:T(8,128)(2,1)S(1)} collective-permute-done((bf16[256,1280]{1,0:T(8,128)(2,1)}, bf16[256,1280]{1,0:T(8,128)(2,1)S(1)}, u32[]{:S(2)}, u32[]{:S(2)}) %collective-permute-start.2) | collective-permute-done | bytes 655392 | tf_op jit(solution)/shard_map/ppermute | solution.py:21
  71.4 6.7 %all-to-all-start = ((f32[16,8,128]{2,1,0:T(8,128)}), f32[16,8,128]{2,1,0:T(8,128)S(1)}, u32[]{:S(2)}, u32[]{:S(2)}) async-start(f32[16,8,128]{2,1,0:T(8,128)} %broadcast_in_dim.65), calls=%async_computation | async-start | bytes 131072 | tf_op jit(solution)/shard_map/all_to_all | solution.py:25
  78.1 0.8 constant_dynamic-slice_fusion.4
  78.9 1.9 %collective-permute-start.14 = (bf16[128,1280]{1,0:T(8,128)(2,1)}, bf16[128,1280]{1,0:T(8,128)(2,1)S(1)}, u32[]{:S(2)}, u32[]{:S(2)}) collective-permute-start(bf16[128,1280]{1,0:T(8,128)(2,1)} %get-tuple-element.72), channel_id=1, source_target_pairs={{0,16},{16,0},{1,17},{17,1},{2,18},{18,2},{3,19},{19,3},{4,20},{20... | collective-permute-start | bytes 983048 | tf_op jit(solution)/shard_map/ppermute | solution.py:21
  80.8 4.9 %all-to-all-done = f32[16,8,128]{2,1,0:T(8,128)S(1)} async-done(((f32[16,8,128]{2,1,0:T(8,128)}), f32[16,8,128]{2,1,0:T(8,128)S(1)}, u32[]{:S(2)}, u32[]{:S(2)}) %all-to-all-start) | async-done | bytes 65568 | tf_op jit(solution)/shard_map/all_to_all | solution.py:25
  86.5 2.7 %collective-permute-done.14 = bf16[128,1280]{1,0:T(8,128)(2,1)S(1)} collective-permute-done((bf16[128,1280]{1,0:T(8,128)(2,1)}, bf16[128,1280]{1,0:T(8,128)(2,1)S(1)}, u32[]{:S(2)}, u32[]{:S(2)}) %collective-permute-start.14) | collective-permute-done | bytes 327712 | tf_op jit(solution)/shard_map/ppermute | solution.py:21
  96.9 1.6 %collective-permute-start.15 = (bf16[128,1024]{0,1:T(8,128)(2,1)S(1)}, bf16[128,1024]{0,1:T(8,128)(2,1)S(1)}, u32[]{:S(2)}, u32[]{:S(2)}) collective-permute-start(bf16[128,1024]{0,1:T(8,128)(2,1)S(1)} %pad_maximum_fusion), channel_id=1, source_target_pairs={{0,1},{1,0},{16,17},{17,16},{2,3},{3,2},{18,19},{19,18},{4,5},{5,4... | collective-permute-start | bytes 786440 | tf_op jit(solution)/shard_map/ppermute | solution.py:21
  98.5 1.4 %collective-permute-start.16 = (bf16[128,1024]{0,1:T(8,128)(2,1)S(1)}, bf16[128,1024]{0,1:T(8,128)(2,1)S(1)}, u32[]{:S(2)}, u32[]{:S(2)}) collective-permute-start(bf16[128,1024]{0,1:T(8,128)(2,1)S(1)} %pad_maximum_fusion.1), channel_id=1, source_target_pairs={{0,16},{1,17},{16,0},{17,1},{2,18},{3,19},{18,2},{19,3},{4,20},{5,... | collective-permute-start | bytes 786440 | tf_op jit(solution)/shard_map/ppermute | solution.py:21
  100.7 0.9 select_reduce_fusion.1
  103.6 6.0 %all-to-all-start.1 = ((f32[16,3,128]{2,1,0:T(4,128)}), f32[16,3,128]{2,1,0:T(4,128)S(1)}, u32[]{:S(2)}, u32[]{:S(2)}) async-start(f32[16,3,128]{2,1,0:T(4,128)} %bitcast.31), calls=%async_computation.1 | async-start | bytes 65536 | tf_op jit(solution)/shard_map/all_to_all | solution.py:25
  109.6 1.6 %collective-permute-done.16 = bf16[128,1024]{0,1:T(8,128)(2,1)S(1)} collective-permute-done((bf16[128,1024]{0,1:T(8,128)(2,1)S(1)}, bf16[128,1024]{0,1:T(8,128)(2,1)S(1)}, u32[]{:S(2)}, u32[]{:S(2)}) %collective-permute-start.16) | collective-permute-done | bytes 262176 | tf_op jit(solution)/shard_map/ppermute | solution.py:21
  111.5 3.4 %collective-permute-start.20 = (bf16[128,256]{0,1:T(8,128)(2,1)S(1)}, bf16[128,256]{0,1:T(8,128)(2,1)S(1)}, u32[]{:S(2)}, u32[]{:S(2)}) collective-permute-start(bf16[128,256]{0,1:T(8,128)(2,1)S(1)} %get-tuple-element.75), channel_id=1, source_target_pairs={{0,6},{2,4},{4,2},{6,0},{1,7},{3,5},{5,3},{7,1},{8,14},{10,12},{12... | collective-permute-start | bytes 196616 | tf_op jit(solution)/shard_map/ppermute | solution.py:21
  114.8 1.1 collective-permute-start.18
  115.9 1.1 all-to-all-done.1
  (163 shorter events, 25.4 us)
Async XLA Ops:
  0.6 10.8 %collective-permute-start.8 = (bf16[128,256]{1,0:T(8,128)(2,1)}, bf16[128,256]{1,0:T(8,128)(2,1)}, u32[]{:S(2)}, u32[]{:S(2)}) collective-permute-start(bf16[128,256]{1,0:T(8,128)(2,1)} %param.5), channel_id=1, source_target_pairs={{0,1},{1,0},{16,17},{17,16},{2,3},{3,2},{18,19},{19,18},{4,5},{5,4... | collective-permute-start | bytes 196616 | tf_op jit(solution)/shard_map/ppermute | solution.py:21
  3.7 9.8 %collective-permute-start.9 = (bf16[128,256]{1,0:T(8,128)(2,1)}, bf16[128,256]{1,0:T(8,128)(2,1)}, u32[]{:S(2)}, u32[]{:S(2)}) collective-permute-start(bf16[128,256]{1,0:T(8,128)(2,1)} %param.5), channel_id=1, source_target_pairs={{0,17},{1,16},{16,1},{17,0},{2,19},{3,18},{18,3},{19,2},{4,21},{5,... | collective-permute-start | bytes 196616 | tf_op jit(solution)/shard_map/ppermute | solution.py:21
  5.2 9.2 %collective-permute-start.7 = (bf16[128,256]{1,0:T(8,128)(2,1)}, bf16[128,256]{1,0:T(8,128)(2,1)S(1)}, u32[]{:S(2)}, u32[]{:S(2)}) collective-permute-start(bf16[128,256]{1,0:T(8,128)(2,1)} %param.5), channel_id=1, source_target_pairs={{0,16},{1,17},{16,0},{17,1},{2,18},{3,19},{18,2},{19,3},{4,20},{5,... | collective-permute-start | bytes 196616 | tf_op jit(solution)/shard_map/ppermute | solution.py:21
  8.2 29.5 %collective-permute-start.4 = (bf16[256,1280]{1,0:T(8,128)(2,1)}, bf16[256,1280]{1,0:T(8,128)(2,1)S(1)}, u32[]{:S(2)}, u32[]{:S(2)}) collective-permute-start(bf16[256,1280]{1,0:T(8,128)(2,1)} %get-tuple-element.67), channel_id=1, source_target_pairs={{0,1},{1,0},{16,17},{17,16},{2,3},{3,2},{18,19},{19,18},{4,5},{5,4... | collective-permute-start | bytes 1966088 | tf_op jit(solution)/shard_map/ppermute | solution.py:21
  10.2 28.0 %collective-permute-start.6 = (bf16[256,1280]{1,0:T(8,128)(2,1)S(1)}, bf16[256,1280]{1,0:T(8,128)(2,1)S(1)}, u32[]{:S(2)}, u32[]{:S(2)}) collective-permute-start(bf16[256,1280]{1,0:T(8,128)(2,1)S(1)} %get-tuple-element.64), channel_id=1, source_target_pairs={{0,8},{8,0},{1,9},{9,1},{2,10},{10,2},{3,11},{11,3},{4,12},{12,4},... | collective-permute-start | bytes 1966088 | tf_op jit(solution)/shard_map/ppermute | solution.py:21
  12.1 6.4 %collective-permute-start.13 = (f32[8,128]{1,0:T(8,128)S(1)}, f32[8,128]{1,0:T(8,128)S(1)}, u32[]{:S(2)}, u32[]{:S(2)}) collective-permute-start(f32[8,128]{1,0:T(8,128)S(1)} %broadcast_in_dim.64), channel_id=1, source_target_pairs={{0,8},{8,0},{1,9},{9,1},{2,10},{10,2},{3,11},{11,3},{4,12},{12,4},... | collective-permute-start | bytes 12296 | tf_op jit(solution)/shard_map/ppermute | solution.py:21
  14.5 21.4 %collective-permute-start.11 = (bf16[256,512]{1,0:T(8,128)(2,1)S(1)}, bf16[256,512]{1,0:T(8,128)(2,1)S(1)}, u32[]{:S(2)}, u32[]{:S(2)}) collective-permute-start(bf16[256,512]{1,0:T(8,128)(2,1)S(1)} %maximum_select_fusion), channel_id=1, source_target_pairs={{0,4},{2,6},{4,0},{6,2},{1,5},{3,7},{5,1},{7,3},{8,12},{10,14},{12... | collective-permute-start | bytes 786440 | tf_op jit(solution)/shard_map/ppermute | solution.py:21
  17.1 20.3 %collective-permute-start.12 = (bf16[256,512]{1,0:T(8,128)(2,1)S(1)}, bf16[256,512]{1,0:T(8,128)(2,1)S(1)}, u32[]{:S(2)}, u32[]{:S(2)}) collective-permute-start(bf16[256,512]{1,0:T(8,128)(2,1)S(1)} %maximum_select_fusion), channel_id=1, source_target_pairs={{0,6},{2,4},{4,2},{6,0},{1,7},{3,5},{5,3},{7,1},{8,14},{10,12},{12... | collective-permute-start | bytes 786440 | tf_op jit(solution)/shard_map/ppermute | solution.py:21
  18.5 19.1 %collective-permute-start.10 = (bf16[256,512]{1,0:T(8,128)(2,1)S(1)}, bf16[256,512]{1,0:T(8,128)(2,1)S(1)}, u32[]{:S(2)}, u32[]{:S(2)}) collective-permute-start(bf16[256,512]{1,0:T(8,128)(2,1)S(1)} %maximum_select_fusion), channel_id=1, source_target_pairs={{0,2},{2,0},{4,6},{6,4},{1,3},{3,1},{5,7},{7,5},{8,10},{10,8},{12,... | collective-permute-start | bytes 786440 | tf_op jit(solution)/shard_map/ppermute | solution.py:21
  35.9 30.3 %collective-permute-start = (bf16[256,1280]{1,0:T(8,128)(2,1)S(1)}, bf16[256,1280]{1,0:T(8,128)(2,1)S(1)}, u32[]{:S(2)}, u32[]{:S(2)}) collective-permute-start(bf16[256,1280]{1,0:T(8,128)(2,1)S(1)} %get-tuple-element.66), channel_id=1, source_target_pairs={{0,17},{1,16},{16,1},{17,0},{2,19},{3,18},{18,3},{19,2},{4,21},{5,... | collective-permute-start | bytes 1966088 | tf_op jit(solution)/shard_map/ppermute | solution.py:21
  37.4 28.3 %collective-permute-start.2 = (bf16[256,1280]{1,0:T(8,128)(2,1)}, bf16[256,1280]{1,0:T(8,128)(2,1)S(1)}, u32[]{:S(2)}, u32[]{:S(2)}) collective-permute-start(bf16[256,1280]{1,0:T(8,128)(2,1)} %get-tuple-element.65), channel_id=1, source_target_pairs={{0,16},{1,17},{16,0},{17,1},{2,18},{3,19},{18,2},{19,3},{4,20},{5,... | collective-permute-start | bytes 1966088 | tf_op jit(solution)/shard_map/ppermute | solution.py:21
  37.7 29.1 %collective-permute-start.5 = (bf16[256,1280]{1,0:T(8,128)(2,1)S(1)}, bf16[256,1280]{1,0:T(8,128)(2,1)S(1)}, u32[]{:S(2)}, u32[]{:S(2)}) collective-permute-start(bf16[256,1280]{1,0:T(8,128)(2,1)S(1)} %collective-permute-done.4), channel_id=1, source_target_pairs={{0,8},{8,0},{1,9},{9,1},{2,10},{10,2},{3,11},{11,3},{4,12},{12,4},... | collective-permute-start | bytes 1966088 | tf_op jit(solution)/shard_map/ppermute | solution.py:21
  65.7 2.4 %collective-permute-start.3 = (bf16[256,1280]{1,0:T(8,128)(2,1)S(1)}, bf16[256,1280]{1,0:T(8,128)(2,1)S(1)}, u32[]{:S(2)}, u32[]{:S(2)}) collective-permute-start(bf16[256,1280]{1,0:T(8,128)(2,1)S(1)} %collective-permute-done.2), channel_id=1, source_target_pairs={{0,8},{8,0},{1,9},{9,1},{2,10},{10,2},{3,11},{11,3},{4,12},{12,4},... | collective-permute-start | bytes 1966088 | tf_op jit(solution)/shard_map/ppermute | solution.py:21
  66.2 3.3 %collective-permute-start.1 = (bf16[256,1280]{1,0:T(8,128)(2,1)S(1)}, bf16[256,1280]{1,0:T(8,128)(2,1)S(1)}, u32[]{:S(2)}, u32[]{:S(2)}) collective-permute-start(bf16[256,1280]{1,0:T(8,128)(2,1)S(1)} %collective-permute-done), channel_id=1, source_target_pairs={{0,8},{8,0},{1,9},{9,1},{2,10},{10,2},{3,11},{11,3},{4,12},{12,4},... | collective-permute-start | bytes 1966088 | tf_op jit(solution)/shard_map/ppermute | solution.py:21
  71.4 14.3 %all-to-all-start = ((f32[16,8,128]{2,1,0:T(8,128)}), f32[16,8,128]{2,1,0:T(8,128)S(1)}, u32[]{:S(2)}, u32[]{:S(2)}) async-start(f32[16,8,128]{2,1,0:T(8,128)} %broadcast_in_dim.65), calls=%async_computation | async-start | bytes 131072 | tf_op jit(solution)/shard_map/all_to_all | solution.py:25
  78.9 10.3 %collective-permute-start.14 = (bf16[128,1280]{1,0:T(8,128)(2,1)}, bf16[128,1280]{1,0:T(8,128)(2,1)S(1)}, u32[]{:S(2)}, u32[]{:S(2)}) collective-permute-start(bf16[128,1280]{1,0:T(8,128)(2,1)} %get-tuple-element.72), channel_id=1, source_target_pairs={{0,16},{16,0},{1,17},{17,1},{2,18},{18,2},{3,19},{19,3},{4,20},{20... | collective-permute-start | bytes 983048 | tf_op jit(solution)/shard_map/ppermute | solution.py:21
  96.9 14.3 %collective-permute-start.15 = (bf16[128,1024]{0,1:T(8,128)(2,1)S(1)}, bf16[128,1024]{0,1:T(8,128)(2,1)S(1)}, u32[]{:S(2)}, u32[]{:S(2)}) collective-permute-start(bf16[128,1024]{0,1:T(8,128)(2,1)S(1)} %pad_maximum_fusion), channel_id=1, source_target_pairs={{0,1},{1,0},{16,17},{17,16},{2,3},{3,2},{18,19},{19,18},{4,5},{5,4... | collective-permute-start | bytes 786440 | tf_op jit(solution)/shard_map/ppermute | solution.py:21
  98.5 12.6 %collective-permute-start.16 = (bf16[128,1024]{0,1:T(8,128)(2,1)S(1)}, bf16[128,1024]{0,1:T(8,128)(2,1)S(1)}, u32[]{:S(2)}, u32[]{:S(2)}) collective-permute-start(bf16[128,1024]{0,1:T(8,128)(2,1)S(1)} %pad_maximum_fusion.1), channel_id=1, source_target_pairs={{0,16},{1,17},{16,0},{17,1},{2,18},{3,19},{18,2},{19,3},{4,20},{5,... | collective-permute-start | bytes 786440 | tf_op jit(solution)/shard_map/ppermute | solution.py:21
  100.0 11.3 %collective-permute-start.17 = (bf16[128,1024]{0,1:T(8,128)(2,1)S(1)}, bf16[128,1024]{0,1:T(8,128)(2,1)S(1)}, u32[]{:S(2)}, u32[]{:S(2)}) collective-permute-start(bf16[128,1024]{0,1:T(8,128)(2,1)S(1)} %pad_maximum_fusion.2), channel_id=1, source_target_pairs={{0,17},{1,16},{16,1},{17,0},{2,19},{3,18},{18,3},{19,2},{4,21},{5,... | collective-permute-start | bytes 786440 | tf_op jit(solution)/shard_map/ppermute | solution.py:21
  103.6 13.4 %all-to-all-start.1 = ((f32[16,3,128]{2,1,0:T(4,128)}), f32[16,3,128]{2,1,0:T(4,128)S(1)}, u32[]{:S(2)}, u32[]{:S(2)}) async-start(f32[16,3,128]{2,1,0:T(4,128)} %bitcast.31), calls=%async_computation.1 | async-start | bytes 65536 | tf_op jit(solution)/shard_map/all_to_all | solution.py:25
  111.5 9.1 %collective-permute-start.20 = (bf16[128,256]{0,1:T(8,128)(2,1)S(1)}, bf16[128,256]{0,1:T(8,128)(2,1)S(1)}, u32[]{:S(2)}, u32[]{:S(2)}) collective-permute-start(bf16[128,256]{0,1:T(8,128)(2,1)S(1)} %get-tuple-element.75), channel_id=1, source_target_pairs={{0,6},{2,4},{4,2},{6,0},{1,7},{3,5},{5,3},{7,1},{8,14},{10,12},{12... | collective-permute-start | bytes 196616 | tf_op jit(solution)/shard_map/ppermute | solution.py:21
  114.8 5.7 %collective-permute-start.19 = (bf16[128,256]{0,1:T(8,128)(2,1)S(1)}, bf16[128,256]{0,1:T(8,128)(2,1)S(1)}, u32[]{:S(2)}, u32[]{:S(2)}) collective-permute-start(bf16[128,256]{0,1:T(8,128)(2,1)S(1)} %get-tuple-element.76), channel_id=1, source_target_pairs={{0,4},{2,6},{4,0},{6,2},{1,5},{3,7},{5,1},{7,3},{8,12},{10,14},{12... | collective-permute-start | bytes 196616 | tf_op jit(solution)/shard_map/ppermute | solution.py:21
  114.8 5.7 %collective-permute-start.18 = (bf16[128,256]{0,1:T(8,128)(2,1)S(1)}, bf16[128,256]{0,1:T(8,128)(2,1)S(1)}, u32[]{:S(2)}, u32[]{:S(2)}) collective-permute-start(bf16[128,256]{0,1:T(8,128)(2,1)S(1)} %get-tuple-element.74), channel_id=1, source_target_pairs={{0,2},{2,0},{4,6},{6,4},{1,3},{3,1},{5,7},{7,5},{8,10},{10,8},{12,... | collective-permute-start | bytes 196616 | tf_op jit(solution)/shard_map/ppermute | solution.py:21
  117.5 1.2 collective-permute-start.21
  (19 other events, 69.7 us)

commit v4 on v3

--- a/solution.py
+++ b/solution.py
@@ -1,8 +1,11 @@
+import functools
 import math
 
 import jax
 import jax.numpy as jnp
 from jax import lax
+from jax.experimental import pallas as pl
+from jax.experimental.pallas import tpu as pltpu
 from jax.sharding import Mesh, PartitionSpec as P
 
 LANES = 128
@@ -25,10 +28,107 @@
     return lax.all_to_all(array, axes, 0, 0, tiled=True)
 
 
+VMEM = pl.BlockSpec(memory_space=pltpu.VMEM)
+SMEM = pl.BlockSpec(memory_space=pltpu.SMEM)
+ANYWHERE = pl.BlockSpec(memory_space=pltpu.HBM)
+
+
+def forward_kernel(places, slabs, *refs):
+    count = len(places)
+    scalars, hidden, own_parts = refs[0], refs[1 : 1 + slabs], refs[1 + slabs]
+    blocks, refs = refs[2 + slabs : 2 + slabs + count], refs[2 + slabs + count :]
+    result, near, far, sent, held, pairs, logits, parts, sems, pair_sems, out_sems, last_sem = refs
+    copies = [
+        pltpu.make_async_copy(block, held.at[k], sems.at[k]) for k, block in enumerate(blocks)
+    ]
+    for k in range(count):
+        for ms in range(slabs):
+
+            @pl.when(scalars[2 + 3 * k] == ms)
+            def _(k=k, ms=ms):
+                pltpu.make_async_copy(hidden[ms], pairs.at[k], pair_sems.at[k]).start()
+
+        copies[k].start()
+    rows, width = held.shape[1:]
+    chunk = count // 4
+    for begin in range(0, count, chunk):
+        lhs = []
+        for k in range(begin, begin + chunk):
+            pltpu.make_async_copy(hidden[0], pairs.at[k], pair_sems.at[k]).wait()
+            even = scalars[3 + 3 * k] == 0
+            lhs.append(jnp.where(even, pairs[k, :, :rows], pairs[k, :, rows:]))
+            copies[k].wait()
+            for side, weight in enumerate((near, far)):
+
+                @pl.when(scalars[4 + 3 * k] == side)
+                def _(k=k, weight=weight):
+                    place = places[k]
+                    pltpu.make_async_copy(held.at[k], weight.at[place], out_sems.at[k]).start()
+
+        rhs = held[begin : begin + chunk].reshape(chunk * rows, width)
+        term = jnp.dot(jnp.concatenate(lhs, axis=1), rhs, preferred_element_type=jnp.float32)
+        logits[...] = logits[...] + term if begin else term
+    leaving = pltpu.make_async_copy(logits, result, last_sem)
+    leaving.start()
+    values = logits[...]
+    mine = lax.broadcasted_iota(jnp.int32, values.shape, 1) >= scalars[0]
+    top = jnp.max(jnp.where(mine, values, -3e38), axis=1, keepdims=True)
+    total = jnp.sum(jnp.where(mine, jnp.exp(values - top), 0.0), axis=1, keepdims=True)
+    lane = lax.broadcasted_iota(jnp.int32, (values.shape[0], LANES), 1)
+    packed = jnp.where(lane == 0, top, jnp.where(lane == 1, total, 0.0))
+    parts[...] = packed.T[:8]
+    tokens = own_parts.shape[1]
+    groups = values.shape[0] // tokens
+    for g in range(groups):
+        begin = pl.multiple_of((scalars[1] ^ g) * tokens, tokens)
+        both = parts[0:2, pl.ds(begin, tokens)]
+        sent[:, 2 * g : 2 * g + 2, :] = jnp.broadcast_to(both, (sent.shape[0], 2, tokens))
+    own = own_parts[...]
+    sent[:, 2 * groups :, :] = jnp.broadcast_to(own, (sent.shape[0],) + own.shape)
+    leaving.wait()
+    for k in range(count):
+        pltpu.make_async_copy(held.at[k], near.at[0], out_sems.at[k]).wait()
+
+
+def forward(scalars, hidden, blocks, places, own_parts, receivers):
+    height = hidden[0].shape[0]
+    rows, width = blocks[0].shape
+    count, slabs = len(blocks), len(hidden)
+    extra, tokens = own_parts.shape
+    kind = blocks[0].dtype
+    return pl.pallas_call(
+        functools.partial(forward_kernel, places, slabs),
+        out_shape=[
+            jax.ShapeDtypeStruct((height, width), jnp.float32),
+            jax.ShapeDtypeStruct((count // 2, rows, width), kind),
+            jax.ShapeDtypeStruct((count // 2, rows, width), kind),
+            jax.ShapeDtypeStruct((receivers, 2 * height // tokens + extra, tokens), jnp.float32),
+        ],
+        in_specs=[SMEM] + [ANYWHERE] * slabs + [VMEM] + [ANYWHERE] * count,
+        out_specs=[ANYWHERE, ANYWHERE, ANYWHERE, VMEM],
+        scratch_shapes=[
+            pltpu.VMEM((count, rows, width), kind),
+            pltpu.VMEM((count,) + hidden[0].shape, kind),
+            pltpu.VMEM((height, width), jnp.float32),
+            pltpu.VMEM((8, height), jnp.float32),
+            pltpu.SemaphoreType.DMA((count,)),
+            pltpu.SemaphoreType.DMA((count,)),
+            pltpu.SemaphoreType.DMA((count,)),
+            pltpu.SemaphoreType.DMA,
+        ],
+        compiler_params=pltpu.CompilerParams(vmem_limit_bytes=62_300_000),
+        cost_estimate=pl.CostEstimate(
+            flops=2 * count * height * rows * width,
+            bytes_accessed=4 * count * rows * width,
+            transcendentals=0,
+        ),
+    )(scalars, *hidden, own_parts, *blocks)
+
+
 def on_device(student_hidden, student_blocks, teacher_logits, token_ids, loss_mask):
     row_g, core, slab, half = (lax.axis_index(axis) for axis in ("g", "c", "s", "h"))
     n_g, n_s = lax.axis_size("g"), lax.axis_size("s")
-    tokens, feature = student_hidden.shape
+    tokens, _ = student_hidden.shape
     piece = student_blocks[0]
     rows = piece.shape[0]
     vt = piece.shape[1] // 2
@@ -49,10 +149,12 @@
     def columns_of(g, h):
         return lax.dynamic_slice_in_dim(piece, h * vt + offset(g), width, 1)
 
-    blocks = {(0, 0, 0): columns_of(row_g, half)}
+    blocks = {}
     for mg, mh in others:
         cut = columns_of(row_g ^ mg, half ^ mh)
+        piece, _ = lax.optimization_barrier((piece, cut))
         blocks[mg, mh, 0] = exchanged(cut, g=mg, h=mh)
+    blocks[0, 0, 0] = columns_of(row_g, half)
     for mg, mh in [(0, 0)] + others:
         blocks[mg, mh, 1] = exchanged(blocks[mg, mh, 0], c=1)
 
@@ -80,23 +182,22 @@
     gathered = [plane_hidden]
     gathered += [exchanged(plane_hidden, s=ms) for ms in range(1, n_s)]
 
-    def hidden_of(mg, mh, mc):
-        index = (half ^ mh) * n_g + (row_g ^ mg)
-        pair = lax.select_n(slab ^ index, *gathered)
-        return jnp.where((core ^ mc) == 0, pair[:, :feature], pair[:, feature:])
-
-    logits = None
-    for mg, mh in [(0, 0)] + others:
-        for mc in range(2):
-            block = blocks[mg, mh, mc]
-            if logits is not None:
-                block, logits = lax.optimization_barrier((block, logits))
-            term = jnp.dot(hidden_of(mg, mh, mc), block, preferred_element_type=jnp.float32)
-            logits = term if logits is None else logits + term
-
     local_column = lax.broadcasted_iota(jnp.int32, (1, width), 1)
     shared = jnp.where(row_g > 0, offset(row_g - 1) + width - offset(row_g), 0)
     mine = local_column >= shared
+
+    crossed = core ^ half
+    members = [(0, 0)] + others
+    keys = [(*member, mc) for member in members[:2] for mc in range(2)]
+    keys += [(*member, mc) for mc in range(2) for member in members[2:]]
+
+    values = [shared, row_g]
+    for mg, mh, mc in keys:
+        values += [slab ^ ((half ^ mh) * n_g + (row_g ^ mg)), core ^ mc, crossed ^ mc]
+    places = [plane.index((mg, mh)) for mg, mh, _ in keys]
+    scalars = jnp.stack(values).astype(jnp.int32)
+    chosen = [blocks[key] for key in keys]
+    logits, *weights, sent = forward(scalars, gathered, chosen, places, own_parts, 2 * n_s * n_g)
 
     def by_group(stack):
         parts = stack.reshape(stack.shape[0], n_g, tokens)
@@ -104,13 +205,8 @@
             [lax.dynamic_index_in_dim(parts, row_g ^ g, 1, False) for g in range(n_g)]
         )
 
-    local_max = jnp.max(jnp.where(mine, logits, jnp.float32(-3e38)), axis=1)
-    local_sum = jnp.sum(jnp.where(mine, jnp.exp(logits - local_max[:, None]), 0.0), axis=1)
-    sent = by_group(jnp.stack([local_max, local_sum])).reshape(2 * n_g, tokens)
-    sent = jnp.concatenate([sent, own_parts])
-    every = from_every(jnp.broadcast_to(sent, (2 * n_s * n_g,) + sent.shape), ("g", "s", "h"))
+    every = from_every(sent, ("g", "s", "h"))
     teacher, _ = lax.optimization_barrier((teacher, every))
-    teacher = jnp.concatenate(teacher).astype(jnp.float32)
     student_parts = every[:, : 2 * n_g].reshape(2 * n_s * n_g, n_g, 2, tokens)
     student_parts = jnp.concatenate(
         [lax.dynamic_index_in_dim(student_parts, row_g ^ mg, 1, False) for mg in range(n_g)], 2
@@ -129,39 +225,39 @@
     coded, ids = teacher_parts[0, 2], teacher_parts[0, 3].astype(jnp.int32)
     chip_counts = jnp.floor(coded * 0.5)
     mask_float = coded - 2.0 * chip_counts
-    mask_total = jnp.sum(chip_counts.reshape(n_g, tokens)[:, 0])
-    factor = (mask_float / mask_total)[:, None]
+    totals = jnp.sum(chip_counts.reshape(n_g, tokens), axis=0)
+    mask_total = totals[0]
+    factor = (mask_float / jnp.concatenate([totals] * n_g))[:, None]
 
     def log_probs(logits, teacher):
         student_logp = logits - top[:, None] - log_total[:, None]
         return student_logp, teacher - t_top[:, None] - t_log[:, None]
 
-    student_logp, teacher_logp = log_probs(logits, teacher)
+    student_logp, teacher_logp = log_probs(logits, jnp.concatenate(teacher).astype(jnp.float32))
     delta = factor * (jnp.exp(student_logp) - jnp.exp(teacher_logp))
     dlogits = jnp.where(mine, delta, 0.0).astype(jnp.bfloat16)
 
-    def features_of(mc, mg, mh):
-        block = blocks[mg, mh, mc]
+    wide = len(plane) * rows
+
+    def features_of(mh):
         return lax.dot_general(
-            dlogits, block, (((1,), (1,)), ((), ())), preferred_element_type=jnp.float32
+            dlogits,
+            weights[mh].reshape(wide, width),
+            (((1,), (1,)), ((), ())),
+            preferred_element_type=jnp.float32,
         )
 
-    grads = [[features_of(mc, mg, mh) for mg, mh in plane] for mc in range(2)]
-    crossed = (core ^ half) == 1
+    far = features_of(1)
+    grads = (features_of(0), far)
 
     def for_half(mg, mh):
-        picks = [jnp.where(crossed, b, a) for a, b in zip(grads[mh], grads[1 - mh])]
-        return jnp.concatenate([p[mg * tokens : (mg + 1) * tokens] for p in picks], axis=1)
+        return grads[mh][mg * tokens : (mg + 1) * tokens]
 
     partial = for_half(0, 0)
     terms = [for_half(mg, mh).astype(jnp.bfloat16) for mg, mh in others]
     arrived = [(exchanged(term, g=mg, h=mh), mg, mh) for term, (mg, mh) in zip(terms, others)]
-    for part, kg, kh in arrived:
-        order = [(mh ^ kh) * n_g + (mg ^ kg) for mg, mh in plane]
-        part = jnp.concatenate([part[:, j * rows : (j + 1) * rows] for j in order], axis=1)
-        partial = partial + part.astype(jnp.float32)
-
     _, logits, teacher = lax.optimization_barrier((terms, logits, teacher))
+    teacher = jnp.concatenate(teacher).astype(jnp.float32)
     student_logp, teacher_logp = log_probs(logits, teacher)
     gap = jnp.exp(teacher_logp) * (teacher_logp - student_logp)
     kl_part = jnp.sum(jnp.where(mine, gap, 0.0), axis=1)
@@ -174,19 +270,23 @@
     every = from_every(sent.reshape(-1, 3, tokens), ("g", "s", "h"))
 
     def for_slab(s):
-        index = (half ^ (s // n_g)) * n_g + (row_g ^ (s % n_g))
-        return lax.dynamic_slice_in_dim(partial, index * rows, rows, 1)
+        total = 0.0
+        for part, kg, kh in [(partial, 0, 0)] + arrived:
+            index = (half ^ kh ^ (s // n_g)) * n_g + (row_g ^ kg ^ (s % n_g))
+            block = lax.dynamic_slice_in_dim(part, index * rows, rows, 1)
+            total = total + block.astype(jnp.float32)
+        return total
 
     result = for_slab(slab)
     slab_terms = [for_slab(slab ^ ms).astype(jnp.bfloat16) for ms in range(1, n_s)]
-    arrived = [exchanged(term, s=ms) for ms, term in enumerate(slab_terms, 1)]
+    slab_parts = [exchanged(term, s=ms) for ms, term in enumerate(slab_terms, 1)]
     every, _ = lax.optimization_barrier((every, slab_terms))
     token_kl, picked, core_loss = jnp.sum(every, axis=0)
     sampled = picked - top[:tokens] - log_total[:tokens]
     core_loss = jnp.broadcast_to(core_loss, (8, LANES))
     loss = (core_loss + exchanged(core_loss, c=1))[0, 0] / mask_total
 
-    for part in arrived:
+    for part in slab_parts:
         result = result + part.astype(jnp.float32)
     return (result.astype(jnp.bfloat16), token_kl, sampled, loss)
 

time: 123 us -> 131 us (1.065)
  Pallas kernels: 0 us -> 7.69 us
  matrix products: 5.67 us -> 1.74 us
  waiting for transfers between devices: 53 us -> 56.7 us
  other arithmetic: 8.07 us -> 11.3 us
  local copies, waits for them, and re-layouts: 14.9 us -> 13.2 us
    pallas_call x0 -> x1, Pallas kernels: none -> 7.69 us  [forward(): pl.pallas_call(functools.partial(forward_kernel, places, slabs), out_shap...]
    all_to_all x2, waiting for transfers between devices: 5.98 us -> 10.1 us  [from_every(): return lax.all_to_all(array, axes, 0, 0, tiled=True)]
    dot_general x16 -> x2, matrix products: 5.67 us -> 1.74 us  [features_of(): lax.dot_general(dlogits, weights[mh].reshape(wide, width), (((1,), (1,)),...]
    unnamed x42 -> x20, local copies, waits for them, and re-layouts: 5.12 us -> 1.51 us
    all_to_all x2, starting transfers between devices: 12.6 us -> 9.45 us  [from_every(): return lax.all_to_all(array, axes, 0, 0, tiled=True)]
    ppermute x22, starting transfers between devices: 23.7 us -> 26.5 us  [exchanged(): return lax.ppermute(array, axes, pairs)]
    select_n x1, other arithmetic: 0.12 us -> 1.76 us  [on_device(): jnp.where(half == 0, jnp.concatenate(sides, axis=1), jnp.concatenate(side...]
    convert_element_type x1, other arithmetic: 0.04 us -> 1.59 us  [on_device(): return (result.astype(jnp.bfloat16), token_kl, sampled, loss)]
  transfers between devices with their start and end apart: 24 -> 24, of which waited for: 7 -> 9; matrix products, arithmetic and copies ran while one was open for 14% -> 14% of each run, Pallas kernels for 0% -> 6%
where the time goes in v4:
time: 131 us; the launch traced here: 130 us
  waiting for transfers between devices  56.7 us (43%)
  starting transfers between devices  36 us (27%)
  local copies, waits for them, and re-layouts  13.2 us (10%)
  other arithmetic  11.3 us (9%)
  Pallas kernels  7.69 us (6%)
  between operations  3.69 us (3%)
  matrix products  1.74 us (1%)
    ppermute x22, waiting for transfers between devices, exchanged(): return lax.ppermute(array, axes, pairs)  46.7 us
    ppermute x22, starting transfers between devices, exchanged(): return lax.ppermute(array, axes, pairs)  26.5 us
    all_to_all x2, waiting for transfers between devices, from_every(): return lax.all_to_all(array, axes, 0, 0, tiled=True)  10.1 us
    all_to_all x2, starting transfers between devices, from_every(): return lax.all_to_all(array, axes, 0, 0, tiled=True)  9.45 us
    pallas_call x1, Pallas kernels, forward(): pl.pallas_call(functools.partial(forward_kernel, places, slabs), out_shap...  7.69 us
    dynamic_slice x4, local copies, waits for them, and re-layouts, columns_of(): return lax.dynamic_slice_in_dim(piece, h * vt + offset(g), width, 1)  3.64 us
  transfers between devices with their start and end apart: 24, of which 9 were waited for; matrix products, arithmetic and copies ran while one was open for 14% of the time, Pallas kernels for 6%

profile of v4, /device:TPU:0, one launch (start us, length us, event | category | flops | bytes accessed | tf_op | source)
XLA Modules:
  0.0 130.4 jit_solution(930619508048813409)
XLA Ops:
  0.6 3.0 %collective-permute-start.1 = (bf16[128,256]{1,0:T(8,128)(2,1)}, bf16[128,256]{1,0:T(8,128)(2,1)}, u32[]{:S(2)}, u32[]{:S(2)}) collective-permute-start(bf16[128,256]{1,0:T(8,128)(2,1)} %param.5), channel_id=1, source_target_pairs={{0,1},{1,0},{16,17},{17,16},{2,3},{3,2},{18,19},{19,18},{4,5},{5,4... | collective-permute-start | bytes 196616 | tf_op jit(solution)/shard_map/ppermute | solution.py:24
  3.7 1.5 %collective-permute-start.2 = (bf16[128,256]{1,0:T(8,128)(2,1)}, bf16[128,256]{1,0:T(8,128)(2,1)}, u32[]{:S(2)}, u32[]{:S(2)}) collective-permute-start(bf16[128,256]{1,0:T(8,128)(2,1)} %param.5), channel_id=1, source_target_pairs={{0,17},{1,16},{16,1},{17,0},{2,19},{3,18},{18,3},{19,2},{4,21},{5,... | collective-permute-start | bytes 196616 | tf_op jit(solution)/shard_map/ppermute | solution.py:24
  6.1 1.5 %collective-permute-start.8 = (bf16[256,1280]{1,0:T(8,128)(2,1)}, bf16[256,1280]{1,0:T(8,128)(2,1)}, u32[]{:S(2)}, u32[]{:S(2)}) collective-permute-start(bf16[256,1280]{1,0:T(8,128)(2,1)} %dynamic-slice_bitcast_fusion), channel_id=1, source_target_pairs={{0,1},{1,0},{16,17},{17,16},{2,3},{3,2},{18,19},{19,18},{4,5},{5,4... | collective-permute-start | bytes 1966088 | tf_op jit(solution)/shard_map/ppermute | solution.py:24
  9.9 1.5 %collective-permute-start.11 = (bf16[256,1280]{1,0:T(8,128)(2,1)}, bf16[256,1280]{1,0:T(8,128)(2,1)}, u32[]{:S(2)}, u32[]{:S(2)}) collective-permute-start(bf16[256,1280]{1,0:T(8,128)(2,1)} %constant_dynamic-slice_fusion.9), channel_id=1, source_target_pairs={{0,17},{1,16},{16,1},{17,0},{2,19},{3,18},{18,3},{19,2},{4,21},{5,... | collective-permute-start | bytes 1966088 | tf_op jit(solution)/shard_map/ppermute | solution.py:24
  17.0 22.8 %collective-permute-done = bf16[128,256]{1,0:T(8,128)(2,1)S(1)} collective-permute-done((bf16[128,256]{1,0:T(8,128)(2,1)S(1)}, bf16[128,256]{1,0:T(8,128)(2,1)S(1)}, u32[]{:S(2)}, u32[]{:S(2)}) %collective-permute-start) | collective-permute-done | bytes 65568 | tf_op jit(solution)/shard_map/ppermute | solution.py:24
  40.4 1.8 %maximum_select_fusion.refs_1_ = bf16[256,512]{1,0:T(8,128)(2,1)} fusion(bf16[256,256]{1,0:T(8,128)(2,1)S(1)} %constant_dynamic-update-slice_fusion.2, bf16[256,256]{1,0:T(8,128)(2,1)} %constant_dynamic-update-slice_fusion, pred[]{:T(512)S(6)} %eq.33), kind=kLoop, calls=%fused_computation.7 | loop fusion | flops 1179648 | bytes 524289 | tf_op jit(solution)/shard_map/jit(_where)/select_n | solution.py:179
  42.1 1.6 %collective-permute-start.3 = (bf16[256,512]{1,0:T(8,128)(2,1)}, bf16[256,512]{1,0:T(8,128)(2,1)}, u32[]{:S(2)}, u32[]{:S(2)}) collective-permute-start(bf16[256,512]{1,0:T(8,128)(2,1)} %maximum_select_fusion.refs_1_), channel_id=1, source_target_pairs={{0,2},{2,0},{4,6},{6,4},{1,3},{3,1},{5,7},{7,5},{8,10},{10,8},{12,... | collective-permute-start | bytes 786440 | tf_op jit(solution)/shard_map/ppermute | solution.py:24
  43.8 5.1 %collective-permute-done.3.refs_2_ = bf16[256,512]{1,0:T(8,128)(2,1)} collective-permute-done((bf16[256,512]{1,0:T(8,128)(2,1)}, bf16[256,512]{1,0:T(8,128)(2,1)}, u32[]{:S(2)}, u32[]{:S(2)}) %collective-permute-start.3) | collective-permute-done | bytes 262176 | tf_op jit(solution)/shard_map/ppermute | solution.py:24
  48.9 2.6 %collective-permute-start.4 = (bf16[256,512]{1,0:T(8,128)(2,1)}, bf16[256,512]{1,0:T(8,128)(2,1)}, u32[]{:S(2)}, u32[]{:S(2)}) collective-permute-start(bf16[256,512]{1,0:T(8,128)(2,1)} %maximum_select_fusion.refs_1_), channel_id=1, source_target_pairs={{0,4},{2,6},{4,0},{6,2},{1,5},{3,7},{5,1},{7,3},{8,12},{10,14},{12... | collective-permute-start | bytes 786440 | tf_op jit(solution)/shard_map/ppermute | solution.py:24
  54.9 6.4 %collective-permute-done.4.refs_3_ = bf16[256,512]{1,0:T(8,128)(2,1)} collective-permute-done((bf16[256,512]{1,0:T(8,128)(2,1)}, bf16[256,512]{1,0:T(8,128)(2,1)}, u32[]{:S(2)}, u32[]{:S(2)}) %collective-permute-start.4) | collective-permute-done | bytes 262176 | tf_op jit(solution)/shard_map/ppermute | solution.py:24
  61.3 3.5 %collective-permute-start.5 = (bf16[256,512]{1,0:T(8,128)(2,1)}, bf16[256,512]{1,0:T(8,128)(2,1)S(1)}, u32[]{:S(2)}, u32[]{:S(2)}) collective-permute-start(bf16[256,512]{1,0:T(8,128)(2,1)} %maximum_select_fusion.refs_1_), channel_id=1, source_target_pairs={{0,6},{2,4},{4,2},{6,0},{1,7},{3,5},{5,3},{7,1},{8,14},{10,12},{12... | collective-permute-start | bytes 786440 | tf_op jit(solution)/shard_map/ppermute | solution.py:24
  65.5 5.4 %collective-permute-done.5.refs_4_ = bf16[256,512]{1,0:T(8,128)(2,1)S(1)} collective-permute-done((bf16[256,512]{1,0:T(8,128)(2,1)}, bf16[256,512]{1,0:T(8,128)(2,1)S(1)}, u32[]{:S(2)}, u32[]{:S(2)}) %collective-permute-start.5) | collective-permute-done | bytes 262176 | tf_op jit(solution)/shard_map/ppermute | solution.py:24
  70.8 2.1 %collective-permute-start.14 = (bf16[128,1280]{1,0:T(8,128)(2,1)}, bf16[128,1280]{1,0:T(8,128)(2,1)S(1)}, u32[]{:S(2)}, u32[]{:S(2)}) collective-permute-start(bf16[128,1280]{1,0:T(8,128)(2,1)} %get-tuple-element.37), channel_id=1, source_target_pairs={{0,16},{16,0},{1,17},{17,1},{2,18},{18,2},{3,19},{19,3},{4,20},{20... | collective-permute-start | bytes 983048 | tf_op jit(solution)/shard_map/ppermute | solution.py:24
  72.9 7.7 %shard_map.84 = (f32[256,1280]{1,0:T(8,128)}, bf16[4,256,1280]{2,1,0:T(8,128)(2,1)}, bf16[4,256,1280]{2,1,0:T(8,128)(2,1)}, f32[16,8,128]{2,1,0:T(8,128)}) custom-call(s32[26]{0:T(128)} %stack.90.refs_0_, bf16[256,512]{1,0:T(8,128)(2,1)} %maximum_select_fusion.refs_1_, bf16[256,512]{1,0:T(8,128)(2,1)} %collective-permute-done.3.refs_2_, ...), custom_call_target="tpu_custom_call" | custom-call | flops 1342177280 | bytes 10485760 | tf_op jit(solution)/shard_map/pallas_call | solution.py:99
  80.6 5.9 %all-to-all-start = ((f32[16,8,128]{2,1,0:T(8,128)}), f32[16,8,128]{2,1,0:T(8,128)S(1)}, u32[]{:S(2)}, u32[]{:S(2)}) async-start(f32[16,8,128]{2,1,0:T(8,128)} %get-tuple-element.20), calls=%async_computation | async-start | bytes 131072 | tf_op jit(solution)/shard_map/all_to_all | solution.py:28
  86.9 7.3 %all-to-all-done = f32[16,8,128]{2,1,0:T(8,128)S(1)} async-done(((f32[16,8,128]{2,1,0:T(8,128)}), f32[16,8,128]{2,1,0:T(8,128)S(1)}, u32[]{:S(2)}, u32[]{:S(2)}) %all-to-all-start) | async-done | bytes 65568 | tf_op jit(solution)/shard_map/all_to_all | solution.py:28
  94.4 2.2 %select_convert_fusion = bf16[256,1280]{1,0:T(8,128)(2,1)S(1)} fusion(f32[256,1280]{1,0:T(8,128)} %get-tuple-element.28, bf16[128,1280]{1,0:T(8,128)(2,1)S(1)} %collective-permute-done.14, bf16[128,1280]{1,0:T(8,128)(2,1)S(1)} %get-tuple-element.26, f32[256]{0:T(256)S(1)} %log.15, f32[256]{0:T(256)S(1)} %fusion.13, f32[256]{0:T(256)S(1)} %log.14, ...), kind=kLoop, calls=%fused_computation.2 | loop fusion | flops 3932160 | bytes 2627840 | tf_op jit(solution)/shard_map/convert_element_type | solution.py:238
  106.5 3.5 %all-to-all-start.1 = ((f32[16,3,128]{2,1,0:T(4,128)}), f32[16,3,128]{2,1,0:T(4,128)S(1)}, u32[]{:S(2)}, u32[]{:S(2)}) async-start(f32[16,3,128]{2,1,0:T(4,128)} %bitcast.36), calls=%async_computation.1 | async-start | bytes 65536 | tf_op jit(solution)/shard_map/all_to_all | solution.py:28
  110.0 1.9 %collective-permute-done.17 = bf16[128,1024]{1,0:T(8,128)(2,1)} collective-permute-done((bf16[128,1024]{1,0:T(8,128)(2,1)}, bf16[128,1024]{1,0:T(8,128)(2,1)}, u32[]{:S(2)}, u32[]{:S(2)}) %collective-permute-start.17) | collective-permute-done | bytes 262176 | tf_op jit(solution)/shard_map/ppermute | solution.py:24
  111.9 1.5 %collective-permute-done.16 = bf16[128,1024]{1,0:T(8,128)(2,1)} collective-permute-done((bf16[128,1024]{1,0:T(8,128)(2,1)}, bf16[128,1024]{1,0:T(8,128)(2,1)}, u32[]{:S(2)}, u32[]{:S(2)}) %collective-permute-start.16) | collective-permute-done | bytes 262176 | tf_op jit(solution)/shard_map/ppermute | solution.py:24
  114.5 2.8 %all-to-all-done.1 = f32[16,3,128]{2,1,0:T(4,128)S(1)} async-done(((f32[16,3,128]{2,1,0:T(4,128)}), f32[16,3,128]{2,1,0:T(4,128)S(1)}, u32[]{:S(2)}, u32[]{:S(2)}) %all-to-all-start.1) | async-done | bytes 24608 | tf_op jit(solution)/shard_map/all_to_all | solution.py:28
  119.7 3.1 %collective-permute-start.20 = (bf16[128,256]{1,0:T(8,128)(2,1)S(1)}, bf16[128,256]{1,0:T(8,128)(2,1)S(1)}, u32[]{:S(2)}, u32[]{:S(2)}) collective-permute-start(bf16[128,256]{1,0:T(8,128)(2,1)S(1)} %get-tuple-element.35), channel_id=1, source_target_pairs={{0,6},{2,4},{4,2},{6,0},{1,7},{3,5},{5,3},{7,1},{8,14},{10,12},{12... | collective-permute-start | bytes 196616 | tf_op jit(solution)/shard_map/ppermute | solution.py:24
  124.0 3.6 %collective-permute-done.19 = bf16[128,256]{1,0:T(8,128)(2,1)S(1)} collective-permute-done((bf16[128,256]{1,0:T(8,128)(2,1)S(1)}, bf16[128,256]{1,0:T(8,128)(2,1)S(1)}, u32[]{:S(2)}, u32[]{:S(2)}) %collective-permute-start.19) | collective-permute-done | bytes 65568 | tf_op jit(solution)/shard_map/ppermute | solution.py:24
  127.6 1.6 %add_convert_fusion = bf16[128,256]{1,0:T(8,128)(2,1)} fusion(bf16[128,256]{1,0:T(8,128)(2,1)S(1)} %collective-permute-done.20, bf16[128,256]{1,0:T(8,128)(2,1)S(1)} %collective-permute-done.19, bf16[128,256]{1,0:T(8,128)(2,1)S(1)} %collective-permute-done.18, f32[128,1024]{1,0:T(8,128)S(1)} %slice.75, s32[]{:T(128)S(6)} %select_n.193, ...), kind=kLoop, calls=%fused_computation.8 | loop fusion | flops 425984 | bytes 589840 | tf_op jit(solution)/shard_map/convert_element_type | solution.py:291
  (102 shorter events, 26.9 us)
Async XLA Ops:
  0.6 13.8 %collective-permute-start.1 = (bf16[128,256]{1,0:T(8,128)(2,1)}, bf16[128,256]{1,0:T(8,128)(2,1)}, u32[]{:S(2)}, u32[]{:S(2)}) collective-permute-start(bf16[128,256]{1,0:T(8,128)(2,1)} %param.5), channel_id=1, source_target_pairs={{0,1},{1,0},{16,17},{17,16},{2,3},{3,2},{18,19},{19,18},{4,5},{5,4... | collective-permute-start | bytes 196616 | tf_op jit(solution)/shard_map/ppermute | solution.py:24
  3.7 11.8 %collective-permute-start.2 = (bf16[128,256]{1,0:T(8,128)(2,1)}, bf16[128,256]{1,0:T(8,128)(2,1)}, u32[]{:S(2)}, u32[]{:S(2)}) collective-permute-start(bf16[128,256]{1,0:T(8,128)(2,1)} %param.5), channel_id=1, source_target_pairs={{0,17},{1,16},{16,1},{17,0},{2,19},{3,18},{18,3},{19,2},{4,21},{5,... | collective-permute-start | bytes 196616 | tf_op jit(solution)/shard_map/ppermute | solution.py:24
  6.1 46.0 %collective-permute-start.8 = (bf16[256,1280]{1,0:T(8,128)(2,1)}, bf16[256,1280]{1,0:T(8,128)(2,1)}, u32[]{:S(2)}, u32[]{:S(2)}) collective-permute-start(bf16[256,1280]{1,0:T(8,128)(2,1)} %dynamic-slice_bitcast_fusion), channel_id=1, source_target_pairs={{0,1},{1,0},{16,17},{17,16},{2,3},{3,2},{18,19},{19,18},{4,5},{5,4... | collective-permute-start | bytes 1966088 | tf_op jit(solution)/shard_map/ppermute | solution.py:24
  8.5 43.0 %collective-permute-start.10 = (bf16[256,1280]{1,0:T(8,128)(2,1)}, bf16[256,1280]{1,0:T(8,128)(2,1)}, u32[]{:S(2)}, u32[]{:S(2)}) collective-permute-start(bf16[256,1280]{1,0:T(8,128)(2,1)} %constant_dynamic-slice_fusion.10), channel_id=1, source_target_pairs={{0,16},{1,17},{16,0},{17,1},{2,18},{3,19},{18,2},{19,3},{4,20},{5,... | collective-permute-start | bytes 1966088 | tf_op jit(solution)/shard_map/ppermute | solution.py:24
  9.9 41.6 %collective-permute-start.11 = (bf16[256,1280]{1,0:T(8,128)(2,1)}, bf16[256,1280]{1,0:T(8,128)(2,1)}, u32[]{:S(2)}, u32[]{:S(2)}) collective-permute-start(bf16[256,1280]{1,0:T(8,128)(2,1)} %constant_dynamic-slice_fusion.9), channel_id=1, source_target_pairs={{0,17},{1,16},{16,1},{17,0},{2,19},{3,18},{18,3},{19,2},{4,21},{5,... | collective-permute-start | bytes 1966088 | tf_op jit(solution)/shard_map/ppermute | solution.py:24
  14.5 25.3 %collective-permute-start = (bf16[128,256]{1,0:T(8,128)(2,1)S(1)}, bf16[128,256]{1,0:T(8,128)(2,1)S(1)}, u32[]{:S(2)}, u32[]{:S(2)}) collective-permute-start(bf16[128,256]{1,0:T(8,128)(2,1)S(1)} %copy-done.4), channel_id=1, source_target_pairs={{0,16},{1,17},{16,0},{17,1},{2,18},{3,19},{18,2},{19,3},{4,20},{5,... | collective-permute-start | bytes 196616 | tf_op jit(solution)/shard_map/ppermute | solution.py:24
  16.1 27.7 %collective-permute-start.6 = (f32[8,128]{1,0:T(8,128)S(1)}, f32[8,128]{1,0:T(8,128)S(1)}, u32[]{:S(2)}, u32[]{:S(2)}) collective-permute-start(f32[8,128]{1,0:T(8,128)S(1)} %broadcast_in_dim.25), channel_id=1, source_target_pairs={{0,8},{8,0},{1,9},{9,1},{2,10},{10,2},{3,11},{11,3},{4,12},{12,4},... | collective-permute-start | bytes 12296 | tf_op jit(solution)/shard_map/ppermute | solution.py:24
  42.1 6.8 %collective-permute-start.3 = (bf16[256,512]{1,0:T(8,128)(2,1)}, bf16[256,512]{1,0:T(8,128)(2,1)}, u32[]{:S(2)}, u32[]{:S(2)}) collective-permute-start(bf16[256,512]{1,0:T(8,128)(2,1)} %maximum_select_fusion.refs_1_), channel_id=1, source_target_pairs={{0,2},{2,0},{4,6},{6,4},{1,3},{3,1},{5,7},{7,5},{8,10},{10,8},{12,... | collective-permute-start | bytes 786440 | tf_op jit(solution)/shard_map/ppermute | solution.py:24
  43.7 29.2 %collective-permute-start.7 = (bf16[256,1280]{1,0:T(8,128)(2,1)}, bf16[256,1280]{1,0:T(8,128)(2,1)}, u32[]{:S(2)}, u32[]{:S(2)}) collective-permute-start(bf16[256,1280]{1,0:T(8,128)(2,1)} %constant_dynamic-slice_fusion.8.refs_6_), channel_id=1, source_target_pairs={{0,8},{8,0},{1,9},{9,1},{2,10},{10,2},{3,11},{11,3},{4,12},{12,4},... | collective-permute-start | bytes 1966088 | tf_op jit(solution)/shard_map/ppermute | solution.py:24
  48.9 12.4 %collective-permute-start.4 = (bf16[256,512]{1,0:T(8,128)(2,1)}, bf16[256,512]{1,0:T(8,128)(2,1)}, u32[]{:S(2)}, u32[]{:S(2)}) collective-permute-start(bf16[256,512]{1,0:T(8,128)(2,1)} %maximum_select_fusion.refs_1_), channel_id=1, source_target_pairs={{0,4},{2,6},{4,0},{6,2},{1,5},{3,7},{5,1},{7,3},{8,12},{10,14},{12... | collective-permute-start | bytes 786440 | tf_op jit(solution)/shard_map/ppermute | solution.py:24
  51.5 21.4 %collective-permute-start.13 = (bf16[256,1280]{1,0:T(8,128)(2,1)}, bf16[256,1280]{1,0:T(8,128)(2,1)}, u32[]{:S(2)}, u32[]{:S(2)}) collective-permute-start(bf16[256,1280]{1,0:T(8,128)(2,1)} %collective-permute-done.11.refs_11_), channel_id=1, source_target_pairs={{0,8},{8,0},{1,9},{9,1},{2,10},{10,2},{3,11},{11,3},{4,12},{12,4},... | collective-permute-start | bytes 1966088 | tf_op jit(solution)/shard_map/ppermute | solution.py:24
  51.5 21.4 %collective-permute-start.12 = (bf16[256,1280]{1,0:T(8,128)(2,1)}, bf16[256,1280]{1,0:T(8,128)(2,1)}, u32[]{:S(2)}, u32[]{:S(2)}) collective-permute-start(bf16[256,1280]{1,0:T(8,128)(2,1)} %collective-permute-done.10.refs_10_), channel_id=1, source_target_pairs={{0,8},{8,0},{1,9},{9,1},{2,10},{10,2},{3,11},{11,3},{4,12},{12,4},... | collective-permute-start | bytes 1966088 | tf_op jit(solution)/shard_map/ppermute | solution.py:24
  52.0 20.9 %collective-permute-start.9 = (bf16[256,1280]{1,0:T(8,128)(2,1)}, bf16[256,1280]{1,0:T(8,128)(2,1)}, u32[]{:S(2)}, u32[]{:S(2)}) collective-permute-start(bf16[256,1280]{1,0:T(8,128)(2,1)} %collective-permute-done.8.refs_8_), channel_id=1, source_target_pairs={{0,8},{8,0},{1,9},{9,1},{2,10},{10,2},{3,11},{11,3},{4,12},{12,4},... | collective-permute-start | bytes 1966088 | tf_op jit(solution)/shard_map/ppermute | solution.py:24
  61.3 9.5 %collective-permute-start.5 = (bf16[256,512]{1,0:T(8,128)(2,1)}, bf16[256,512]{1,0:T(8,128)(2,1)S(1)}, u32[]{:S(2)}, u32[]{:S(2)}) collective-permute-start(bf16[256,512]{1,0:T(8,128)(2,1)} %maximum_select_fusion.refs_1_), channel_id=1, source_target_pairs={{0,6},{2,4},{4,2},{6,0},{1,7},{3,5},{5,3},{7,1},{8,14},{10,12},{12... | collective-permute-start | bytes 786440 | tf_op jit(solution)/shard_map/ppermute | solution.py:24
  70.8 23.5 %collective-permute-start.14 = (bf16[128,1280]{1,0:T(8,128)(2,1)}, bf16[128,1280]{1,0:T(8,128)(2,1)S(1)}, u32[]{:S(2)}, u32[]{:S(2)}) collective-permute-start(bf16[128,1280]{1,0:T(8,128)(2,1)} %get-tuple-element.37), channel_id=1, source_target_pairs={{0,16},{16,0},{1,17},{17,1},{2,18},{18,2},{3,19},{19,3},{4,20},{20... | collective-permute-start | bytes 983048 | tf_op jit(solution)/shard_map/ppermute | solution.py:24
  80.6 13.5 %all-to-all-start = ((f32[16,8,128]{2,1,0:T(8,128)}), f32[16,8,128]{2,1,0:T(8,128)S(1)}, u32[]{:S(2)}, u32[]{:S(2)}) async-start(f32[16,8,128]{2,1,0:T(8,128)} %get-tuple-element.20), calls=%async_computation | async-start | bytes 131072 | tf_op jit(solution)/shard_map/all_to_all | solution.py:28
  100.0 10.0 %collective-permute-start.15 = (bf16[128,1024]{1,0:T(8,128)(2,1)}, bf16[128,1024]{1,0:T(8,128)(2,1)}, u32[]{:S(2)}, u32[]{:S(2)}) collective-permute-start(bf16[128,1024]{1,0:T(8,128)(2,1)} %get-tuple-element.39), channel_id=1, source_target_pairs={{0,1},{1,0},{16,17},{17,16},{2,3},{3,2},{18,19},{19,18},{4,5},{5,4... | collective-permute-start | bytes 786440 | tf_op jit(solution)/shard_map/ppermute | solution.py:24
  100.8 11.1 %collective-permute-start.17 = (bf16[128,1024]{1,0:T(8,128)(2,1)}, bf16[128,1024]{1,0:T(8,128)(2,1)}, u32[]{:S(2)}, u32[]{:S(2)}) collective-permute-start(bf16[128,1024]{1,0:T(8,128)(2,1)} %get-tuple-element.40), channel_id=1, source_target_pairs={{0,17},{1,16},{16,1},{17,0},{2,19},{3,18},{18,3},{19,2},{4,21},{5,... | collective-permute-start | bytes 786440 | tf_op jit(solution)/shard_map/ppermute | solution.py:24
  102.1 11.2 %collective-permute-start.16 = (bf16[128,1024]{1,0:T(8,128)(2,1)}, bf16[128,1024]{1,0:T(8,128)(2,1)}, u32[]{:S(2)}, u32[]{:S(2)}) collective-permute-start(bf16[128,1024]{1,0:T(8,128)(2,1)} %slice.96), channel_id=1, source_target_pairs={{0,16},{1,17},{16,0},{17,1},{2,18},{3,19},{18,2},{19,3},{4,20},{5,... | collective-permute-start | bytes 786440 | tf_op jit(solution)/shard_map/ppermute | solution.py:24
  106.5 10.9 %all-to-all-start.1 = ((f32[16,3,128]{2,1,0:T(4,128)}), f32[16,3,128]{2,1,0:T(4,128)S(1)}, u32[]{:S(2)}, u32[]{:S(2)}) async-start(f32[16,3,128]{2,1,0:T(4,128)} %bitcast.36), calls=%async_computation.1 | async-start | bytes 65536 | tf_op jit(solution)/shard_map/all_to_all | solution.py:28
  117.9 4.9 %collective-permute-start.21 = (f32[8,128]{1,0:T(8,128)S(1)}, f32[8,128]{1,0:T(8,128)S(1)}, u32[]{:S(2)}, u32[]{:S(2)}) collective-permute-start(f32[8,128]{1,0:T(8,128)S(1)} %broadcast_in_dim.28), channel_id=1, source_target_pairs={{0,8},{8,0},{1,9},{9,1},{2,10},{10,2},{3,11},{11,3},{4,12},{12,4},... | collective-permute-start | bytes 12296 | tf_op jit(solution)/shard_map/ppermute | solution.py:24
  118.4 5.6 %collective-permute-start.18 = (bf16[128,256]{1,0:T(8,128)(2,1)S(1)}, bf16[128,256]{1,0:T(8,128)(2,1)S(1)}, u32[]{:S(2)}, u32[]{:S(2)}) collective-permute-start(bf16[128,256]{1,0:T(8,128)(2,1)S(1)} %get-tuple-element.34), channel_id=1, source_target_pairs={{0,2},{2,0},{4,6},{6,4},{1,3},{3,1},{5,7},{7,5},{8,10},{10,8},{12,... | collective-permute-start | bytes 196616 | tf_op jit(solution)/shard_map/ppermute | solution.py:24
  119.0 8.6 %collective-permute-start.19 = (bf16[128,256]{1,0:T(8,128)(2,1)S(1)}, bf16[128,256]{1,0:T(8,128)(2,1)S(1)}, u32[]{:S(2)}, u32[]{:S(2)}) collective-permute-start(bf16[128,256]{1,0:T(8,128)(2,1)S(1)} %get-tuple-element.36), channel_id=1, source_target_pairs={{0,4},{2,6},{4,0},{6,2},{1,5},{3,7},{5,1},{7,3},{8,12},{10,14},{12... | collective-permute-start | bytes 196616 | tf_op jit(solution)/shard_map/ppermute | solution.py:24
  119.7 7.9 %collective-permute-start.20 = (bf16[128,256]{1,0:T(8,128)(2,1)S(1)}, bf16[128,256]{1,0:T(8,128)(2,1)S(1)}, u32[]{:S(2)}, u32[]{:S(2)}) collective-permute-start(bf16[128,256]{1,0:T(8,128)(2,1)S(1)} %get-tuple-element.35), channel_id=1, source_target_pairs={{0,6},{2,4},{4,2},{6,0},{1,7},{3,5},{5,3},{7,1},{8,14},{10,12},{12... | collective-permute-start | bytes 196616 | tf_op jit(solution)/shard_map/ppermute | solution.py:24
  (9 other events, 56.2 us)

commit v5 on v4

--- a/solution.py
+++ b/solution.py
@@ -33,10 +33,55 @@
 ANYWHERE = pl.BlockSpec(memory_space=pltpu.HBM)
 
 
-def forward_kernel(places, slabs, *refs):
+def placed(scalars, k, source, near, far, place, sem):
+    for side, weight in enumerate((near, far)):
+
+        @pl.when(scalars[4 + 3 * k] == side)
+        def _(weight=weight):
+            pltpu.make_async_copy(source, weight.at[place], sem).start()
+
+
+def stage_kernel(places, scalars, *refs):
+    count = len(places)
+    blocks, (near, far, held, sems, out_sems) = refs[:count], refs[count:]
+    copies = [
+        pltpu.make_async_copy(block, held.at[k], sems.at[k]) for k, block in enumerate(blocks)
+    ]
+    for copy in copies:
+        copy.start()
+    for k, copy in enumerate(copies):
+        copy.wait()
+        placed(scalars, k, held.at[k], near, far, places[k], out_sems.at[k])
+    for k in range(count):
+        pltpu.make_async_copy(held.at[k], near.at[0], out_sems.at[k]).wait()
+
+
+def staged(scalars, blocks, places, total):
+    rows, width = blocks[0].shape
+    kind, count = blocks[0].dtype, len(blocks)
+    return pl.pallas_call(
+        functools.partial(stage_kernel, places),
+        out_shape=[jax.ShapeDtypeStruct((total // 2, rows, width), kind)] * 2,
+        in_specs=[SMEM] + [ANYWHERE] * count,
+        out_specs=[ANYWHERE] * 2,
+        scratch_shapes=[
+            pltpu.VMEM((count, rows, width), kind),
+            pltpu.SemaphoreType.DMA((count,)),
+            pltpu.SemaphoreType.DMA((count,)),
+        ],
+        compiler_params=pltpu.CompilerParams(vmem_limit_bytes=64_600_000),
+        cost_estimate=pl.CostEstimate(
+            flops=2 * count * rows * width,
+            bytes_accessed=4 * count * rows * width,
+            transcendentals=0,
+        ),
+    )(scalars, *blocks)
+
+
+def forward_kernel(places, slabs, bound, early, *refs):
     count = len(places)
     scalars, hidden, own_parts = refs[0], refs[1 : 1 + slabs], refs[1 + slabs]
-    blocks, refs = refs[2 + slabs : 2 + slabs + count], refs[2 + slabs + count :]
+    blocks, refs = refs[2 + slabs : 2 + slabs + count], refs[4 + slabs + count :]
     result, near, far, sent, held, pairs, logits, parts, sems, pair_sems, out_sems, last_sem = refs
     copies = [
         pltpu.make_async_copy(block, held.at[k], sems.at[k]) for k, block in enumerate(blocks)
@@ -58,22 +103,19 @@
             even = scalars[3 + 3 * k] == 0
             lhs.append(jnp.where(even, pairs[k, :, :rows], pairs[k, :, rows:]))
             copies[k].wait()
-            for side, weight in enumerate((near, far)):
-
-                @pl.when(scalars[4 + 3 * k] == side)
-                def _(k=k, weight=weight):
-                    place = places[k]
-                    pltpu.make_async_copy(held.at[k], weight.at[place], out_sems.at[k]).start()
-
         rhs = held[begin : begin + chunk].reshape(chunk * rows, width)
         term = jnp.dot(jnp.concatenate(lhs, axis=1), rhs, preferred_element_type=jnp.float32)
         logits[...] = logits[...] + term if begin else term
+    for k in range(early, count):
+        placed(scalars, k, held.at[k], near, far, places[k], out_sems.at[k])
     leaving = pltpu.make_async_copy(logits, result, last_sem)
     leaving.start()
-    values = logits[...]
-    mine = lax.broadcasted_iota(jnp.int32, values.shape, 1) >= scalars[0]
-    top = jnp.max(jnp.where(mine, values, -3e38), axis=1, keepdims=True)
-    total = jnp.sum(jnp.where(mine, jnp.exp(values - top), 0.0), axis=1, keepdims=True)
+    values, edge = logits[:, bound:], logits[:, :bound]
+    mine = lax.broadcasted_iota(jnp.int32, edge.shape, 1) >= scalars[0]
+    edge_top = jnp.max(jnp.where(mine, edge, -3e38), axis=1, keepdims=True)
+    top = jnp.maximum(jnp.max(values, axis=1, keepdims=True), edge_top)
+    total = jnp.sum(jnp.exp(values - top), axis=1, keepdims=True)
+    total += jnp.sum(jnp.where(mine, jnp.exp(edge - top), 0.0), axis=1, keepdims=True)
     lane = lax.broadcasted_iota(jnp.int32, (values.shape[0], LANES), 1)
     packed = jnp.where(lane == 0, top, jnp.where(lane == 1, total, 0.0))
     parts[...] = packed.T[:8]
@@ -86,25 +128,25 @@
     own = own_parts[...]
     sent[:, 2 * groups :, :] = jnp.broadcast_to(own, (sent.shape[0],) + own.shape)
     leaving.wait()
-    for k in range(count):
+    for k in range(early, count):
         pltpu.make_async_copy(held.at[k], near.at[0], out_sems.at[k]).wait()
 
 
-def forward(scalars, hidden, blocks, places, own_parts, receivers):
+def forward(scalars, hidden, blocks, places, bound, early, weights, own_parts, receivers):
     height = hidden[0].shape[0]
     rows, width = blocks[0].shape
     count, slabs = len(blocks), len(hidden)
     extra, tokens = own_parts.shape
     kind = blocks[0].dtype
     return pl.pallas_call(
-        functools.partial(forward_kernel, places, slabs),
+        functools.partial(forward_kernel, places, slabs, bound, early),
         out_shape=[
             jax.ShapeDtypeStruct((height, width), jnp.float32),
             jax.ShapeDtypeStruct((count // 2, rows, width), kind),
             jax.ShapeDtypeStruct((count // 2, rows, width), kind),
             jax.ShapeDtypeStruct((receivers, 2 * height // tokens + extra, tokens), jnp.float32),
         ],
-        in_specs=[SMEM] + [ANYWHERE] * slabs + [VMEM] + [ANYWHERE] * count,
+        in_specs=[SMEM] + [ANYWHERE] * slabs + [VMEM] + [ANYWHERE] * (count + 2),
         out_specs=[ANYWHERE, ANYWHERE, ANYWHERE, VMEM],
         scratch_shapes=[
             pltpu.VMEM((count, rows, width), kind),
@@ -116,18 +158,20 @@
             pltpu.SemaphoreType.DMA((count,)),
             pltpu.SemaphoreType.DMA,
         ],
-        compiler_params=pltpu.CompilerParams(vmem_limit_bytes=62_300_000),
+        input_output_aliases={2 + slabs + count: 1, 3 + slabs + count: 2},
+        compiler_params=pltpu.CompilerParams(vmem_limit_bytes=64_600_000),
         cost_estimate=pl.CostEstimate(
             flops=2 * count * height * rows * width,
             bytes_accessed=4 * count * rows * width,
             transcendentals=0,
         ),
-    )(scalars, *hidden, own_parts, *blocks)
+    )(scalars, *hidden, own_parts, *blocks, *weights)
 
 
 def on_device(student_hidden, student_blocks, teacher_logits, token_ids, loss_mask):
     row_g, core, slab, half = (lax.axis_index(axis) for axis in ("g", "c", "s", "h"))
     n_g, n_s = lax.axis_size("g"), lax.axis_size("s")
+    n_blocks = 4 * n_g
     tokens, _ = student_hidden.shape
     piece = student_blocks[0]
     rows = piece.shape[0]
@@ -140,7 +184,7 @@
         return (g * (tiles - wide_tiles)) // max(n_g - 1, 1) * LANES
 
     plane = [(mg, mh) for mh in range(2) for mg in range(n_g)]
-    others = sorted(plane[1:], key=lambda m: (m[0].bit_count() + m[1], m))
+    others = others_of(n_g)
 
     hidden_plane = {(0, 0): student_hidden}
     for mg, mh in others:
@@ -150,9 +194,10 @@
         return lax.dynamic_slice_in_dim(piece, h * vt + offset(g), width, 1)
 
     blocks = {}
-    for mg, mh in others:
+    for k, (mg, mh) in enumerate(others):
         cut = columns_of(row_g ^ mg, half ^ mh)
-        piece, _ = lax.optimization_barrier((piece, cut))
+        if k:
+            piece, _ = lax.optimization_barrier((piece, cut))
         blocks[mg, mh, 0] = exchanged(cut, g=mg, h=mh)
     blocks[0, 0, 0] = columns_of(row_g, half)
     for mg, mh in [(0, 0)] + others:
@@ -175,6 +220,8 @@
         exchanged(teacher_of(row_g ^ mg), g=mg) for mg in range(1, n_g)
     ]
 
+    student_hidden, _ = lax.optimization_barrier((student_hidden, hidden_plane[others[-1]]))
+    hidden_plane[0, 0] = student_hidden
     sides = [jnp.concatenate([hidden_plane[mg, mh] for mg in range(n_g)]) for mh in range(2)]
     plane_hidden = jnp.where(
         half == 0, jnp.concatenate(sides, axis=1), jnp.concatenate(sides[::-1], axis=1)
@@ -195,9 +242,13 @@
     for mg, mh, mc in keys:
         values += [slab ^ ((half ^ mh) * n_g + (row_g ^ mg)), core ^ mc, crossed ^ mc]
     places = [plane.index((mg, mh)) for mg, mh, _ in keys]
+    bound = max([offset(g - 1) + width - offset(g) for g in range(1, n_g)] + [LANES])
     scalars = jnp.stack(values).astype(jnp.int32)
     chosen = [blocks[key] for key in keys]
-    logits, *weights, sent = forward(scalars, gathered, chosen, places, own_parts, 2 * n_s * n_g)
+    weights = staged(scalars, chosen[:4], places[:4], n_blocks)
+    logits, *weights, sent = forward(
+        scalars, gathered, chosen, places, bound, 4, weights, own_parts, 2 * n_s * n_g
+    )
 
     def by_group(stack):
         parts = stack.reshape(stack.shape[0], n_g, tokens)
@@ -247,8 +298,7 @@
             preferred_element_type=jnp.float32,
         )
 
-    far = features_of(1)
-    grads = (features_of(0), far)
+    grads = (features_of(0), features_of(1))
 
     def for_half(mg, mh):
         return grads[mh][mg * tokens : (mg + 1) * tokens]
@@ -277,8 +327,8 @@
             total = total + block.astype(jnp.float32)
         return total
 
+    slab_terms = [for_slab(slab ^ ms).astype(jnp.bfloat16) for ms in range(1, n_s)]
     result = for_slab(slab)
-    slab_terms = [for_slab(slab ^ ms).astype(jnp.bfloat16) for ms in range(1, n_s)]
     slab_parts = [exchanged(term, s=ms) for ms, term in enumerate(slab_terms, 1)]
     every, _ = lax.optimization_barrier((every, slab_terms))
     token_kl, picked, core_loss = jnp.sum(every, axis=0)
@@ -289,6 +339,11 @@
     for part in slab_parts:
         result = result + part.astype(jnp.float32)
     return (result.astype(jnp.bfloat16), token_kl, sampled, loss)
+
+
+def others_of(n_g):
+    masks = [(mg, mh) for mh in range(2) for mg in range(n_g)][1:]
+    return sorted(masks, key=lambda m: (m[0].bit_count() + m[1], m))
 
 
 def solution(mesh):

time: 131 us -> 131 us (level)
  other arithmetic: 11.3 us -> 7.95 us
  Pallas kernels: 7.69 us -> 10.3 us
  starting transfers between devices: 36 us -> 37.4 us
    pallas_call x1 -> x2, Pallas kernels: 7.69 us -> 10.3 us  [the longest x1 6.93 us: forward(): pl.pallas_call(functools.partial(forward_kernel, places, slabs, bound, ea...]
    all_to_all x2, waiting for transfers between devices: 10.1 us -> 12.5 us  [from_every(): return lax.all_to_all(array, axes, 0, 0, tiled=True)]
    dynamic_slice x4 -> x3, local copies, waits for them, and re-layouts: 3.64 us -> 5.63 us  [columns_of(): return lax.dynamic_slice_in_dim(piece, h * vt + offset(g), width, 1)]
    all_to_all x2, starting transfers between devices: 9.45 us -> 11.4 us  [from_every(): return lax.all_to_all(array, axes, 0, 0, tiled=True)]
    ppermute x22, waiting for transfers between devices: 46.7 us -> 44.8 us  [exchanged(): return lax.ppermute(array, axes, pairs)]
    select_n x1, other arithmetic: 1.76 us -> 0.12 us  [on_device(): jnp.where(half == 0, jnp.concatenate(sides, axis=1), jnp.concatenate(side...]
    slice x3, local copies, waits for them, and re-layouts: 1.61 us -> 0.1 us  [for_half(): return grads[mh][mg * tokens:(mg + 1) * tokens]]
    concatenate x2, local copies, waits for them, and re-layouts: 1.47 us -> 0.01 us  [on_device(): jnp.concatenate([hidden_plane[mg, mh] for mg in range(n_g)])]
  transfers between devices with their start and end apart: 24 -> 24, of which waited for: 9 -> 10; matrix products, arithmetic and copies ran while one was open for 14% -> 9% of each run, Pallas kernels for 6% -> 8%
where the time goes in v5:
time: 131 us; the launch traced here: 130 us
  waiting for transfers between devices  57.3 us (44%)
  starting transfers between devices  37.4 us (29%)
  local copies, waits for them, and re-layouts  11.9 us (9%)
  Pallas kernels  10.3 us (8%)
  other arithmetic  7.95 us (6%)
  between operations  3.8 us (3%)
  matrix products  1.74 us (1%)
    ppermute x22, waiting for transfers between devices, exchanged(): return lax.ppermute(array, axes, pairs)  44.8 us
    ppermute x22, starting transfers between devices, exchanged(): return lax.ppermute(array, axes, pairs)  26 us
    all_to_all x2, waiting for transfers between devices, from_every(): return lax.all_to_all(array, axes, 0, 0, tiled=True)  12.5 us
    all_to_all x2, starting transfers between devices, from_every(): return lax.all_to_all(array, axes, 0, 0, tiled=True)  11.4 us
    pallas_call x1, Pallas kernels, forward(): pl.pallas_call(functools.partial(forward_kernel, places, slabs, bound, ea...  6.93 us
    dynamic_slice x3, local copies, waits for them, and re-layouts, columns_of(): return lax.dynamic_slice_in_dim(piece, h * vt + offset(g), width, 1)  5.63 us
    pallas_call x1, Pallas kernels, staged(): pl.pallas_call(functools.partial(stage_kernel, places), out_shape=[jax.Sh...  3.37 us
  transfers between devices with their start and end apart: 24, of which 10 were waited for; matrix products, arithmetic and copies ran while one was open for 9% of the time, Pallas kernels for 8%

profile of v5, /device:TPU:0, one launch (start us, length us, event | category | flops | bytes accessed | tf_op | source)
XLA Modules:
  0.0 130.3 jit_solution(17126222879967763864)
XLA Ops:
  0.7 2.4 %dynamic-slice_bitcast_fusion = (bf16[256,1280]{1,0:T(8,128)(2,1)}, bf16[256,1280]{1,0:T(8,128)(2,1)}) fusion(bf16[1,256,4864]{2,1,0:T(8,128)(2,1)} %param.6, s32[]{:T(128)S(6)} %select_n.185, s32[]{:T(128)S(6)} %select_n.182), kind=kLoop, calls=%fused_computation.5 | loop fusion | bytes 2621448 | tf_op jit(solution)/shard_map/dynamic_slice | solution.py:194
  3.1 3.0 %collective-permute-start.10 = (bf16[256,1280]{1,0:T(8,128)(2,1)}, bf16[256,1280]{1,0:T(8,128)(2,1)}, u32[]{:S(2)}, u32[]{:S(2)}) collective-permute-start(bf16[256,1280]{1,0:T(8,128)(2,1)} %get-tuple-element.39), channel_id=1, source_target_pairs={{0,16},{1,17},{16,0},{17,1},{2,18},{3,19},{18,2},{19,3},{4,20},{5,... | collective-permute-start | bytes 1966088 | tf_op jit(solution)/shard_map/ppermute | solution.py:24
  6.1 2.0 %constant_dynamic-slice_fusion.9 = bf16[256,1280]{1,0:T(8,128)(2,1)} fusion(bf16[256,4864]{1,0:T(8,128)(2,1)} %bitcast.85, s32[]{:T(128)S(6)} %select_n.183), kind=kLoop, calls=%fused_computation.47 | loop fusion | bytes 1310724 | tf_op jit(solution)/shard_map/dynamic_slice | solution.py:194
  8.1 1.4 %collective-permute-start.11 = (bf16[256,1280]{1,0:T(8,128)(2,1)}, bf16[256,1280]{1,0:T(8,128)(2,1)}, u32[]{:S(2)}, u32[]{:S(2)}) collective-permute-start(bf16[256,1280]{1,0:T(8,128)(2,1)} %constant_dynamic-slice_fusion.9), channel_id=1, source_target_pairs={{0,17},{1,16},{16,1},{17,0},{2,19},{3,18},{18,3},{19,2},{4,21},{5,... | collective-permute-start | bytes 1966088 | tf_op jit(solution)/shard_map/ppermute | solution.py:24
  14.1 2.7 %collective-permute-start = (bf16[128,256]{1,0:T(8,128)(2,1)S(1)}, bf16[128,256]{1,0:T(8,128)(2,1)S(1)}, u32[]{:S(2)}, u32[]{:S(2)}) collective-permute-start(bf16[128,256]{1,0:T(8,128)(2,1)S(1)} %copy-done.9), channel_id=1, source_target_pairs={{0,17},{1,16},{16,1},{17,0},{2,19},{3,18},{18,3},{19,2},{4,21},{5,... | collective-permute-start | bytes 196616 | tf_op jit(solution)/shard_map/ppermute | solution.py:24
  16.8 22.3 %collective-permute-done.8.refs_2_.refs_8_ = bf16[256,1280]{1,0:T(8,128)(2,1)S(1)} collective-permute-done((bf16[256,1280]{1,0:T(8,128)(2,1)}, bf16[256,1280]{1,0:T(8,128)(2,1)S(1)}, u32[]{:S(2)}, u32[]{:S(2)}) %collective-permute-start.8) | collective-permute-done | bytes 655392 | tf_op jit(solution)/shard_map/ppermute | solution.py:24
  41.0 1.7 %collective-permute-start.2 = (bf16[128,256]{1,0:T(8,128)(2,1)S(1)}, bf16[128,256]{1,0:T(8,128)(2,1)S(1)}, u32[]{:S(2)}, u32[]{:S(2)}) collective-permute-start(bf16[128,256]{1,0:T(8,128)(2,1)S(1)} %copy-done.9), channel_id=1, source_target_pairs={{0,1},{1,0},{16,17},{17,16},{2,3},{3,2},{18,19},{19,18},{4,5},{5,4... | collective-permute-start | bytes 196616 | tf_op jit(solution)/shard_map/ppermute | solution.py:24
  42.7 2.8 %collective-permute-done.2 = bf16[128,256]{1,0:T(8,128)(2,1)S(1)} collective-permute-done((bf16[128,256]{1,0:T(8,128)(2,1)S(1)}, bf16[128,256]{1,0:T(8,128)(2,1)S(1)}, u32[]{:S(2)}, u32[]{:S(2)}) %collective-permute-start.2) | collective-permute-done | bytes 65568 | tf_op jit(solution)/shard_map/ppermute | solution.py:24
  45.5 1.7 %collective-permute-start.1 = (bf16[128,256]{1,0:T(8,128)(2,1)S(1)}, bf16[128,256]{1,0:T(8,128)(2,1)S(1)}, u32[]{:S(2)}, u32[]{:S(2)}) collective-permute-start(bf16[128,256]{1,0:T(8,128)(2,1)S(1)} %copy-done.9), channel_id=1, source_target_pairs={{0,16},{1,17},{16,0},{17,1},{2,18},{3,19},{18,2},{19,3},{4,20},{5,... | collective-permute-start | bytes 196616 | tf_op jit(solution)/shard_map/ppermute | solution.py:24
  47.8 2.0 %collective-permute-done.1 = bf16[128,256]{1,0:T(8,128)(2,1)S(1)} collective-permute-done((bf16[128,256]{1,0:T(8,128)(2,1)S(1)}, bf16[128,256]{1,0:T(8,128)(2,1)S(1)}, u32[]{:S(2)}, u32[]{:S(2)}) %collective-permute-start.1) | collective-permute-done | bytes 65568 | tf_op jit(solution)/shard_map/ppermute | solution.py:24
  49.9 1.8 %collective-permute-start.3 = (bf16[256,512]{1,0:T(8,128)(2,1)S(1)}, bf16[256,512]{1,0:T(8,128)(2,1)}, u32[]{:S(2)}, u32[]{:S(2)}) collective-permute-start(bf16[256,512]{1,0:T(8,128)(2,1)S(1)} %maximum_select_fusion.refs_1_), channel_id=1, source_target_pairs={{0,2},{2,0},{4,6},{6,4},{1,3},{3,1},{5,7},{7,5},{8,10},{10,8},{12,... | collective-permute-start | bytes 786440 | tf_op jit(solution)/shard_map/ppermute | solution.py:24
  51.8 2.6 %collective-permute-start.4 = (bf16[256,512]{1,0:T(8,128)(2,1)S(1)}, bf16[256,512]{1,0:T(8,128)(2,1)}, u32[]{:S(2)}, u32[]{:S(2)}) collective-permute-start(bf16[256,512]{1,0:T(8,128)(2,1)S(1)} %maximum_select_fusion.refs_1_), channel_id=1, source_target_pairs={{0,4},{2,6},{4,0},{6,2},{1,5},{3,7},{5,1},{7,3},{8,12},{10,14},{12... | collective-permute-start | bytes 786440 | tf_op jit(solution)/shard_map/ppermute | solution.py:24
  55.9 3.4 %shard_map.84 = (bf16[4,256,1280]{2,1,0:T(8,128)(2,1)}, bf16[4,256,1280]{2,1,0:T(8,128)(2,1)}) custom-call(s32[26]{0:T(128)} %stack.90.scalars.refs_0_, bf16[256,1280]{1,0:T(8,128)(2,1)} %copy-done, bf16[256,1280]{1,0:T(8,128)(2,1)} %copy-done.3, bf16[256,1280]{1,0:T(8,128)(2,1)} %copy-done.4, bf16[256,1280]{1,0:T(8,128)(2,1)} %copy-done.5), custom_call_target="tpu_custom_call" | custom-call | flops 2621440 | bytes 5242880 | tf_op jit(solution)/shard_map/pallas_call | solution.py:62
  59.3 1.5 %collective-permute-done.3.refs_2_ = bf16[256,512]{1,0:T(8,128)(2,1)} collective-permute-done((bf16[256,512]{1,0:T(8,128)(2,1)S(1)}, bf16[256,512]{1,0:T(8,128)(2,1)}, u32[]{:S(2)}, u32[]{:S(2)}) %collective-permute-start.3) | collective-permute-done | bytes 262176 | tf_op jit(solution)/shard_map/ppermute | solution.py:24
  60.8 1.7 %collective-permute-start.14 = (bf16[128,1280]{1,0:T(8,128)(2,1)S(1)}, bf16[128,1280]{1,0:T(8,128)(2,1)S(1)}, u32[]{:S(2)}, u32[]{:S(2)}) collective-permute-start(bf16[128,1280]{1,0:T(8,128)(2,1)S(1)} %get-tuple-element.43), channel_id=1, source_target_pairs={{0,16},{16,0},{1,17},{17,1},{2,18},{18,2},{3,19},{19,3},{4,20},{20... | collective-permute-start | bytes 983048 | tf_op jit(solution)/shard_map/ppermute | solution.py:24
  62.6 10.6 %collective-permute-done.4.refs_3_ = bf16[256,512]{1,0:T(8,128)(2,1)} collective-permute-done((bf16[256,512]{1,0:T(8,128)(2,1)S(1)}, bf16[256,512]{1,0:T(8,128)(2,1)}, u32[]{:S(2)}, u32[]{:S(2)}) %collective-permute-start.4) | collective-permute-done | bytes 262176 | tf_op jit(solution)/shard_map/ppermute | solution.py:24
  73.2 6.9 %shard_map.85 = (f32[256,1280]{1,0:T(8,128)}, bf16[4,256,1280]{2,1,0:T(8,128)(2,1)}, bf16[4,256,1280]{2,1,0:T(8,128)(2,1)}, f32[16,8,128]{2,1,0:T(8,128)}) custom-call(s32[26]{0:T(128)} %stack.90.scalars.refs_0_, bf16[256,512]{1,0:T(8,128)(2,1)} %copy-done.8, ...), custom_call_target="tpu_custom_call", output_to_operand_aliasing={{1}: (14, {}), {2}: (15, {})} | custom-call | flops 1342177280 | bytes 10485760 | tf_op jit(solution)/shard_map/pallas_call | solution.py:141
  80.2 7.9 %all-to-all-start = ((f32[16,8,128]{2,1,0:T(8,128)}), f32[16,8,128]{2,1,0:T(8,128)S(1)}, u32[]{:S(2)}, u32[]{:S(2)}) async-start(f32[16,8,128]{2,1,0:T(8,128)} %get-tuple-element.24), calls=%async_computation | async-start | bytes 131072 | tf_op jit(solution)/shard_map/all_to_all | solution.py:28
  88.3 7.3 %all-to-all-done = f32[16,8,128]{2,1,0:T(8,128)S(1)} async-done(((f32[16,8,128]{2,1,0:T(8,128)}), f32[16,8,128]{2,1,0:T(8,128)S(1)}, u32[]{:S(2)}, u32[]{:S(2)}) %all-to-all-start) | async-done | bytes 65568 | tf_op jit(solution)/shard_map/all_to_all | solution.py:28
  95.8 2.2 %select_convert_fusion = bf16[256,1280]{1,0:T(8,128)(2,1)S(1)} fusion(f32[256,1280]{1,0:T(8,128)} %get-tuple-element.32, bf16[128,1280]{1,0:T(8,128)(2,1)S(1)} %collective-permute-done.14, bf16[128,1280]{1,0:T(8,128)(2,1)S(1)} %get-tuple-element.30, f32[256]{0:T(256)S(1)} %log.15, f32[256]{0:T(256)S(1)} %fusion.13, f32[256]{0:T(256)S(1)} %log.14, ...), kind=kLoop, calls=%fused_computation.2 | loop fusion | flops 3932160 | bytes 2627840 | tf_op jit(solution)/shard_map/convert_element_type | solution.py:289
  107.3 3.5 %all-to-all-start.1 = ((f32[16,3,128]{2,1,0:T(4,128)}), f32[16,3,128]{2,1,0:T(4,128)S(1)}, u32[]{:S(2)}, u32[]{:S(2)}) async-start(f32[16,3,128]{2,1,0:T(4,128)} %bitcast.37), calls=%async_computation.1 | async-start | bytes 65536 | tf_op jit(solution)/shard_map/all_to_all | solution.py:28
  112.9 5.2 %all-to-all-done.1 = f32[16,3,128]{2,1,0:T(4,128)S(1)} async-done(((f32[16,3,128]{2,1,0:T(4,128)}), f32[16,3,128]{2,1,0:T(4,128)S(1)}, u32[]{:S(2)}, u32[]{:S(2)}) %all-to-all-start.1) | async-done | bytes 24608 | tf_op jit(solution)/shard_map/all_to_all | solution.py:28
  120.5 3.1 %collective-permute-start.20 = (bf16[128,256]{1,0:T(8,128)(2,1)S(1)}, bf16[128,256]{1,0:T(8,128)(2,1)S(1)}, u32[]{:S(2)}, u32[]{:S(2)}) collective-permute-start(bf16[128,256]{1,0:T(8,128)(2,1)S(1)} %get-tuple-element.41), channel_id=1, source_target_pairs={{0,6},{2,4},{4,2},{6,0},{1,7},{3,5},{5,3},{7,1},{8,14},{10,12},{12... | collective-permute-start | bytes 196616 | tf_op jit(solution)/shard_map/ppermute | solution.py:24
  124.8 3.6 %collective-permute-done.19 = bf16[128,256]{1,0:T(8,128)(2,1)S(1)} collective-permute-done((bf16[128,256]{1,0:T(8,128)(2,1)S(1)}, bf16[128,256]{1,0:T(8,128)(2,1)S(1)}, u32[]{:S(2)}, u32[]{:S(2)}) %collective-permute-start.19) | collective-permute-done | bytes 65568 | tf_op jit(solution)/shard_map/ppermute | solution.py:24
  (108 shorter events, 23.0 us)
Async XLA Ops:
  3.1 44.2 %collective-permute-start.10 = (bf16[256,1280]{1,0:T(8,128)(2,1)}, bf16[256,1280]{1,0:T(8,128)(2,1)}, u32[]{:S(2)}, u32[]{:S(2)}) collective-permute-start(bf16[256,1280]{1,0:T(8,128)(2,1)} %get-tuple-element.39), channel_id=1, source_target_pairs={{0,16},{1,17},{16,0},{17,1},{2,18},{3,19},{18,2},{19,3},{4,20},{5,... | collective-permute-start | bytes 1966088 | tf_op jit(solution)/shard_map/ppermute | solution.py:24
  8.1 39.1 %collective-permute-start.11 = (bf16[256,1280]{1,0:T(8,128)(2,1)}, bf16[256,1280]{1,0:T(8,128)(2,1)}, u32[]{:S(2)}, u32[]{:S(2)}) collective-permute-start(bf16[256,1280]{1,0:T(8,128)(2,1)} %constant_dynamic-slice_fusion.9), channel_id=1, source_target_pairs={{0,17},{1,16},{16,1},{17,0},{2,19},{3,18},{18,3},{19,2},{4,21},{5,... | collective-permute-start | bytes 1966088 | tf_op jit(solution)/shard_map/ppermute | solution.py:24
  10.7 41.0 %collective-permute-start.7 = (bf16[256,1280]{1,0:T(8,128)(2,1)S(1)}, bf16[256,1280]{1,0:T(8,128)(2,1)S(1)}, u32[]{:S(2)}, u32[]{:S(2)}) collective-permute-start(bf16[256,1280]{1,0:T(8,128)(2,1)S(1)} %constant_dynamic-slice_fusion.8.refs_0_.refs_6_), channel_id=1, source_target_pairs={{0,8},{8,0},{1,9},{9,1},{2,10},{10,2},{3,11},{11,3},{4,12},{12,4},... | collective-permute-start | bytes 1966088 | tf_op jit(solution)/shard_map/ppermute | solution.py:24
  10.8 28.3 %collective-permute-start.8 = (bf16[256,1280]{1,0:T(8,128)(2,1)}, bf16[256,1280]{1,0:T(8,128)(2,1)S(1)}, u32[]{:S(2)}, u32[]{:S(2)}) collective-permute-start(bf16[256,1280]{1,0:T(8,128)(2,1)} %get-tuple-element.38), channel_id=1, source_target_pairs={{0,1},{1,0},{16,17},{17,16},{2,3},{3,2},{18,19},{19,18},{4,5},{5,4... | collective-permute-start | bytes 1966088 | tf_op jit(solution)/shard_map/ppermute | solution.py:24
  12.3 1.8 %collective-permute-start.6 = (f32[8,128]{1,0:T(8,128)S(1)}, f32[8,128]{1,0:T(8,128)S(1)}, u32[]{:S(2)}, u32[]{:S(2)}) collective-permute-start(f32[8,128]{1,0:T(8,128)S(1)} %broadcast_in_dim.25), channel_id=1, source_target_pairs={{0,8},{8,0},{1,9},{9,1},{2,10},{10,2},{3,11},{11,3},{4,12},{12,4},... | collective-permute-start | bytes 12296 | tf_op jit(solution)/shard_map/ppermute | solution.py:24
  14.1 26.8 %collective-permute-start = (bf16[128,256]{1,0:T(8,128)(2,1)S(1)}, bf16[128,256]{1,0:T(8,128)(2,1)S(1)}, u32[]{:S(2)}, u32[]{:S(2)}) collective-permute-start(bf16[128,256]{1,0:T(8,128)(2,1)S(1)} %copy-done.9), channel_id=1, source_target_pairs={{0,17},{1,16},{16,1},{17,0},{2,19},{3,18},{18,3},{19,2},{4,21},{5,... | collective-permute-start | bytes 196616 | tf_op jit(solution)/shard_map/ppermute | solution.py:24
  39.1 15.3 %collective-permute-start.9 = (bf16[256,1280]{1,0:T(8,128)(2,1)S(1)}, bf16[256,1280]{1,0:T(8,128)(2,1)S(1)}, u32[]{:S(2)}, u32[]{:S(2)}) collective-permute-start(bf16[256,1280]{1,0:T(8,128)(2,1)S(1)} %collective-permute-done.8.refs_2_.refs_8_), channel_id=1, source_target_pairs={{0,8},{8,0},{1,9},{9,1},{2,10},{10,2},{3,11},{11,3},{4,12},{12,4},... | collective-permute-start | bytes 1966088 | tf_op jit(solution)/shard_map/ppermute | solution.py:24
  41.0 4.6 %collective-permute-start.2 = (bf16[128,256]{1,0:T(8,128)(2,1)S(1)}, bf16[128,256]{1,0:T(8,128)(2,1)S(1)}, u32[]{:S(2)}, u32[]{:S(2)}) collective-permute-start(bf16[128,256]{1,0:T(8,128)(2,1)S(1)} %copy-done.9), channel_id=1, source_target_pairs={{0,1},{1,0},{16,17},{17,16},{2,3},{3,2},{18,19},{19,18},{4,5},{5,4... | collective-permute-start | bytes 196616 | tf_op jit(solution)/shard_map/ppermute | solution.py:24
  45.5 4.3 %collective-permute-start.1 = (bf16[128,256]{1,0:T(8,128)(2,1)S(1)}, bf16[128,256]{1,0:T(8,128)(2,1)S(1)}, u32[]{:S(2)}, u32[]{:S(2)}) collective-permute-start(bf16[128,256]{1,0:T(8,128)(2,1)S(1)} %copy-done.9), channel_id=1, source_target_pairs={{0,16},{1,17},{16,0},{17,1},{2,18},{3,19},{18,2},{19,3},{4,20},{5,... | collective-permute-start | bytes 196616 | tf_op jit(solution)/shard_map/ppermute | solution.py:24
  47.3 25.9 %collective-permute-start.13 = (bf16[256,1280]{1,0:T(8,128)(2,1)}, bf16[256,1280]{1,0:T(8,128)(2,1)}, u32[]{:S(2)}, u32[]{:S(2)}) collective-permute-start(bf16[256,1280]{1,0:T(8,128)(2,1)} %collective-permute-done.11.refs_11_), channel_id=1, source_target_pairs={{0,8},{8,0},{1,9},{9,1},{2,10},{10,2},{3,11},{11,3},{4,12},{12,4},... | collective-permute-start | bytes 1966088 | tf_op jit(solution)/shard_map/ppermute | solution.py:24
  47.3 25.9 %collective-permute-start.12 = (bf16[256,1280]{1,0:T(8,128)(2,1)}, bf16[256,1280]{1,0:T(8,128)(2,1)}, u32[]{:S(2)}, u32[]{:S(2)}) collective-permute-start(bf16[256,1280]{1,0:T(8,128)(2,1)} %collective-permute-done.10.refs_10_), channel_id=1, source_target_pairs={{0,8},{8,0},{1,9},{9,1},{2,10},{10,2},{3,11},{11,3},{4,12},{12,4},... | collective-permute-start | bytes 1966088 | tf_op jit(solution)/shard_map/ppermute | solution.py:24
  49.9 10.9 %collective-permute-start.3 = (bf16[256,512]{1,0:T(8,128)(2,1)S(1)}, bf16[256,512]{1,0:T(8,128)(2,1)}, u32[]{:S(2)}, u32[]{:S(2)}) collective-permute-start(bf16[256,512]{1,0:T(8,128)(2,1)S(1)} %maximum_select_fusion.refs_1_), channel_id=1, source_target_pairs={{0,2},{2,0},{4,6},{6,4},{1,3},{3,1},{5,7},{7,5},{8,10},{10,8},{12,... | collective-permute-start | bytes 786440 | tf_op jit(solution)/shard_map/ppermute | solution.py:24
  51.8 21.4 %collective-permute-start.4 = (bf16[256,512]{1,0:T(8,128)(2,1)S(1)}, bf16[256,512]{1,0:T(8,128)(2,1)}, u32[]{:S(2)}, u32[]{:S(2)}) collective-permute-start(bf16[256,512]{1,0:T(8,128)(2,1)S(1)} %maximum_select_fusion.refs_1_), channel_id=1, source_target_pairs={{0,4},{2,6},{4,0},{6,2},{1,5},{3,7},{5,1},{7,3},{8,12},{10,14},{12... | collective-permute-start | bytes 786440 | tf_op jit(solution)/shard_map/ppermute | solution.py:24
  55.2 18.0 %collective-permute-start.5 = (bf16[256,512]{1,0:T(8,128)(2,1)S(1)}, bf16[256,512]{1,0:T(8,128)(2,1)}, u32[]{:S(2)}, u32[]{:S(2)}) collective-permute-start(bf16[256,512]{1,0:T(8,128)(2,1)S(1)} %maximum_select_fusion.refs_1_), channel_id=1, source_target_pairs={{0,6},{2,4},{4,2},{6,0},{1,7},{3,5},{5,3},{7,1},{8,14},{10,12},{12... | collective-permute-start | bytes 786440 | tf_op jit(solution)/shard_map/ppermute | solution.py:24
  60.8 35.0 %collective-permute-start.14 = (bf16[128,1280]{1,0:T(8,128)(2,1)S(1)}, bf16[128,1280]{1,0:T(8,128)(2,1)S(1)}, u32[]{:S(2)}, u32[]{:S(2)}) collective-permute-start(bf16[128,1280]{1,0:T(8,128)(2,1)S(1)} %get-tuple-element.43), channel_id=1, source_target_pairs={{0,16},{16,0},{1,17},{17,1},{2,18},{18,2},{3,19},{19,3},{4,20},{20... | collective-permute-start | bytes 983048 | tf_op jit(solution)/shard_map/ppermute | solution.py:24
  80.2 15.4 %all-to-all-start = ((f32[16,8,128]{2,1,0:T(8,128)}), f32[16,8,128]{2,1,0:T(8,128)S(1)}, u32[]{:S(2)}, u32[]{:S(2)}) async-start(f32[16,8,128]{2,1,0:T(8,128)} %get-tuple-element.24), calls=%async_computation | async-start | bytes 131072 | tf_op jit(solution)/shard_map/all_to_all | solution.py:28
  100.7 10.1 %collective-permute-start.15 = (bf16[128,1024]{1,0:T(8,128)(2,1)S(1)}, bf16[128,1024]{1,0:T(8,128)(2,1)S(1)}, u32[]{:S(2)}, u32[]{:S(2)}) collective-permute-start(bf16[128,1024]{1,0:T(8,128)(2,1)S(1)} %get-tuple-element.45), channel_id=1, source_target_pairs={{0,1},{1,0},{16,17},{17,16},{2,3},{3,2},{18,19},{19,18},{4,5},{5,4... | collective-permute-start | bytes 786440 | tf_op jit(solution)/shard_map/ppermute | solution.py:24
  101.6 9.8 %collective-permute-start.17 = (bf16[128,1024]{1,0:T(8,128)(2,1)S(1)}, bf16[128,1024]{1,0:T(8,128)(2,1)S(1)}, u32[]{:S(2)}, u32[]{:S(2)}) collective-permute-start(bf16[128,1024]{1,0:T(8,128)(2,1)S(1)} %get-tuple-element.46), channel_id=1, source_target_pairs={{0,17},{1,16},{16,1},{17,0},{2,19},{3,18},{18,3},{19,2},{4,21},{5,... | collective-permute-start | bytes 786440 | tf_op jit(solution)/shard_map/ppermute | solution.py:24
  102.9 9.8 %collective-permute-start.16 = (bf16[128,1024]{1,0:T(8,128)(2,1)S(1)}, bf16[128,1024]{1,0:T(8,128)(2,1)S(1)}, u32[]{:S(2)}, u32[]{:S(2)}) collective-permute-start(bf16[128,1024]{1,0:T(8,128)(2,1)S(1)} %slice.96), channel_id=1, source_target_pairs={{0,16},{1,17},{16,0},{17,1},{2,18},{3,19},{18,2},{19,3},{4,20},{5,... | collective-permute-start | bytes 786440 | tf_op jit(solution)/shard_map/ppermute | solution.py:24
  107.3 10.9 %all-to-all-start.1 = ((f32[16,3,128]{2,1,0:T(4,128)}), f32[16,3,128]{2,1,0:T(4,128)S(1)}, u32[]{:S(2)}, u32[]{:S(2)}) async-start(f32[16,3,128]{2,1,0:T(4,128)} %bitcast.37), calls=%async_computation.1 | async-start | bytes 65536 | tf_op jit(solution)/shard_map/all_to_all | solution.py:28
  118.7 4.9 %collective-permute-start.21 = (f32[8,128]{1,0:T(8,128)S(1)}, f32[8,128]{1,0:T(8,128)S(1)}, u32[]{:S(2)}, u32[]{:S(2)}) collective-permute-start(f32[8,128]{1,0:T(8,128)S(1)} %broadcast_in_dim.28), channel_id=1, source_target_pairs={{0,8},{8,0},{1,9},{9,1},{2,10},{10,2},{3,11},{11,3},{4,12},{12,4},... | collective-permute-start | bytes 12296 | tf_op jit(solution)/shard_map/ppermute | solution.py:24
  119.2 5.6 %collective-permute-start.18 = (bf16[128,256]{1,0:T(8,128)(2,1)S(1)}, bf16[128,256]{1,0:T(8,128)(2,1)S(1)}, u32[]{:S(2)}, u32[]{:S(2)}) collective-permute-start(bf16[128,256]{1,0:T(8,128)(2,1)S(1)} %get-tuple-element.40), channel_id=1, source_target_pairs={{0,2},{2,0},{4,6},{6,4},{1,3},{3,1},{5,7},{7,5},{8,10},{10,8},{12,... | collective-permute-start | bytes 196616 | tf_op jit(solution)/shard_map/ppermute | solution.py:24
  119.8 8.6 %collective-permute-start.19 = (bf16[128,256]{1,0:T(8,128)(2,1)S(1)}, bf16[128,256]{1,0:T(8,128)(2,1)S(1)}, u32[]{:S(2)}, u32[]{:S(2)}) collective-permute-start(bf16[128,256]{1,0:T(8,128)(2,1)S(1)} %get-tuple-element.42), channel_id=1, source_target_pairs={{0,4},{2,6},{4,0},{6,2},{1,5},{3,7},{5,1},{7,3},{8,12},{10,14},{12... | collective-permute-start | bytes 196616 | tf_op jit(solution)/shard_map/ppermute | solution.py:24
  120.5 7.9 %collective-permute-start.20 = (bf16[128,256]{1,0:T(8,128)(2,1)S(1)}, bf16[128,256]{1,0:T(8,128)(2,1)S(1)}, u32[]{:S(2)}, u32[]{:S(2)}) collective-permute-start(bf16[128,256]{1,0:T(8,128)(2,1)S(1)} %get-tuple-element.41), channel_id=1, source_target_pairs={{0,6},{2,4},{4,2},{6,0},{1,7},{3,5},{5,3},{7,1},{8,14},{10,12},{12... | collective-permute-start | bytes 196616 | tf_op jit(solution)/shard_map/ppermute | solution.py:24
  (12 other events, 73.0 us)
